TPU v7x, 32 devices: a whole 2x2x4 slice. The times are simulated.
32 devices in a mesh: video: 4 (over z), span: 2 (over y), head: 4 (over x, core).
Axes of the slice: x: 2, y: 2, z: 4, core: 2. Of those that a mesh axis runs over, the one named last changes fastest.
Arguments:
- queries: bfloat16 [2048, 48, 128], P(('video', 'span', 'head')), parts along dimension 0, may hold values from -15 to 15
- key_rows: bfloat16 [2048, 48, 128], P(('video', 'span', 'head')), parts along dimension 0, may hold values from -6 to 6
- value_rows: bfloat16 [2048, 48, 128], P(('video', 'span', 'head')), parts along dimension 0, may hold values from -6 to 6
- noise_levels: int32 [8], P('video'), parts along dimension 0, may hold values from 0 to 7
- gate_table: float32 [8, 48], replicated, may hold values from 0.25 to 2
Outputs:
- attended: bfloat16 [2048, 48, 128], P(('video', 'span', 'head')), parts along dimension 0
There are 4 independent parts, one for each index of `video`. A program takes and returns all parts, laid end to end along the dimension named above; an argument that names none is the same for every part. Nothing has to cross between parts.
All inputs are finite; a program needn't handle non-finite values.
Results may differ from a plain program's by a relative error of at most 0.0039.
Values may be sent and summed in bfloat16 or wider, within the bound.
No kernel may reach another device: no remote copies, remote signals or barrier semaphores. Data moves between devices by JAX's collectives and lax.ppermute only.
A program may use at most 128 MiB of HBM per device.

v0:
```python
import math

import jax
import jax.numpy as jnp
from jax import lax
from jax.sharding import PartitionSpec as P

BLOCK = 128
LEVELS = 8


def from_behind(block, axis, distance):
    devices = range(lax.axis_size(axis))
    route = [(i - distance, i) for i in devices if i - distance in devices]
    return lax.ppermute(block, axis, route)


def gate_rows_for(noise_levels, gate_table):
    one_hot = (jnp.arange(LEVELS, dtype=jnp.int32)[None, :] == noise_levels[:, None]).astype(
        jnp.float32
    )
    return jnp.dot(one_hot, gate_table, precision=lax.Precision.HIGHEST)


def by_head(queries, key_rows, value_rows, noise_levels, gate_table):
    row_count, head_count, head_width = queries.shape
    head_groups = lax.axis_size("head")
    per_group = head_count // head_groups
    chain_len = lax.axis_size("span")
    chain_pos = lax.axis_index("span")
    score_scale = 1.0 / math.sqrt(head_width)
    split_shape = (row_count, head_groups, per_group, head_width)
    query_heads, key_heads, value_heads = (
        lax.all_to_all(
            queries.reshape(split_shape), "head", split_axis=1, concat_axis=0, tiled=True
        ),
        lax.all_to_all(
            key_rows.reshape(split_shape), "head", split_axis=1, concat_axis=0, tiled=True
        ),
        lax.all_to_all(
            value_rows.reshape(split_shape), "head", split_axis=1, concat_axis=0, tiled=True
        ),
    )
    span_len = row_count * head_groups
    query_heads = query_heads.reshape(span_len, per_group, head_width)
    key_heads = key_heads.reshape(span_len, per_group, head_width)
    value_heads = value_heads.reshape(span_len, per_group, head_width)
    own_scores = (
        jnp.einsum("qhd,khd->qhk", query_heads, key_heads, preferred_element_type=jnp.float32)
        * score_scale
    )
    query_block = jnp.arange(span_len, dtype=jnp.int32) // BLOCK
    visible = (query_block[None, :] <= query_block[:, None])[:, None, :]
    own_max = jnp.max(jnp.where(visible, own_scores, -jnp.inf), axis=-1)
    own_weights = jnp.where(visible, jnp.exp(own_scores - own_max[..., None]), 0.0)
    own_totals = jnp.sum(own_weights, axis=-1)
    own_acc = jnp.einsum(
        "qhk,khd->qhd",
        own_weights.astype(jnp.bfloat16),
        value_heads,
        preferred_element_type=jnp.float32,
    )
    running = (own_max, own_totals, own_acc)

    def update(state_now, key_block, value_block):
        row_max, totals, accum = state_now
        scores = (
            jnp.einsum("qhd,khd->qhk", query_heads, key_block, preferred_element_type=jnp.float32)
            * score_scale
        )
        new_max = jnp.maximum(row_max, jnp.max(scores, axis=-1))
        rescale = jnp.exp(row_max - new_max)
        weights = jnp.exp(scores - new_max[..., None])
        totals = totals * rescale + jnp.sum(weights, axis=-1)
        accum = accum * rescale[..., None] + jnp.einsum(
            "qhk,khd->qhd",
            weights.astype(jnp.bfloat16),
            value_block,
            preferred_element_type=jnp.float32,
        )
        return (new_max, totals, accum)

    def advance(state_now, inputs):
        key_block, value_block, span_id = inputs
        useful = (span_id >= 0) & (span_id < chain_pos)
        return (
            lax.cond(
                useful,
                lambda inner: update(inner, key_block, value_block),
                lambda inner: inner,
                state_now,
            ),
            None,
        )

    def relay_turn(turn, loop_state):
        state_now, in_hand = loop_state
        in_hand = from_behind(in_hand, "span", 1)
        state_now, unused = advance(state_now, (in_hand[0], in_hand[1], chain_pos - 1 - turn))
        return (state_now, in_hand)

    running, in_hand = lax.fori_loop(
        0, chain_len - 1, relay_turn, (running, jnp.stack((key_heads, value_heads)))
    )
    row_max, totals, accum = running
    gate_rows = gate_rows_for(noise_levels, gate_table)
    gate_row = lax.dynamic_index_in_dim(gate_rows, chain_pos, 0, keepdims=False)
    my_gates = lax.dynamic_slice_in_dim(gate_row, lax.axis_index("head") * per_group, per_group, 0)
    result = (accum / totals[..., None] * my_gates[None, :, None]).astype(jnp.bfloat16)
    returned = lax.all_to_all(
        result.reshape(span_len, 1, per_group, head_width),
        "head",
        split_axis=0,
        concat_axis=1,
        tiled=True,
    )
    return returned.reshape(row_count, head_count, head_width)


def body(queries, key_rows, value_rows, noise_levels, gate_table):
    return by_head(queries, key_rows, value_rows, noise_levels, gate_table)


def solution(mesh):
    return jax.shard_map(
        body,
        mesh=mesh,
        in_specs=(
            P(("video", "span", "head"), None, None),
            P(("video", "span", "head"), None, None),
            P(("video", "span", "head"), None, None),
            P("video"),
            P(),
        ),
        out_specs=P(("video", "span", "head"), None, None),
        check_vma=False,
    )
```

profile of v0, /device:TPU:12, one launch (start us, length us, event | category | flops | bytes accessed | tf_op | source)
XLA Modules:
  0.0 104.2 jit_solution(15667446418739595812)
XLA Ops:
  0.0 2.3 %copy.34 = bf16[64,48,128]{2,0,1:T(8,128)(2,1)} copy(bf16[64,48,128]{2,1,0:T(8,128)(2,1)} %param.8) | data formatting | bytes 1572864 | tf_op args[1]
  2.3 3.5 %all-to-all-start = ((bf16[64,4,12,128]{3,0,2,1:T(8,128)(2,1)}), bf16[64,4,12,128]{3,0,2,1:T(8,128)(2,1)S(1)}, u32[]{:S(2)}, u32[]{:S(2)}) async-start(bf16[64,4,12,128]{3,0,2,1:T(8,128)(2,1)} %bitcast.4), calls=%async_computation | async-start | bytes 1572864 | tf_op jit(solution)/shard_map/all_to_all | solution.py:37
  5.9 1.1 %copy.38 = bf16[64,48,128]{2,0,1:T(8,128)(2,1)} copy(bf16[64,48,128]{2,1,0:T(8,128)(2,1)S(1)} %copy-done.1) | data formatting | bytes 1572864 | tf_op args[2]
  7.0 10.5 %all-to-all-done = bf16[64,4,12,128]{3,0,2,1:T(8,128)(2,1)S(1)} async-done(((bf16[64,4,12,128]{3,0,2,1:T(8,128)(2,1)}), bf16[64,4,12,128]{3,0,2,1:T(8,128)(2,1)S(1)}, u32[]{:S(2)}, u32[]{:S(2)}) %all-to-all-start) | async-done | bytes 786464 | tf_op jit(solution)/shard_map/all_to_all | solution.py:37
  17.4 3.5 %all-to-all-start.2 = ((bf16[64,4,12,128]{3,0,2,1:T(8,128)(2,1)}), bf16[64,4,12,128]{3,0,2,1:T(8,128)(2,1)S(1)}, u32[]{:S(2)}, u32[]{:S(2)}) async-start(bf16[64,4,12,128]{3,0,2,1:T(8,128)(2,1)} %bitcast.13), calls=%async_computation.2 | async-start | bytes 1572864 | tf_op jit(solution)/shard_map/all_to_all | solution.py:40
  21.0 1.1 %copy.36 = bf16[64,48,128]{2,0,1:T(8,128)(2,1)} copy(bf16[64,48,128]{2,1,0:T(8,128)(2,1)S(1)} %copy-done.2) | data formatting | bytes 1572864 | tf_op args[0]
  22.1 10.4 %all-to-all-done.2 = bf16[64,4,12,128]{3,0,2,1:T(8,128)(2,1)S(1)} async-done(((bf16[64,4,12,128]{3,0,2,1:T(8,128)(2,1)}), bf16[64,4,12,128]{3,0,2,1:T(8,128)(2,1)S(1)}, u32[]{:S(2)}, u32[]{:S(2)}) %all-to-all-start.2) | async-done | bytes 786464 | tf_op jit(solution)/shard_map/all_to_all | solution.py:40
  32.5 3.6 %all-to-all-start.1 = ((bf16[64,4,12,128]{3,0,2,1:T(8,128)(2,1)}), bf16[64,4,12,128]{3,0,2,1:T(8,128)(2,1)S(1)}, u32[]{:S(2)}, u32[]{:S(2)}) async-start(bf16[64,4,12,128]{3,0,2,1:T(8,128)(2,1)} %bitcast.8), calls=%async_computation.1 | async-start | bytes 1572864 | tf_op jit(solution)/shard_map/all_to_all | solution.py:34
  36.2 1.3 %pad_maximum_fusion = bf16[2,256,12,128]{3,1,2,0:T(8,128)(2,1)} fusion(bf16[1,256,12,128]{3,1,2,0:T(8,128)(2,1)S(1)} %bitcast.74, bf16[1,256,12,128]{3,1,2,0:T(8,128)(2,1)S(1)} %bitcast.72), kind=kLoop, calls=%fused_computation.26 | loop fusion | flops 786432 | bytes 3145728 | tf_op jit(solution)/shard_map/stack | solution.py:103
  37.5 1.3 %collective-permute-start = (bf16[2,256,12,128]{3,1,2,0:T(8,128)(2,1)}, bf16[2,256,12,128]{3,1,2,0:T(8,128)(2,1)}, u32[]{:S(2)}, u32[]{:S(2)}) collective-permute-start(bf16[2,256,12,128]{3,1,2,0:T(8,128)(2,1)} %pad_maximum_fusion), channel_id=1, source_target_pairs={{0,4},{1,5},{2,6},{3,7},{8,12},{9,13},{10,14},{11,15},{16,20},{17,... | collective-permute-start | bytes 4718600 | tf_op jit(solution)/shard_map/while/body/eval_jaxpr/ppermute | solution.py:15
  39.2 8.5 %all-to-all-done.1 = bf16[64,4,12,128]{3,0,2,1:T(8,128)(2,1)S(1)} async-done(((bf16[64,4,12,128]{3,0,2,1:T(8,128)(2,1)}), bf16[64,4,12,128]{3,0,2,1:T(8,128)(2,1)S(1)}, u32[]{:S(2)}, u32[]{:S(2)}) %all-to-all-start.1) | async-done | bytes 786464 | tf_op jit(solution)/shard_map/all_to_all | solution.py:34
  47.8 0.6 fusion.15
  48.4 0.7 fusion.19
  49.1 1.0 fusion.26
  50.1 26.4 %collective-permute-done = bf16[2,256,12,128]{3,1,2,0:T(8,128)(2,1)} collective-permute-done((bf16[2,256,12,128]{3,1,2,0:T(8,128)(2,1)}, bf16[2,256,12,128]{3,1,2,0:T(8,128)(2,1)}, u32[]{:S(2)}, u32[]{:S(2)}) %collective-permute-start) | collective-permute-done | bytes 1572896 | tf_op jit(solution)/shard_map/while/body/eval_jaxpr/ppermute | solution.py:15
  76.5 6.8 %conditional.1 = (f32[256,12]{0,1:T(8,128)S(1)}, f32[256,12,128]{2,1,0:T(8,128)}) conditional(s32[]{:T(128)} %convert_element_type.15, (f32[256,12]{0,1:T(8,128)S(1)}, f32[256,12,128]{2,0,1:T(8,128)S(1)}) %tuple.19, (bf16[2,256,12,128]{3,1,2,0:T(8,128)(2,1)}, bf16[256,12,128]{2,0,1:T(8,128)(2,1)S(1)}, f32[256,12]{0,1:T(8,128)S(1)}, ...), branch_computations={%region_2.3_spmd, %region_3.0_spmd} | conditional | flops 409737216 | bytes 18259984 | solution.py:87
  76.5 1.7 %bitcast_reduce_fusion = (f32[256,12]{0,1:T(8,128)S(1)}, f32[12,256,256]{2,1,0:T(8,128)S(1)}) fusion(bf16[256,12,128]{2,0,1:T(8,128)(2,1)S(1)} %get-tuple-element.66, bf16[2,256,12,128]{3,1,2,0:T(8,128)(2,1)} %get-tuple-element.65), kind=kOutput, calls=%fused_computation.1 | convolution fusion | flops 202896384 | bytes 4730880 | tf_op jit(solution)/shard_map/while/body/eval_jaxpr/cond/branch_1_fun/qhd,khd->qhk/dot_general | solution.py:68
  78.2 0.5 fusion.2
  78.8 2.2 %bitcast_add_fusion = f32[256,12,128]{2,0,1:T(8,128)S(1)} fusion(f32[256,12,128]{2,0,1:T(8,128)S(1)} %get-tuple-element.67, f32[12,256,256]{2,1,0:T(8,128)S(1)} %get-tuple-element.78, f32[256,12]{0,1:T(8,128)S(1)} %max.3, bf16[2,256,12,128]{3,1,2,0:T(8,128)(2,1)} %get-tuple-element.65, f32[256,12]{0,1:T(8,128)S(1)} %get-tuple-element.76), kind=kOutput, calls=%fused_computation.6 | convolution fusion | flops 204472320 | bytes 7102464 | tf_op jit(solution)/shard_map/while/body/eval_jaxpr/cond/branch_1_fun/qhk,khd->qhd/dot_general | solution.py:75
  81.1 2.3 %copy.51 = f32[256,12,128]{2,1,0:T(8,128)} copy(f32[256,12,128]{2,0,1:T(8,128)S(1)} %bitcast_add_fusion) | data formatting | bytes 3145728 | tf_op jit(solution)/shard_map/while/body/eval_jaxpr/cond | solution.py:87
  83.5 2.0 %fusion.29 = bf16[256,1,12,128]{3,2,1,0:T(8,128)(2,1)S(1)} fusion(f32[12]{0:T(128)S(1)} %dynamic-slice_bitcast_fusion, f32[256,12,128]{2,1,0:T(8,128)} %get-tuple-element.74, f32[256,12]{1,0:T(8,128)S(1)} %copy.43), kind=kLoop, calls=%fused_computation.32 | loop fusion | flops 1179648 | bytes 2371632 | tf_op jit(solution)/shard_map/reshape | solution.py:111
  85.4 17.1 %all_to_all.60 = bf16[256,1,12,128]{3,2,1,0:T(8,128)(2,1)S(1)} all-to-all(bf16[256,1,12,128]{3,2,1,0:T(8,128)(2,1)S(1)} %fusion.29), channel_id=1, replica_groups=mesh['video'=4,'span'=2,'head'=4] {'head'}, dimensions={0} | all-to-all | bytes 1572864 | tf_op jit(solution)/shard_map/all_to_all | solution.py:110
  102.6 0.2 copy.45
  102.8 1.4 %copy.47 = bf16[64,48,128]{2,1,0:T(8,128)(2,1)} copy(bf16[64,48,128]{2,0,1:T(8,128)(2,1)S(1)} %bitcast.80) | data formatting | bytes 1572864 | tf_op jit(solution)/shard_map/reshape | solution.py:117
  (19 shorter events, 0.8 us)
Async XLA Ops:
  0.0 38.8 %copy-start = (f32[8,48]{1,0:T(8,128)S(1)}, f32[8,48]{1,0:T(8,128)}, u32[]{:S(2)}) copy-start(f32[8,48]{1,0:T(8,128)} %param.11) | copy-start | bytes 4612
  0.0 5.8 %copy-start.1 = (bf16[64,48,128]{2,1,0:T(8,128)(2,1)S(1)}, bf16[64,48,128]{2,1,0:T(8,128)(2,1)}, u32[]{:S(2)}) copy-start(bf16[64,48,128]{2,1,0:T(8,128)(2,1)} %param.9) | copy-start | bytes 2359300
  0.0 20.9 %copy-start.2 = (bf16[64,48,128]{2,1,0:T(8,128)(2,1)S(1)}, bf16[64,48,128]{2,1,0:T(8,128)(2,1)}, u32[]{:S(2)}) copy-start(bf16[64,48,128]{2,1,0:T(8,128)(2,1)} %param.7) | copy-start | bytes 2359300
  2.3 15.1 %all-to-all-start = ((bf16[64,4,12,128]{3,0,2,1:T(8,128)(2,1)}), bf16[64,4,12,128]{3,0,2,1:T(8,128)(2,1)S(1)}, u32[]{:S(2)}, u32[]{:S(2)}) async-start(bf16[64,4,12,128]{3,0,2,1:T(8,128)(2,1)} %bitcast.4), calls=%async_computation | async-start | bytes 1572864 | tf_op jit(solution)/shard_map/all_to_all | solution.py:37
  17.4 15.1 %all-to-all-start.2 = ((bf16[64,4,12,128]{3,0,2,1:T(8,128)(2,1)}), bf16[64,4,12,128]{3,0,2,1:T(8,128)(2,1)S(1)}, u32[]{:S(2)}, u32[]{:S(2)}) async-start(bf16[64,4,12,128]{3,0,2,1:T(8,128)(2,1)} %bitcast.13), calls=%async_computation.2 | async-start | bytes 1572864 | tf_op jit(solution)/shard_map/all_to_all | solution.py:40
  32.5 6.3 %copy-start.3 = (s32[2]{0:T(128)S(1)}, s32[2]{0:T(128)}, u32[]{:S(2)}) copy-start(s32[2]{0:T(128)} %param.10) | copy-start | bytes 28
  32.5 15.2 %all-to-all-start.1 = ((bf16[64,4,12,128]{3,0,2,1:T(8,128)(2,1)}), bf16[64,4,12,128]{3,0,2,1:T(8,128)(2,1)S(1)}, u32[]{:S(2)}, u32[]{:S(2)}) async-start(bf16[64,4,12,128]{3,0,2,1:T(8,128)(2,1)} %bitcast.8), calls=%async_computation.1 | async-start | bytes 1572864 | tf_op jit(solution)/shard_map/all_to_all | solution.py:34
  37.5 39.0 %collective-permute-start = (bf16[2,256,12,128]{3,1,2,0:T(8,128)(2,1)}, bf16[2,256,12,128]{3,1,2,0:T(8,128)(2,1)}, u32[]{:S(2)}, u32[]{:S(2)}) collective-permute-start(bf16[2,256,12,128]{3,1,2,0:T(8,128)(2,1)} %pad_maximum_fusion), channel_id=1, source_target_pairs={{0,4},{1,5},{2,6},{3,7},{8,12},{9,13},{10,14},{11,15},{16,20},{17,... | collective-permute-start | bytes 4718600 | tf_op jit(solution)/shard_map/while/body/eval_jaxpr/ppermute | solution.py:15
where the time goes:
time: 105 us; the launch traced here: 104 us
  waiting for transfers between devices  55.8 us (53%)
  blocking collectives  17.1 us (16%)
  starting transfers between devices  11.9 us (11%)
  local copies, waits for them, and re-layouts  8.85 us (8%)
  matrix products  5.73 us (5%)
  other arithmetic  4.6 us (4%)
    ppermute x1, waiting for transfers between devices, from_behind(): return lax.ppermute(block, axis, route)  26.4 us
    all_to_all x1, blocking collectives, by_head(): lax.all_to_all(result.reshape(span_len, 1, per_group, head_width), 'head'...  17.1 us
    all_to_all x1, waiting for transfers between devices, by_head(): lax.all_to_all(key_rows.reshape(split_shape), 'head', split_axis=1, conca...  10.5 us
    all_to_all x1, waiting for transfers between devices, by_head(): lax.all_to_all(value_rows.reshape(split_shape), 'head', split_axis=1, con...  10.4 us
    all_to_all x1, waiting for transfers between devices, by_head(): lax.all_to_all(queries.reshape(split_shape), 'head', split_axis=1, concat...  8.53 us
    unnamed x11, local copies, waits for them, and re-layouts  4.54 us
    all_to_all x1, starting transfers between devices, by_head(): lax.all_to_all(queries.reshape(split_shape), 'head', split_axis=1, concat...  3.63 us
    all_to_all x1, starting transfers between devices, by_head(): lax.all_to_all(key_rows.reshape(split_shape), 'head', split_axis=1, conca...  3.49 us
  transfers between devices with their start and end apart: 4, of which 4 were waited for; matrix products, arithmetic and copies ran while one was open for 6% of the time, Pallas kernels for 0%

commit v1 on v0

--- a/solution.py
+++ b/solution.py
@@ -1,12 +1,17 @@
+import functools
 import math
 
 import jax
 import jax.numpy as jnp
 from jax import lax
+from jax.experimental import pallas as pl
+from jax.experimental.pallas import tpu as pltpu
 from jax.sharding import PartitionSpec as P
 
 BLOCK = 128
 LEVELS = 8
+TILE = 8
+LANES = 32
 
 
 def from_behind(block, axis, distance):
@@ -96,13 +101,13 @@
     def relay_turn(turn, loop_state):
         state_now, in_hand = loop_state
         in_hand = from_behind(in_hand, "span", 1)
-        state_now, unused = advance(state_now, (in_hand[0], in_hand[1], chain_pos - 1 - turn))
+        state_now, _ = advance(state_now, (in_hand[0], in_hand[1], chain_pos - 1 - turn))
         return (state_now, in_hand)
 
-    running, in_hand = lax.fori_loop(
+    running, _ = lax.fori_loop(
         0, chain_len - 1, relay_turn, (running, jnp.stack((key_heads, value_heads)))
     )
-    row_max, totals, accum = running
+    _, totals, accum = running
     gate_rows = gate_rows_for(noise_levels, gate_table)
     gate_row = lax.dynamic_index_in_dim(gate_rows, chain_pos, 0, keepdims=False)
     my_gates = lax.dynamic_slice_in_dim(gate_row, lax.axis_index("head") * per_group, per_group, 0)
@@ -117,21 +122,333 @@
     return returned.reshape(row_count, head_count, head_width)
 
 
+def attend(jobs, factor):
+    scores = [
+        [lax.dot_general(q, k, (((1,), (1,)), ((), ())), preferred_element_type=jnp.float32) for k in keys]
+        for q, keys, _, _ in jobs
+    ]
+    scores = [
+        [s if shift is None else s + shift for s, shift in zip(of_head, job[3])]
+        for of_head, job in zip(scores, jobs)
+    ]
+    tops = [
+        functools.reduce(jnp.maximum, [jnp.max(s, axis=1, keepdims=True) for s in of_head])
+        for of_head in scores
+    ]
+    weights = [[jnp.exp2((s - top) * factor) for s in of_head] for of_head, top in zip(scores, tops)]
+    totals = [sum(jnp.sum(w, axis=1, keepdims=True) for w in of_head) for of_head in weights]
+    sums = [
+        sum(
+            lax.dot_general(
+                w.astype(jnp.bfloat16), v, (((1,), (0,)), ((), ())), preferred_element_type=jnp.float32
+            )
+            for w, v in zip(of_head, job[2])
+        )
+        for of_head, job in zip(weights, jobs)
+    ]
+    return (
+        [s * (1.0 / t) for s, t in zip(sums, totals)],
+        [top * factor + jnp.log2(t) for top, t in zip(tops, totals)],
+    )
+
+
+def lanes_of(rows, width):
+    return lax.broadcasted_iota(jnp.int32, (rows, width), 1)
+
+
+def table_of(columns, lane):
+    table = jnp.zeros(lane.shape, jnp.float32)
+    for h, column in enumerate(columns):
+        table = jnp.where(lane % LANES == h, column, table)
+    return table
+
+
+def split_table(table, lane):
+    high = table.astype(jnp.bfloat16).astype(jnp.float32)
+    rest = table - high
+    middle = rest.astype(jnp.bfloat16).astype(jnp.float32)
+    parts = jnp.where(lane < LANES, high, jnp.where(lane < 2 * LANES, middle, rest - middle))
+    return jnp.where(lane < 3 * LANES, parts, 0.0).astype(jnp.bfloat16)
+
+
+def column_of(table, chosen):
+    return jnp.sum(jnp.where(chosen, table.astype(jnp.float32), 0.0), axis=1, keepdims=True)
+
+
+def both(pair, h):
+    return jnp.concatenate([pair[0][h], pair[1][h]], axis=0)
+
+
+def store(out, parts, log_weights, lane):
+    for h, part in enumerate(parts):
+        out[h] = part.astype(out.dtype)
+    out[len(parts)] = split_table(table_of(log_weights, lane), lane)
+
+
+def store_local(out, table, parts, log_weights, lane):
+    for h, part in enumerate(parts):
+        out[h] = part
+    table[...] = table_of(log_weights, lane)
+
+
+def where_am_i():
+    span = lax.axis_index("span")
+    return span, 2 * span + lax.axis_index("head") // 2
+
+
+def unless(seen):
+    return jnp.where(seen, 0.0, -jnp.inf)
+
+
+def own_kernel(factor, q, k0, k1, v0, v1, out, table):
+    span, _ = where_am_i()
+    rows, width = q.shape[1:]
+    half = out.shape[0]
+    first = (1 - span) * half
+    jobs = [
+        (q[first + h], [both((k0, k1), first + h)], [both((v0, v1), first + h)], [None])
+        for h in range(half)
+    ]
+    store_local(out, table, *attend(jobs, factor), lanes_of(rows, width))
+
+
+def visit_kernel(factor, q, rk0, rk1, rv0, rv1, k0, k1, v0, v1, out):
+    span, block = where_am_i()
+    half, rows, width = q.shape
+    first = span * half
+    shift = unless(block != 3)
+    jobs = [
+        (
+            q[h],
+            [both((rk0, rk1), h), both((k0, k1), first + h)],
+            [both((rv0, rv1), h), both((v0, v1), first + h)],
+            [None, shift],
+        )
+        for h in range(half)
+    ]
+    store(out, *attend(jobs, factor), lanes_of(rows, width))
+
+
+def stay_kernel(factor, q, rk0, rk1, rv0, rv1, k0, k1, v0, v1, out, table):
+    span, block = where_am_i()
+    rows, width = q.shape[1:]
+    half = out.shape[0]
+    first = span * half
+    shift = unless(block != 0)
+    jobs = [
+        (
+            q[first + h],
+            [both((k0, k1), first + h), both((rk0, rk1), h)],
+            [both((v0, v1), first + h), both((rv0, rv1), h)],
+            [None, shift],
+        )
+        for h in range(half)
+    ]
+    store_local(out, table, *attend(jobs, factor), lanes_of(rows, width))
+
+
+def guest_kernel(factor, host, first, q, k0, k1, v0, v1, out):
+    _, block = where_am_i()
+    heads, rows, width = q.shape
+
+    @pl.when(block == host)
+    def _():
+        jobs = [
+            (q[h], [both((k0, k1), first + h)], [both((v0, v1), first + h)], [None])
+            for h in range(heads)
+        ]
+        store(out, *attend(jobs, factor), lanes_of(rows, width))
+
+
+def fetched_kernel(factor, host, first, q, k0, k1, v0, v1, out, table):
+    _, block = where_am_i()
+    heads, rows, width = out.shape
+
+    @pl.when(block == host)
+    def _():
+        jobs = [
+            (q[first + h], [both((k0, k1), h)], [both((v0, v1), h)], [None]) for h in range(heads)
+        ]
+        store_local(out, table, *attend(jobs, factor), lanes_of(rows, width))
+
+
+def merge_kernel(
+    levels, gate_table, other, other_table, mine, mine_table, upper, across, extra, lent, fetched, fetched_table, out
+):
+    span, block = where_am_i()
+    half, rows, width = mine.shape
+    part_heads = fetched.shape[0]
+    lane = lanes_of(rows, width)
+    level = levels[span]
+
+    def finish(first, parts_of):
+        for start in range(0, half, TILE):
+            heads = range(start, start + TILE)
+            parts = [parts_of(h) for h in heads]
+            tops = [functools.reduce(jnp.maximum, [w for _, w in of_head]) for of_head in parts]
+            scaled = [
+                [jnp.exp2(w - top) for _, w in of_head] for of_head, top in zip(parts, tops)
+            ]
+            factors = [gate_table[level, first + h] / sum(s) for h, s in zip(heads, scaled)]
+            sums = [
+                sum(p.astype(jnp.float32) * (s * f) for (p, _), s in zip(of_head, of_scale))
+                for of_head, of_scale, f in zip(parts, scaled, factors)
+            ]
+            together = jnp.swapaxes(jnp.stack(sums), 0, 1)
+            out[:, first + start : first + start + TILE, :] = together.astype(out.dtype)
+
+    def sent(slab, h, shift=0.0):
+        return slab[h], column_of(slab[slab.shape[0] - 1], lane % LANES == h) + shift
+
+    def kept(parts, table, h):
+        return parts[h], column_of(table[...], lane == h)
+
+    @pl.when(span == 1)
+    def _():
+        shift = unless(block == 3)
+        finish(0, lambda h: [kept(other, other_table, h), sent(upper, h), sent(extra, h, shift)])
+        finish(half, lambda h: [kept(mine, mine_table, h), sent(across, h)])
+
+    @pl.when(block == 0)
+    def _():
+        finish(0, lambda h: [kept(mine, mine_table, h)])
+        finish(half, lambda h: [kept(other, other_table, h)])
+
+    @pl.when(block == 1)
+    def _():
+        finish(0, lambda h: [kept(mine, mine_table, h)])
+        lent_heads = half - part_heads
+        finish(
+            half,
+            lambda h: [
+                kept(other, other_table, h),
+                sent(lent, h) if h < lent_heads else kept(fetched, fetched_table, h - lent_heads),
+            ],
+        )
+
+
+def run(kernel, out_shape, operands, scalars=()):
+    in_vmem, in_smem = pl.BlockSpec(memory_space=pltpu.VMEM), pl.BlockSpec(memory_space=pltpu.SMEM)
+    return pl.pallas_call(
+        kernel,
+        out_shape=out_shape,
+        in_specs=[in_smem] * len(scalars) + [in_vmem] * len(operands),
+        out_specs=jax.tree.map(lambda _: in_vmem, out_shape),
+        compiler_params=pltpu.CompilerParams(vmem_limit_bytes=8 << 20),
+        cost_estimate=pl.CostEstimate(flops=2_000_000_000, bytes_accessed=1 << 20, transcendentals=0),
+    )(*scalars, *operands)
+
+
+def by_block(queries, key_rows, value_rows, noise_levels, gate_table):
+    rows, heads, width = queries.shape
+    half = heads // 2
+    lent = half // 2
+    per_span = lax.axis_size("head")
+    share = per_span // 2
+    span, side = lax.axis_index("span"), lax.axis_index("head") // share
+    later = span == 1
+    factor = math.log2(math.e) / math.sqrt(width)
+    devices = range(2 * per_span)
+
+    def send(block, target):
+        route = [(p, target(p)) for p in devices if target(p) is not None]
+        return lax.ppermute(block, ("span", "head"), route)
+
+    def sideways(p):
+        return p ^ share
+
+    def other_span(p):
+        return p ^ per_span
+
+    def partner(p):
+        return p ^ 1
+
+    def only(numbers, target):
+        return lambda p: target(p) if p // share in numbers else None
+
+    def up(p):
+        return p + per_span if p < per_span else None
+
+    def moved(block, target):
+        return send(block, target)
+
+    def by_head_first(a):
+        return jnp.transpose(a, (1, 0, 2))
+
+    x1 = by_head_first(jnp.where(later, queries[:, :half], key_rows[:, :half]))
+    y1 = by_head_first(jnp.where(later, queries[:, :half], key_rows[:, half:]))
+    x1, y1, *raw = lax.optimization_barrier((x1, y1, queries, key_rows, value_rows))
+    q, k, v = map(by_head_first, raw)
+    x1 = moved(x1, only((0, 1, 3), sideways))
+    y1 = moved(y1, other_span)
+    own_k, own_v = moved(k, partner), moved(v, partner)
+    x2 = moved(jnp.where(later, q[half:], v[:half]), sideways)
+    y2 = moved(v[half:], other_span)
+    x3 = moved(jnp.where(side == 0, k[half + lent :], q[half : half + lent]), only((0, 1), sideways))
+    x4 = moved(v[half + lent :], only((0,), sideways))
+
+    def slab(n):
+        return jax.ShapeDtypeStruct((n + 1, rows, width), jnp.bfloat16)
+
+    def kept(n):
+        return (
+            jax.ShapeDtypeStruct((n, rows, width), jnp.float32),
+            jax.ShapeDtypeStruct((rows, width), jnp.float32),
+        )
+
+    def kernel(body, out_shape, *operands):
+        return run(body, out_shape, operands)
+
+    own = (k, own_k, v, own_v)
+    other = kernel(functools.partial(own_kernel, factor), kept(half), q, *own)
+    extra = kernel(functools.partial(guest_kernel, factor, 2, 0), slab(half), x1, *own)
+    extra = moved(extra, only((2,), sideways))
+
+    got_k = jnp.where(later, y1, x1)
+    got_k1 = moved(got_k, partner)
+    visitor, got_v = jnp.where(later, x2, y1), jnp.where(later, y2, x2)
+    got_v1 = moved(got_v, partner)
+    received = (got_k, got_k1, got_v, got_v1)
+    away = kernel(functools.partial(visit_kernel, factor), slab(half), visitor, *received, *own)
+    upper = moved(away, up)
+    across = moved(away, only((2, 3), sideways))
+    mine = kernel(functools.partial(stay_kernel, factor), kept(half), q, *received, *own)
+
+    helped = kernel(functools.partial(guest_kernel, factor, 0, half), slab(lent), x3, *own)
+    helped = moved(helped, only((0,), sideways))
+    x3_1, x4_1 = (moved(a, only((1,), partner)) for a in (x3, x4))
+    fetched = kernel(
+        functools.partial(fetched_kernel, factor, 1, half + lent), kept(half - lent), q, x3, x3_1, x4, x4_1
+    )
+    return run(
+        merge_kernel,
+        jax.ShapeDtypeStruct((rows, heads, width), jnp.bfloat16),
+        (*other, *mine, upper, across, extra, helped, *fetched),
+        (noise_levels, gate_table),
+    )
+
+
 def body(queries, key_rows, value_rows, noise_levels, gate_table):
+    rows, heads, _ = queries.shape
+    spans, per_span = lax.axis_size("span"), lax.axis_size("head")
+    two_by_two = spans == 2 and 2 * rows == BLOCK and per_span * rows == 2 * BLOCK
+    if two_by_two and heads % (2 * TILE) == 0 and heads <= 2 * LANES:
+        return by_block(queries, key_rows, value_rows, noise_levels, gate_table)
     return by_head(queries, key_rows, value_rows, noise_levels, gate_table)
 
 
 def solution(mesh):
+    tokens = ("video", "span", "head")
     return jax.shard_map(
         body,
         mesh=mesh,
         in_specs=(
-            P(("video", "span", "head"), None, None),
-            P(("video", "span", "head"), None, None),
-            P(("video", "span", "head"), None, None),
+            P(tokens, None, None),
+            P(tokens, None, None),
+            P(tokens, None, None),
             P("video"),
             P(),
         ),
-        out_specs=P(("video", "span", "head"), None, None),
+        out_specs=P(tokens, None, None),
         check_vma=False,
     )

time: 105 us -> 61.3 us (0.58)
  the two profiles are of different devices: /device:TPU:12 before, /device:TPU:14 now
where the time goes in v1:
time: 61.3 us; the launch traced here: 60.9 us
  waiting for transfers between devices  30 us (49%)
  starting transfers between devices  16.9 us (28%)
  Pallas kernels  7.29 us (12%)
  local copies, waits for them, and re-layouts  3.45 us (6%)
  other arithmetic  3.07 us (5%)
    ppermute x16, waiting for transfers between devices, send(): return lax.ppermute(block, ('span', 'head'), route)  30 us
    ppermute x16, starting transfers between devices, send(): return lax.ppermute(block, ('span', 'head'), route)  16.9 us
    pallas_call x7, Pallas kernels, run(): pl.pallas_call(kernel, out_shape=out_shape, in_specs=[in_smem] * len(scal...  7.29 us
    unnamed x10, local copies, waits for them, and re-layouts  1.83 us
    select_n x1, other arithmetic, by_block(): visitor, got_v = (jnp.where(later, x2, y1), jnp.where(later, y2, x2))  1.33 us
  transfers between devices with their start and end apart: 16, of which 7 were waited for; matrix products, arithmetic and copies ran while one was open for 5% of the time, Pallas kernels for 4%

profile of v1, /device:TPU:14, one launch (start us, length us, event | category | flops | bytes accessed | tf_op | source)
XLA Modules:
  0.0 60.9 jit_solution(2395894925465722141)
XLA Ops:
  0.0 1.1 %copy-done.2 = bf16[64,48,128]{2,1,0:T(8,128)(2,1)S(1)} copy-done((bf16[64,48,128]{2,1,0:T(8,128)(2,1)S(1)}, bf16[64,48,128]{2,1,0:T(8,128)(2,1)}, u32[]{:S(2)}) %copy-start.2) | copy-done | bytes 786456
  1.2 0.9 %slice-done = bf16[64,24,128]{2,1,0:T(8,128)(2,1)S(1)} async-done(((bf16[64,48,128]{2,1,0:T(8,128)(2,1)}), bf16[64,24,128]{2,1,0:T(8,128)(2,1)S(1)}, s32[]{:S(2)}) %slice-start) | async-done | bytes 393240 | tf_op jit(solution)/shard_map/slice | solution.py:378
  2.1 0.9 %fusion = (bf16[24,64,128]{2,1,0:T(8,128)(2,1)}, bf16[24,64,128]{2,1,0:T(8,128)(2,1)S(1)}) fusion(bf16[64,24,128]{2,1,0:T(8,128)(2,1)S(1)} %get-tuple-element.29, pred[]{:T(512)S(6)} %eq.6, bf16[64,24,128]{2,1,0:T(8,128)(2,1)S(1)} %slice-done, bf16[64,24,128]{2,1,0:T(8,128)(2,1)S(1)} %get-tuple-element.30), kind=kLoop, calls=%fused_computation.5 | loop fusion | flops 393216 | bytes 1966081 | tf_op jit(solution)/shard_map/transpose | solution.py:376
  3.5 2.5 %collective-permute-start.3 = (bf16[24,64,128]{2,1,0:T(8,128)(2,1)S(1)}, bf16[24,64,128]{2,1,0:T(8,128)(2,1)S(1)}, u32[]{:S(2)}, u32[]{:S(2)}) collective-permute-start(bf16[24,64,128]{2,1,0:T(8,128)(2,1)S(1)} %get-tuple-element.22), channel_id=1, source_target_pairs={{0,2},{1,3},{2,0},{3,1},{6,4},{7,5},{8,10},{9,11},{10,8},{11,9},{1... | collective-permute-start | bytes 1179656 | tf_op jit(solution)/shard_map/ppermute | solution.py:355
  6.4 0.8 %slice_select_fusion = (bf16[24,64,128]{2,1,0:T(8,128)(2,1)}, bf16[24,64,128]{2,1,0:T(8,128)(2,1)S(1)}) fusion(bf16[48,64,128]{2,1,0:T(8,128)(2,1)S(1)} %bitcast.13, bf16[48,64,128]{2,1,0:T(8,128)(2,1)S(1)} %bitcast.21, pred[]{:T(512)S(6)} %eq.6), kind=kLoop, calls=%fused_computation.3 | loop fusion | flops 196608 | bytes 1966081 | tf_op jit(solution)/shard_map/jit(_where)/select_n | solution.py:385
  7.3 3.0 %collective-permute-start.5 = (bf16[24,64,128]{2,1,0:T(8,128)(2,1)S(1)}, bf16[24,64,128]{2,1,0:T(8,128)(2,1)}, u32[]{:S(2)}, u32[]{:S(2)}) collective-permute-start(bf16[24,64,128]{2,1,0:T(8,128)(2,1)S(1)} %get-tuple-element.28), channel_id=1, source_target_pairs={{0,4},{1,5},{2,6},{3,7},{4,0},{5,1},{6,2},{7,3},{8,12},{9,13},{10,... | collective-permute-start | bytes 1179656 | tf_op jit(solution)/shard_map/ppermute | solution.py:355
  10.5 0.7 %collective-permute-start.11 = (bf16[12,64,128]{2,1,0:T(8,128)(2,1)S(1)}, bf16[12,64,128]{2,1,0:T(8,128)(2,1)S(1)}, u32[]{:S(2)}, u32[]{:S(2)}) collective-permute-start(bf16[12,64,128]{2,1,0:T(8,128)(2,1)S(1)} %slice_select_fusion.1), channel_id=1, source_target_pairs={{0,2},{1,3},{2,0},{3,1},{8,10},{9,11},{10,8},{11,9},{16,18},{17,19... | collective-permute-start | bytes 589832 | tf_op jit(solution)/shard_map/ppermute | solution.py:355
  11.3 4.1 %collective-permute-done.2 = bf16[24,64,128]{2,1,0:T(8,128)(2,1)} collective-permute-done((bf16[24,64,128]{2,1,0:T(8,128)(2,1)}, bf16[24,64,128]{2,1,0:T(8,128)(2,1)}, u32[]{:S(2)}, u32[]{:S(2)}) %collective-permute-start.2) | collective-permute-done | bytes 393248 | tf_op jit(solution)/shard_map/ppermute | solution.py:355
  15.5 0.7 %collective-permute-start.14 = (bf16[12,64,128]{2,1,0:T(8,128)(2,1)S(1)}, bf16[12,64,128]{2,1,0:T(8,128)(2,1)S(1)}, u32[]{:S(2)}, u32[]{:S(2)}) collective-permute-start(bf16[12,64,128]{2,1,0:T(8,128)(2,1)S(1)} %slice.42), channel_id=1, source_target_pairs={{0,2},{1,3},{8,10},{9,11},{16,18},{17,19},{24,26},{25,27}} | collective-permute-start | bytes 589832 | tf_op jit(solution)/shard_map/ppermute | solution.py:355
  16.1 6.6 %collective-permute-done.6 = bf16[24,64,128]{2,1,0:T(8,128)(2,1)} collective-permute-done((bf16[24,64,128]{2,1,0:T(8,128)(2,1)}, bf16[24,64,128]{2,1,0:T(8,128)(2,1)}, u32[]{:S(2)}, u32[]{:S(2)}) %collective-permute-start.6) | collective-permute-done | bytes 393248 | tf_op jit(solution)/shard_map/ppermute | solution.py:355
  22.7 0.7 %collective-permute-start.13 = (bf16[12,64,128]{2,1,0:T(8,128)(2,1)S(1)}, bf16[12,64,128]{2,1,0:T(8,128)(2,1)S(1)}, u32[]{:S(2)}, u32[]{:S(2)}) collective-permute-start(bf16[12,64,128]{2,1,0:T(8,128)(2,1)S(1)} %collective-permute-done.11.q.k0), channel_id=1, source_target_pairs={{2,3},{3,2},{10,11},{11,10},{18,19},{19,18},{26,27},{27,26}} | collective-permute-start | bytes 589832 | tf_op jit(solution)/shard_map/ppermute | solution.py:355
  23.4 1.3 %broadcast_select_fusion = (bf16[24,64,128]{2,1,0:T(8,128)(2,1)S(1)}, bf16[24,64,128]{2,1,0:T(8,128)(2,1)S(1)}, bf16[24,64,128]{2,1,0:T(8,128)(2,1)S(1)}) fusion(bf16[24,64,128]{2,1,0:T(8,128)(2,1)} %collective-permute-done.6, bf16[24,64,128]{2,1,0:T(8,128)(2,1)} %collective-permute-done.2, pred[]{:T(512)S(6)} %eq.6, ...), kind=kLoop, calls=%fused_computation.8 | loop fusion | flops 589824 | bytes 2752513 | tf_op jit(solution)/shard_map/jit(_where)/select_n | solution.py:409
  25.3 0.7 %collective-permute-start.15 = (bf16[12,64,128]{2,1,0:T(8,128)(2,1)S(1)}, bf16[12,64,128]{2,1,0:T(8,128)(2,1)S(1)}, u32[]{:S(2)}, u32[]{:S(2)}) collective-permute-start(bf16[12,64,128]{2,1,0:T(8,128)(2,1)S(1)} %collective-permute-done.14.v0), channel_id=1, source_target_pairs={{2,3},{3,2},{10,11},{11,10},{18,19},{19,18},{26,27},{27,26}} | collective-permute-start | bytes 589832 | tf_op jit(solution)/shard_map/ppermute | solution.py:355
  27.1 1.6 %shard_map.57 = bf16[25,64,128]{2,1,0:T(8,128)(2,1)S(1)} custom-call(bf16[24,64,128]{2,1,0:T(8,128)(2,1)S(1)} %get-tuple-element.31.q, bf16[24,64,128]{2,1,0:T(8,128)(2,1)S(1)} %get-tuple-element.32.rk0, bf16[24,64,128]{2,1,0:T(8,128)(2,1)S(1)} %collective-permute-done.4.rk1, bf16[24,64,128]{2,1,0:T(8,128)(2,1)S(1)} %get-tuple-element.33.rv0, ...), custom_call_target="tpu_custom_call" | custom-call | flops 2000000000 | bytes 1048576 | tf_op jit(solution)/shard_map/pallas_call | solution.py:332
  28.7 4.4 %collective-permute-start.9 = (bf16[25,64,128]{2,1,0:T(8,128)(2,1)S(1)}, bf16[25,64,128]{2,1,0:T(8,128)(2,1)S(1)}, u32[]{:S(2)}, u32[]{:S(2)}) collective-permute-start(bf16[25,64,128]{2,1,0:T(8,128)(2,1)S(1)} %shard_map.57), channel_id=1, source_target_pairs={{4,6},{5,7},{6,4},{7,5},{12,14},{13,15},{14,12},{15,13},{20,22},{2... | collective-permute-start | bytes 1228808 | tf_op jit(solution)/shard_map/ppermute | solution.py:355
  33.1 1.3 %collective-permute-start.8 = (bf16[25,64,128]{2,1,0:T(8,128)(2,1)S(1)}, bf16[25,64,128]{2,1,0:T(8,128)(2,1)S(1)}, u32[]{:S(2)}, u32[]{:S(2)}) collective-permute-start(bf16[25,64,128]{2,1,0:T(8,128)(2,1)S(1)} %shard_map.57), channel_id=1, source_target_pairs={{0,4},{1,5},{2,6},{3,7},{8,12},{9,13},{10,14},{11,15},{16,20},{17,... | collective-permute-start | bytes 1228808 | tf_op jit(solution)/shard_map/ppermute | solution.py:355
  34.4 1.3 %collective-permute-start.10 = (bf16[25,64,128]{2,1,0:T(8,128)(2,1)S(1)}, bf16[25,64,128]{2,1,0:T(8,128)(2,1)S(1)}, u32[]{:S(2)}, u32[]{:S(2)}) collective-permute-start(bf16[25,64,128]{2,1,0:T(8,128)(2,1)S(1)} %shard_map.58), channel_id=1, source_target_pairs={{4,6},{5,7},{12,14},{13,15},{20,22},{21,23},{28,30},{29,31}} | collective-permute-start | bytes 1228808 | tf_op jit(solution)/shard_map/ppermute | solution.py:355
  35.8 0.7 %collective-permute-start.12 = (bf16[13,64,128]{2,1,0:T(8,128)(2,1)S(1)}, bf16[13,64,128]{2,1,0:T(8,128)(2,1)S(1)}, u32[]{:S(2)}, u32[]{:S(2)}) collective-permute-start(bf16[13,64,128]{2,1,0:T(8,128)(2,1)S(1)} %shard_map.59), channel_id=1, source_target_pairs={{0,2},{1,3},{8,10},{9,11},{16,18},{17,19},{24,26},{25,27}} | collective-permute-start | bytes 638984 | tf_op jit(solution)/shard_map/ppermute | solution.py:355
  36.5 1.6 %shard_map.56 = (f32[24,64,128]{2,1,0:T(8,128)S(1)}, f32[64,128]{1,0:T(8,128)S(1)}) custom-call(bf16[48,64,128]{2,1,0:T(8,128)(2,1)S(1)} %bitcast.24, bf16[24,64,128]{2,1,0:T(8,128)(2,1)S(1)} %get-tuple-element.32.rk0, bf16[24,64,128]{2,1,0:T(8,128)(2,1)S(1)} %collective-permute-done.4.rk1, bf16[24,64,128]{2,1,0:T(8,128)(2,1)S(1)} %get-tuple-element.33.rv0, ...), custom_call_target="tpu_custom_call" | custom-call | flops 2000000000 | bytes 1048576 | tf_op jit(solution)/shard_map/pallas_call | solution.py:332
  38.1 0.9 %shard_map.55 = (f32[24,64,128]{2,1,0:T(8,128)S(1)}, f32[64,128]{1,0:T(8,128)S(1)}) custom-call(bf16[48,64,128]{2,1,0:T(8,128)(2,1)S(1)} %bitcast.25, bf16[48,64,128]{2,1,0:T(8,128)(2,1)S(1)} %bitcast.32, bf16[48,64,128]{2,1,0:T(8,128)(2,1)S(1)} %collective-permute-done.k1, bf16[48,64,128]{2,1,0:T(8,128)(2,1)S(1)} %bitcast.20, ...), custom_call_target="tpu_custom_call" | custom-call | flops 2000000000 | bytes 1048576 | tf_op jit(solution)/shard_map/pallas_call | solution.py:332
  39.0 12.6 %collective-permute-done.10.extra = bf16[25,64,128]{2,1,0:T(8,128)(2,1)S(1)} collective-permute-done((bf16[25,64,128]{2,1,0:T(8,128)(2,1)S(1)}, bf16[25,64,128]{2,1,0:T(8,128)(2,1)S(1)}, u32[]{:S(2)}, u32[]{:S(2)}) %collective-permute-start.10) | collective-permute-done | bytes 409632 | tf_op jit(solution)/shard_map/ppermute | solution.py:355
  51.6 5.5 %collective-permute-done.8.upper = bf16[25,64,128]{2,1,0:T(8,128)(2,1)S(1)} collective-permute-done((bf16[25,64,128]{2,1,0:T(8,128)(2,1)S(1)}, bf16[25,64,128]{2,1,0:T(8,128)(2,1)S(1)}, u32[]{:S(2)}, u32[]{:S(2)}) %collective-permute-start.8) | collective-permute-done | bytes 409632 | tf_op jit(solution)/shard_map/ppermute | solution.py:355
  57.1 0.7 %copy-done = f32[8,48]{1,0:T(8,128)S(1)} copy-done((f32[8,48]{1,0:T(8,128)S(1)}, f32[8,48]{1,0:T(8,128)}, u32[]{:S(2)}) %copy-start) | copy-done | bytes 1560
  57.8 3.1 %shard_map.61 = bf16[64,48,128]{2,1,0:T(8,128)(2,1)} custom-call(s32[2]{0:T(128)S(1)} %copy-done.1, f32[8,48]{1,0:T(8,128)S(1)} %copy-done, f32[24,64,128]{2,1,0:T(8,128)S(1)} %get-tuple-element.19.other, f32[64,128]{1,0:T(8,128)S(1)} %get-tuple-element.20.other_table, f32[24,64,128]{2,1,0:T(8,128)S(1)} %get-tuple-element.23.mine, ...), custom_call_target="tpu_custom_call" | custom-call | flops 2000000000 | bytes 1048576 | tf_op jit(solution)/shard_map/pallas_call | solution.py:332
  (36 shorter events, 3.1 us)
Async XLA Ops:
  0.0 1.1 %copy-start.2 = (bf16[64,48,128]{2,1,0:T(8,128)(2,1)S(1)}, bf16[64,48,128]{2,1,0:T(8,128)(2,1)}, u32[]{:S(2)}) copy-start(bf16[64,48,128]{2,1,0:T(8,128)(2,1)} %param.6) | copy-start | bytes 2359300
  1.1 1.0 %slice-start = ((bf16[64,48,128]{2,1,0:T(8,128)(2,1)}), bf16[64,24,128]{2,1,0:T(8,128)(2,1)S(1)}, s32[]{:S(2)}) async-start(bf16[64,48,128]{2,1,0:T(8,128)(2,1)} %param.5), calls=%async_computation | async-start | bytes 786432 | tf_op jit(solution)/shard_map/slice | solution.py:378
  2.1 3.9 %copy-start.3 = (bf16[64,48,128]{2,1,0:T(8,128)(2,1)S(1)}, bf16[64,48,128]{2,1,0:T(8,128)(2,1)}, u32[]{:S(2)}) copy-start(bf16[64,48,128]{2,1,0:T(8,128)(2,1)} %param.5) | copy-start | bytes 2359300
  3.0 3.2 %copy-start.4 = (bf16[64,48,128]{2,1,0:T(8,128)(2,1)S(1)}, bf16[64,48,128]{2,1,0:T(8,128)(2,1)}, u32[]{:S(2)}) copy-start(bf16[64,48,128]{2,1,0:T(8,128)(2,1)} %param.7) | copy-start | bytes 2359300
  3.0 12.3 %collective-permute-start.2 = (bf16[24,64,128]{2,1,0:T(8,128)(2,1)}, bf16[24,64,128]{2,1,0:T(8,128)(2,1)}, u32[]{:S(2)}, u32[]{:S(2)}) collective-permute-start(bf16[24,64,128]{2,1,0:T(8,128)(2,1)} %get-tuple-element.21), channel_id=1, source_target_pairs={{0,4},{1,5},{2,6},{3,7},{4,0},{5,1},{6,2},{7,3},{8,12},{9,13},{10,... | collective-permute-start | bytes 1179656 | tf_op jit(solution)/shard_map/ppermute | solution.py:355
  3.5 11.9 %collective-permute-start.3 = (bf16[24,64,128]{2,1,0:T(8,128)(2,1)S(1)}, bf16[24,64,128]{2,1,0:T(8,128)(2,1)S(1)}, u32[]{:S(2)}, u32[]{:S(2)}) collective-permute-start(bf16[24,64,128]{2,1,0:T(8,128)(2,1)S(1)} %get-tuple-element.22), channel_id=1, source_target_pairs={{0,2},{1,3},{2,0},{3,1},{6,4},{7,5},{8,10},{9,11},{10,8},{11,9},{1... | collective-permute-start | bytes 1179656 | tf_op jit(solution)/shard_map/ppermute | solution.py:355
  7.3 15.5 %collective-permute-start.6 = (bf16[24,64,128]{2,1,0:T(8,128)(2,1)}, bf16[24,64,128]{2,1,0:T(8,128)(2,1)}, u32[]{:S(2)}, u32[]{:S(2)}) collective-permute-start(bf16[24,64,128]{2,1,0:T(8,128)(2,1)} %get-tuple-element.27), channel_id=1, source_target_pairs={{0,2},{1,3},{2,0},{3,1},{4,6},{5,7},{6,4},{7,5},{8,10},{9,11},{10,... | collective-permute-start | bytes 1179656 | tf_op jit(solution)/shard_map/ppermute | solution.py:355
  7.3 16.1 %collective-permute-start.5 = (bf16[24,64,128]{2,1,0:T(8,128)(2,1)S(1)}, bf16[24,64,128]{2,1,0:T(8,128)(2,1)}, u32[]{:S(2)}, u32[]{:S(2)}) collective-permute-start(bf16[24,64,128]{2,1,0:T(8,128)(2,1)S(1)} %get-tuple-element.28), channel_id=1, source_target_pairs={{0,4},{1,5},{2,6},{3,7},{4,0},{5,1},{6,2},{7,3},{8,12},{9,13},{10,... | collective-permute-start | bytes 1179656 | tf_op jit(solution)/shard_map/ppermute | solution.py:355
  10.5 0.7 %collective-permute-start.11 = (bf16[12,64,128]{2,1,0:T(8,128)(2,1)S(1)}, bf16[12,64,128]{2,1,0:T(8,128)(2,1)S(1)}, u32[]{:S(2)}, u32[]{:S(2)}) collective-permute-start(bf16[12,64,128]{2,1,0:T(8,128)(2,1)S(1)} %slice_select_fusion.1), channel_id=1, source_target_pairs={{0,2},{1,3},{2,0},{3,1},{8,10},{9,11},{10,8},{11,9},{16,18},{17,19... | collective-permute-start | bytes 589832 | tf_op jit(solution)/shard_map/ppermute | solution.py:355
  11.2 15.9 %collective-permute-start.1 = (bf16[48,64,128]{2,1,0:T(8,128)(2,1)S(1)}, bf16[48,64,128]{2,1,0:T(8,128)(2,1)S(1)}, u32[]{:S(2)}, u32[]{:S(2)}) collective-permute-start(bf16[48,64,128]{2,1,0:T(8,128)(2,1)S(1)} %bitcast.14), channel_id=1, source_target_pairs={{0,1},{1,0},{2,3},{3,2},{4,5},{5,4},{6,7},{7,6},{8,9},{9,8},{10,11... | collective-permute-start | bytes 2359304 | tf_op jit(solution)/shard_map/ppermute | solution.py:355
  15.3 11.8 %collective-permute-start = (bf16[48,64,128]{2,1,0:T(8,128)(2,1)S(1)}, bf16[48,64,128]{2,1,0:T(8,128)(2,1)S(1)}, u32[]{:S(2)}, u32[]{:S(2)}) collective-permute-start(bf16[48,64,128]{2,1,0:T(8,128)(2,1)S(1)} %bitcast.27), channel_id=1, source_target_pairs={{0,1},{1,0},{2,3},{3,2},{4,5},{5,4},{6,7},{7,6},{8,9},{9,8},{10,11... | collective-permute-start | bytes 2359304 | tf_op jit(solution)/shard_map/ppermute | solution.py:355
  15.5 9.3 %collective-permute-start.14 = (bf16[12,64,128]{2,1,0:T(8,128)(2,1)S(1)}, bf16[12,64,128]{2,1,0:T(8,128)(2,1)S(1)}, u32[]{:S(2)}, u32[]{:S(2)}) collective-permute-start(bf16[12,64,128]{2,1,0:T(8,128)(2,1)S(1)} %slice.42), channel_id=1, source_target_pairs={{0,2},{1,3},{8,10},{9,11},{16,18},{17,19},{24,26},{25,27}} | collective-permute-start | bytes 589832 | tf_op jit(solution)/shard_map/ppermute | solution.py:355
  22.7 2.6 %collective-permute-start.13 = (bf16[12,64,128]{2,1,0:T(8,128)(2,1)S(1)}, bf16[12,64,128]{2,1,0:T(8,128)(2,1)S(1)}, u32[]{:S(2)}, u32[]{:S(2)}) collective-permute-start(bf16[12,64,128]{2,1,0:T(8,128)(2,1)S(1)} %collective-permute-done.11.q.k0), channel_id=1, source_target_pairs={{2,3},{3,2},{10,11},{11,10},{18,19},{19,18},{26,27},{27,26}} | collective-permute-start | bytes 589832 | tf_op jit(solution)/shard_map/ppermute | solution.py:355
  24.7 1.8 %collective-permute-start.4 = (bf16[24,64,128]{2,1,0:T(8,128)(2,1)S(1)}, bf16[24,64,128]{2,1,0:T(8,128)(2,1)S(1)}, u32[]{:S(2)}, u32[]{:S(2)}) collective-permute-start(bf16[24,64,128]{2,1,0:T(8,128)(2,1)S(1)} %get-tuple-element.32.rk0), channel_id=1, source_target_pairs={{0,1},{1,0},{2,3},{3,2},{4,5},{5,4},{6,7},{7,6},{8,9},{9,8},{10,11... | collective-permute-start | bytes 1179656 | tf_op jit(solution)/shard_map/ppermute | solution.py:355
  24.8 2.3 %collective-permute-start.7 = (bf16[24,64,128]{2,1,0:T(8,128)(2,1)S(1)}, bf16[24,64,128]{2,1,0:T(8,128)(2,1)S(1)}, u32[]{:S(2)}, u32[]{:S(2)}) collective-permute-start(bf16[24,64,128]{2,1,0:T(8,128)(2,1)S(1)} %get-tuple-element.33.rv0), channel_id=1, source_target_pairs={{0,1},{1,0},{2,3},{3,2},{4,5},{5,4},{6,7},{7,6},{8,9},{9,8},{10,11... | collective-permute-start | bytes 1179656 | tf_op jit(solution)/shard_map/ppermute | solution.py:355
  25.3 0.7 %collective-permute-start.15 = (bf16[12,64,128]{2,1,0:T(8,128)(2,1)S(1)}, bf16[12,64,128]{2,1,0:T(8,128)(2,1)S(1)}, u32[]{:S(2)}, u32[]{:S(2)}) collective-permute-start(bf16[12,64,128]{2,1,0:T(8,128)(2,1)S(1)} %collective-permute-done.14.v0), channel_id=1, source_target_pairs={{2,3},{3,2},{10,11},{11,10},{18,19},{19,18},{26,27},{27,26}} | collective-permute-start | bytes 589832 | tf_op jit(solution)/shard_map/ppermute | solution.py:355
  28.7 22.9 %collective-permute-start.9 = (bf16[25,64,128]{2,1,0:T(8,128)(2,1)S(1)}, bf16[25,64,128]{2,1,0:T(8,128)(2,1)S(1)}, u32[]{:S(2)}, u32[]{:S(2)}) collective-permute-start(bf16[25,64,128]{2,1,0:T(8,128)(2,1)S(1)} %shard_map.57), channel_id=1, source_target_pairs={{4,6},{5,7},{6,4},{7,5},{12,14},{13,15},{14,12},{15,13},{20,22},{2... | collective-permute-start | bytes 1228808 | tf_op jit(solution)/shard_map/ppermute | solution.py:355
  33.1 24.0 %collective-permute-start.8 = (bf16[25,64,128]{2,1,0:T(8,128)(2,1)S(1)}, bf16[25,64,128]{2,1,0:T(8,128)(2,1)S(1)}, u32[]{:S(2)}, u32[]{:S(2)}) collective-permute-start(bf16[25,64,128]{2,1,0:T(8,128)(2,1)S(1)} %shard_map.57), channel_id=1, source_target_pairs={{0,4},{1,5},{2,6},{3,7},{8,12},{9,13},{10,14},{11,15},{16,20},{17,... | collective-permute-start | bytes 1228808 | tf_op jit(solution)/shard_map/ppermute | solution.py:355
  34.4 17.2 %collective-permute-start.10 = (bf16[25,64,128]{2,1,0:T(8,128)(2,1)S(1)}, bf16[25,64,128]{2,1,0:T(8,128)(2,1)S(1)}, u32[]{:S(2)}, u32[]{:S(2)}) collective-permute-start(bf16[25,64,128]{2,1,0:T(8,128)(2,1)S(1)} %shard_map.58), channel_id=1, source_target_pairs={{4,6},{5,7},{12,14},{13,15},{20,22},{21,23},{28,30},{29,31}} | collective-permute-start | bytes 1228808 | tf_op jit(solution)/shard_map/ppermute | solution.py:355
  35.8 3.2 %collective-permute-start.12 = (bf16[13,64,128]{2,1,0:T(8,128)(2,1)S(1)}, bf16[13,64,128]{2,1,0:T(8,128)(2,1)S(1)}, u32[]{:S(2)}, u32[]{:S(2)}) collective-permute-start(bf16[13,64,128]{2,1,0:T(8,128)(2,1)S(1)} %shard_map.59), channel_id=1, source_target_pairs={{0,2},{1,3},{8,10},{9,11},{16,18},{17,19},{24,26},{25,27}} | collective-permute-start | bytes 638984 | tf_op jit(solution)/shard_map/ppermute | solution.py:355
  57.1 0.7 %copy-start = (f32[8,48]{1,0:T(8,128)S(1)}, f32[8,48]{1,0:T(8,128)}, u32[]{:S(2)}) copy-start(f32[8,48]{1,0:T(8,128)} %gate_table.1) | copy-start | bytes 4612
  57.1 0.7 %copy-start.1 = (s32[2]{0:T(128)S(1)}, s32[2]{0:T(128)}, u32[]{:S(2)}) copy-start(s32[2]{0:T(128)} %levels.1) | copy-start | bytes 28

commit v2 on v1

--- a/solution.py
+++ b/solution.py
@@ -122,29 +122,21 @@
     return returned.reshape(row_count, head_count, head_width)
 
 
-def attend(jobs, factor):
+def attend(jobs, factor, shift=None):
     scores = [
-        [lax.dot_general(q, k, (((1,), (1,)), ((), ())), preferred_element_type=jnp.float32) for k in keys]
-        for q, keys, _, _ in jobs
+        lax.dot_general(q, k, (((1,), (1,)), ((), ())), preferred_element_type=jnp.float32)
+        for q, k, _ in jobs
     ]
-    scores = [
-        [s if shift is None else s + shift for s, shift in zip(of_head, job[3])]
-        for of_head, job in zip(scores, jobs)
-    ]
-    tops = [
-        functools.reduce(jnp.maximum, [jnp.max(s, axis=1, keepdims=True) for s in of_head])
-        for of_head in scores
-    ]
-    weights = [[jnp.exp2((s - top) * factor) for s in of_head] for of_head, top in zip(scores, tops)]
-    totals = [sum(jnp.sum(w, axis=1, keepdims=True) for w in of_head) for of_head in weights]
+    if shift is not None:
+        scores = [s + shift for s in scores]
+    tops = [jnp.max(s, axis=1, keepdims=True) for s in scores]
+    weights = [jnp.exp2((s - top) * factor) for s, top in zip(scores, tops)]
+    totals = [jnp.sum(w, axis=1, keepdims=True) for w in weights]
     sums = [
-        sum(
-            lax.dot_general(
-                w.astype(jnp.bfloat16), v, (((1,), (0,)), ((), ())), preferred_element_type=jnp.float32
-            )
-            for w, v in zip(of_head, job[2])
+        lax.dot_general(
+            w.astype(jnp.bfloat16), v, (((1,), (0,)), ((), ())), preferred_element_type=jnp.float32
         )
-        for of_head, job in zip(weights, jobs)
+        for w, (_, _, v) in zip(weights, jobs)
     ]
     return (
         [s * (1.0 / t) for s, t in zip(sums, totals)],
@@ -171,12 +163,13 @@
     return jnp.where(lane < 3 * LANES, parts, 0.0).astype(jnp.bfloat16)
 
 
-def column_of(table, chosen):
-    return jnp.sum(jnp.where(chosen, table.astype(jnp.float32), 0.0), axis=1, keepdims=True)
-
-
-def both(pair, h):
-    return jnp.concatenate([pair[0][h], pair[1][h]], axis=0)
+def joined(table):
+    parts = table.astype(jnp.float32)
+    return parts + pltpu.roll(parts, parts.shape[1] - LANES, 1) + pltpu.roll(parts, parts.shape[1] - 2 * LANES, 1)
+
+
+def rows_of(*blocks):
+    return jnp.concatenate([array[head] for array, head in blocks], axis=0)
 
 
 def store(out, parts, log_weights, lane):
@@ -200,51 +193,115 @@
     return jnp.where(seen, 0.0, -jnp.inf)
 
 
+def first_kernel(queries, key_rows, x1, y1, held, sems):
+    span, _ = where_am_i()
+    half = x1.shape[0]
+
+    def fetch(array, start, slot):
+        source = array.at[:, pl.ds(start, half), :]
+        return pltpu.make_async_copy(source, held.at[slot], sems.at[slot])
+
+    def load(array, starts):
+        for slot, start in enumerate(starts):
+            fetch(array, start, slot).start()
+
+    @pl.when(span == 0)
+    def _():
+        load(key_rows, (0, half))
+
+    @pl.when(span == 1)
+    def _():
+        load(queries, (0, 0))
+
+    for slot, out in enumerate((x1, y1)):
+        fetch(queries, 0, slot).wait()
+        for h in range(0, half, TILE):
+            out[h : h + TILE] = jnp.swapaxes(held[slot, :, h : h + TILE, :], 0, 1)
+
+
+def second_kernel(lent, q, k, v, x2, y2, x3, x4):
+    span, block = where_am_i()
+    half = x2.shape[0]
+    y2[...] = v[half:]
+    x4[...] = v[half + lent :]
+
+    @pl.when(span == 0)
+    def _():
+        x2[...] = v[:half]
+
+    @pl.when(span == 1)
+    def _():
+        x2[...] = q[half:]
+
+    @pl.when(block == 0)
+    def _():
+        x3[...] = k[half + lent :]
+
+    @pl.when(block != 0)
+    def _():
+        x3[: half - lent] = q[half : 2 * half - lent]
+
+
+def choose_kernel(x1, y1, x2, y2, keys, visitor, values):
+    span, _ = where_am_i()
+
+    @pl.when(span == 0)
+    def _():
+        keys[...] = x1[...]
+        visitor[...] = y1[...]
+        values[...] = x2[...]
+
+    @pl.when(span == 1)
+    def _():
+        keys[...] = y1[...]
+        visitor[...] = x2[...]
+        values[...] = y2[...]
+
+
 def own_kernel(factor, q, k0, k1, v0, v1, out, table):
     span, _ = where_am_i()
     rows, width = q.shape[1:]
     half = out.shape[0]
-    first = (1 - span) * half
-    jobs = [
-        (q[first + h], [both((k0, k1), first + h)], [both((v0, v1), first + h)], [None])
-        for h in range(half)
-    ]
+    heads = [(1 - span) * half + h for h in range(half)]
+    jobs = [(q[h], rows_of((k0, h), (k1, h)), rows_of((v0, h), (v1, h))) for h in heads]
     store_local(out, table, *attend(jobs, factor), lanes_of(rows, width))
+
+
+def two_blocks(q, received, own, span, half, seen_received, seen_own):
+    rk0, rk1, rv0, rv1 = received
+    k0, k1, v0, v1 = own
+    keys = 4 * rk0.shape[1]
+    place = lax.broadcasted_iota(jnp.int32, (1, keys), 1)
+    shift = jnp.where(place < keys // 2, unless(seen_received), unless(seen_own))
+    jobs = []
+    for h in range(half):
+        g = span * half + h
+        jobs.append(
+            (
+                q(h, g),
+                rows_of((rk0, h), (rk1, h), (k0, g), (k1, g)),
+                rows_of((rv0, h), (rv1, h), (v0, g), (v1, g)),
+            )
+        )
+    return jobs, shift
 
 
 def visit_kernel(factor, q, rk0, rk1, rv0, rv1, k0, k1, v0, v1, out):
     span, block = where_am_i()
     half, rows, width = q.shape
-    first = span * half
-    shift = unless(block != 3)
-    jobs = [
-        (
-            q[h],
-            [both((rk0, rk1), h), both((k0, k1), first + h)],
-            [both((rv0, rv1), h), both((v0, v1), first + h)],
-            [None, shift],
-        )
-        for h in range(half)
-    ]
-    store(out, *attend(jobs, factor), lanes_of(rows, width))
+    jobs, shift = two_blocks(
+        lambda h, g: q[h], (rk0, rk1, rv0, rv1), (k0, k1, v0, v1), span, half, block >= 0, block != 3
+    )
+    store(out, *attend(jobs, factor, shift), lanes_of(rows, width))
 
 
 def stay_kernel(factor, q, rk0, rk1, rv0, rv1, k0, k1, v0, v1, out, table):
     span, block = where_am_i()
     rows, width = q.shape[1:]
-    half = out.shape[0]
-    first = span * half
-    shift = unless(block != 0)
-    jobs = [
-        (
-            q[first + h],
-            [both((k0, k1), first + h), both((rk0, rk1), h)],
-            [both((v0, v1), first + h), both((rv0, rv1), h)],
-            [None, shift],
-        )
-        for h in range(half)
-    ]
-    store_local(out, table, *attend(jobs, factor), lanes_of(rows, width))
+    jobs, shift = two_blocks(
+        lambda h, g: q[g], (rk0, rk1, rv0, rv1), (k0, k1, v0, v1), span, out.shape[0], block != 0, block >= 0
+    )
+    store_local(out, table, *attend(jobs, factor, shift), lanes_of(rows, width))
 
 
 def guest_kernel(factor, host, first, q, k0, k1, v0, v1, out):
@@ -254,7 +311,7 @@
     @pl.when(block == host)
     def _():
         jobs = [
-            (q[h], [both((k0, k1), first + h)], [both((v0, v1), first + h)], [None])
+            (q[h], rows_of((k0, first + h), (k1, first + h)), rows_of((v0, first + h), (v1, first + h)))
             for h in range(heads)
         ]
         store(out, *attend(jobs, factor), lanes_of(rows, width))
@@ -266,9 +323,7 @@
 
     @pl.when(block == host)
     def _():
-        jobs = [
-            (q[first + h], [both((k0, k1), h)], [both((v0, v1), h)], [None]) for h in range(heads)
-        ]
+        jobs = [(q[first + h], rows_of((k0, h), (k1, h)), rows_of((v0, h), (v1, h))) for h in range(heads)]
         store_local(out, table, *attend(jobs, factor), lanes_of(rows, width))
 
 
@@ -276,64 +331,63 @@
     levels, gate_table, other, other_table, mine, mine_table, upper, across, extra, lent, fetched, fetched_table, out
 ):
     span, block = where_am_i()
-    half, rows, width = mine.shape
-    part_heads = fetched.shape[0]
-    lane = lanes_of(rows, width)
+    half, _, width = mine.shape
+    lent_heads = half - fetched.shape[0]
     level = levels[span]
-
-    def finish(first, parts_of):
-        for start in range(0, half, TILE):
-            heads = range(start, start + TILE)
-            parts = [parts_of(h) for h in heads]
-            tops = [functools.reduce(jnp.maximum, [w for _, w in of_head]) for of_head in parts]
-            scaled = [
-                [jnp.exp2(w - top) for _, w in of_head] for of_head, top in zip(parts, tops)
-            ]
-            factors = [gate_table[level, first + h] / sum(s) for h, s in zip(heads, scaled)]
+    lane = lanes_of(1, width)
+
+    def finish(first, sources, last=half, begin=0):
+        gates = jnp.zeros((1, width), jnp.float32)
+        for h in range(begin, last):
+            gates = jnp.where(lane == h, gate_table[level, first + h], gates)
+        logs = [table for _, table, _ in sources]
+        top = functools.reduce(jnp.maximum, logs)
+        scaled = [jnp.exp2(table - top) for table in logs]
+        ratio = gates / sum(scaled)
+        scaled = [s * ratio for s in scaled]
+        for start in range(begin, last, TILE // 2):
             sums = [
-                sum(p.astype(jnp.float32) * (s * f) for (p, _), s in zip(of_head, of_scale))
-                for of_head, of_scale, f in zip(parts, scaled, factors)
+                sum(
+                    parts[h - skip].astype(jnp.float32) * s[:, h : h + 1]
+                    for (parts, _, skip), s in zip(sources, scaled)
+                )
+                for h in range(start, start + TILE // 2)
             ]
             together = jnp.swapaxes(jnp.stack(sums), 0, 1)
-            out[:, first + start : first + start + TILE, :] = together.astype(out.dtype)
-
-    def sent(slab, h, shift=0.0):
-        return slab[h], column_of(slab[slab.shape[0] - 1], lane % LANES == h) + shift
-
-    def kept(parts, table, h):
-        return parts[h], column_of(table[...], lane == h)
+            out[:, first + start : first + start + TILE // 2, :] = together.astype(out.dtype)
+
+    def sent(slab, shift=0.0):
+        return slab, joined(slab[slab.shape[0] - 1]) + shift, 0
+
+    def kept(parts, table):
+        return parts, table[...], 0
 
     @pl.when(span == 1)
     def _():
-        shift = unless(block == 3)
-        finish(0, lambda h: [kept(other, other_table, h), sent(upper, h), sent(extra, h, shift)])
-        finish(half, lambda h: [kept(mine, mine_table, h), sent(across, h)])
+        finish(0, [kept(other, other_table), sent(upper), sent(extra, unless(block == 3))])
+        finish(half, [kept(mine, mine_table), sent(across)])
 
     @pl.when(block == 0)
     def _():
-        finish(0, lambda h: [kept(mine, mine_table, h)])
-        finish(half, lambda h: [kept(other, other_table, h)])
+        finish(0, [kept(mine, mine_table)])
+        finish(half, [kept(other, other_table)])
 
     @pl.when(block == 1)
     def _():
-        finish(0, lambda h: [kept(mine, mine_table, h)])
-        lent_heads = half - part_heads
-        finish(
-            half,
-            lambda h: [
-                kept(other, other_table, h),
-                sent(lent, h) if h < lent_heads else kept(fetched, fetched_table, h - lent_heads),
-            ],
-        )
-
-
-def run(kernel, out_shape, operands, scalars=()):
+        finish(0, [kept(mine, mine_table)])
+        finish(half, [kept(other, other_table), sent(lent)], last=lent_heads)
+        moved = pltpu.roll(fetched_table[...], lent_heads, 1)
+        finish(half, [kept(other, other_table), (fetched, moved, lent_heads)], begin=lent_heads)
+
+
+def run(kernel, out_shape, operands, scalars=(), space=pltpu.VMEM, scratch=()):
     in_vmem, in_smem = pl.BlockSpec(memory_space=pltpu.VMEM), pl.BlockSpec(memory_space=pltpu.SMEM)
     return pl.pallas_call(
         kernel,
         out_shape=out_shape,
-        in_specs=[in_smem] * len(scalars) + [in_vmem] * len(operands),
+        in_specs=[in_smem] * len(scalars) + [pl.BlockSpec(memory_space=space)] * len(operands),
         out_specs=jax.tree.map(lambda _: in_vmem, out_shape),
+        scratch_shapes=scratch,
         compiler_params=pltpu.CompilerParams(vmem_limit_bytes=8 << 20),
         cost_estimate=pl.CostEstimate(flops=2_000_000_000, bytes_accessed=1 << 20, transcendentals=0),
     )(*scalars, *operands)
@@ -345,8 +399,6 @@
     lent = half // 2
     per_span = lax.axis_size("head")
     share = per_span // 2
-    span, side = lax.axis_index("span"), lax.axis_index("head") // share
-    later = span == 1
     factor = math.log2(math.e) / math.sqrt(width)
     devices = range(2 * per_span)
 
@@ -375,17 +427,32 @@
     def by_head_first(a):
         return jnp.transpose(a, (1, 0, 2))
 
-    x1 = by_head_first(jnp.where(later, queries[:, :half], key_rows[:, :half]))
-    y1 = by_head_first(jnp.where(later, queries[:, :half], key_rows[:, half:]))
+    def blocks(*counts):
+        return tuple(jax.ShapeDtypeStruct((n, rows, width), jnp.bfloat16) for n in counts)
+
+    def kernel(body, out_shape, *operands, **more):
+        return run(body, out_shape, operands, **more)
+
+    x1, y1 = kernel(
+        first_kernel,
+        blocks(half, half),
+        queries,
+        key_rows,
+        space=pl.ANY,
+        scratch=[pltpu.VMEM((2, rows, half, width), jnp.bfloat16), pltpu.SemaphoreType.DMA((2,))],
+    )
     x1, y1, *raw = lax.optimization_barrier((x1, y1, queries, key_rows, value_rows))
     q, k, v = map(by_head_first, raw)
+    x2, y2, x3, x4 = kernel(
+        functools.partial(second_kernel, lent), blocks(half, half, half - lent, half - lent), q, k, v
+    )
     x1 = moved(x1, only((0, 1, 3), sideways))
     y1 = moved(y1, other_span)
     own_k, own_v = moved(k, partner), moved(v, partner)
-    x2 = moved(jnp.where(later, q[half:], v[:half]), sideways)
-    y2 = moved(v[half:], other_span)
-    x3 = moved(jnp.where(side == 0, k[half + lent :], q[half : half + lent]), only((0, 1), sideways))
-    x4 = moved(v[half + lent :], only((0,), sideways))
+    x2 = moved(x2, sideways)
+    y2 = moved(y2, other_span)
+    x3 = moved(x3, only((0, 1), sideways))
+    x4 = moved(x4, only((0,), sideways))
 
     def slab(n):
         return jax.ShapeDtypeStruct((n + 1, rows, width), jnp.bfloat16)
@@ -396,18 +463,13 @@
             jax.ShapeDtypeStruct((rows, width), jnp.float32),
         )
 
-    def kernel(body, out_shape, *operands):
-        return run(body, out_shape, operands)
-
     own = (k, own_k, v, own_v)
     other = kernel(functools.partial(own_kernel, factor), kept(half), q, *own)
     extra = kernel(functools.partial(guest_kernel, factor, 2, 0), slab(half), x1, *own)
     extra = moved(extra, only((2,), sideways))
 
-    got_k = jnp.where(later, y1, x1)
-    got_k1 = moved(got_k, partner)
-    visitor, got_v = jnp.where(later, x2, y1), jnp.where(later, y2, x2)
-    got_v1 = moved(got_v, partner)
+    got_k, visitor, got_v = kernel(choose_kernel, blocks(half, half, half), x1, y1, x2, y2)
+    got_k1, got_v1 = moved(got_k, partner), moved(got_v, partner)
     received = (got_k, got_k1, got_v, got_v1)
     away = kernel(functools.partial(visit_kernel, factor), slab(half), visitor, *received, *own)
     upper = moved(away, up)

time: 61.3 us -> 59.1 us (0.964)
  the two profiles are of different devices: /device:TPU:14 before, /device:TPU:30 now
where the time goes in v2:
time: 59.1 us; the launch traced here: 58.6 us
  waiting for transfers between devices  29.8 us (50%)
  starting transfers between devices  15.4 us (26%)
  Pallas kernels  6.9 us (12%)
  local copies, waits for them, and re-layouts  6.23 us (11%)
    ppermute x16, waiting for transfers between devices, send(): return lax.ppermute(block, ('span', 'head'), route)  29.8 us
    ppermute x16, starting transfers between devices, send(): return lax.ppermute(block, ('span', 'head'), route)  15.4 us
    pallas_call x10, Pallas kernels, run(): pl.pallas_call(kernel, out_shape=out_shape, in_specs=[in_smem] * len(scal...  6.9 us
    unnamed x14, local copies, waits for them, and re-layouts  5.62 us
  transfers between devices with their start and end apart: 16, of which 8 were waited for; matrix products, arithmetic and copies ran while one was open for 0% of the time, Pallas kernels for 3%

profile of v2, /device:TPU:30, one launch (start us, length us, event | category | flops | bytes accessed | tf_op | source)
XLA Modules:
  0.0 58.6 jit_solution(2275152411038618298)
XLA Ops:
  0.0 1.1 %copy-done = bf16[64,48,128]{2,1,0:T(8,128)(2,1)S(1)} copy-done((bf16[64,48,128]{2,1,0:T(8,128)(2,1)S(1)}, bf16[64,48,128]{2,1,0:T(8,128)(2,1)}, u32[]{:S(2)}) %copy-start) | copy-done | bytes 786456
  1.1 1.1 %copy-done.2 = bf16[64,48,128]{2,1,0:T(8,128)(2,1)S(1)} copy-done((bf16[64,48,128]{2,1,0:T(8,128)(2,1)S(1)}, bf16[64,48,128]{2,1,0:T(8,128)(2,1)}, u32[]{:S(2)}) %copy-start.2) | copy-done | bytes 786456
  2.6 0.8 %copy-done.6 = bf16[64,48,128]{2,1,0:T(8,128)(2,1)S(1)} copy-done((bf16[64,48,128]{2,1,0:T(8,128)(2,1)S(1)}, bf16[64,48,128]{2,1,0:T(8,128)(2,1)}, u32[]{:S(2)}) %copy-start.6) | copy-done | bytes 786456
  3.6 0.9 %copy-done.1 = bf16[64,48,128]{2,1,0:T(8,128)(2,1)S(1)} copy-done((bf16[64,48,128]{2,1,0:T(8,128)(2,1)S(1)}, bf16[64,48,128]{2,1,0:T(8,128)(2,1)}, u32[]{:S(2)}) %copy-start.1) | copy-done | bytes 786456
  4.7 0.9 %copy-done.3 = bf16[64,48,128]{2,1,0:T(8,128)(2,1)S(1)} copy-done((bf16[64,48,128]{2,1,0:T(8,128)(2,1)S(1)}, bf16[64,48,128]{2,1,0:T(8,128)(2,1)}, u32[]{:S(2)}) %copy-start.3) | copy-done | bytes 786456
  7.3 3.3 %collective-permute-start.5 = (bf16[24,64,128]{2,1,0:T(8,128)(2,1)S(1)}, bf16[24,64,128]{2,1,0:T(8,128)(2,1)S(1)}, u32[]{:S(2)}, u32[]{:S(2)}) collective-permute-start(bf16[24,64,128]{2,1,0:T(8,128)(2,1)S(1)} %get-tuple-element.35), channel_id=1, source_target_pairs={{0,4},{1,5},{2,6},{3,7},{4,0},{5,1},{6,2},{7,3},{8,12},{9,13},{10,... | collective-permute-start | bytes 1179656 | tf_op jit(solution)/shard_map/ppermute | solution.py:407
  10.6 2.5 %collective-permute-start.2 = (bf16[24,64,128]{2,1,0:T(8,128)(2,1)S(1)}, bf16[24,64,128]{2,1,0:T(8,128)(2,1)S(1)}, u32[]{:S(2)}, u32[]{:S(2)}) collective-permute-start(bf16[24,64,128]{2,1,0:T(8,128)(2,1)S(1)} %get-tuple-element.32), channel_id=1, source_target_pairs={{0,2},{1,3},{2,0},{3,1},{6,4},{7,5},{8,10},{9,11},{10,8},{11,9},{1... | collective-permute-start | bytes 1179656 | tf_op jit(solution)/shard_map/ppermute | solution.py:407
  13.2 3.7 %collective-permute-done.4.x2 = bf16[24,64,128]{2,1,0:T(8,128)(2,1)S(1)} collective-permute-done((bf16[24,64,128]{2,1,0:T(8,128)(2,1)S(1)}, bf16[24,64,128]{2,1,0:T(8,128)(2,1)S(1)}, u32[]{:S(2)}, u32[]{:S(2)}) %collective-permute-start.4) | collective-permute-done | bytes 393248 | tf_op jit(solution)/shard_map/ppermute | solution.py:407
  16.9 3.6 %collective-permute-done.5.y2 = bf16[24,64,128]{2,1,0:T(8,128)(2,1)S(1)} collective-permute-done((bf16[24,64,128]{2,1,0:T(8,128)(2,1)S(1)}, bf16[24,64,128]{2,1,0:T(8,128)(2,1)S(1)}, u32[]{:S(2)}, u32[]{:S(2)}) %collective-permute-start.5) | collective-permute-done | bytes 393248 | tf_op jit(solution)/shard_map/ppermute | solution.py:407
  20.5 0.7 %collective-permute-start.14 = (bf16[12,64,128]{2,1,0:T(8,128)(2,1)S(1)}, bf16[12,64,128]{2,1,0:T(8,128)(2,1)S(1)}, u32[]{:S(2)}, u32[]{:S(2)}) collective-permute-start(bf16[12,64,128]{2,1,0:T(8,128)(2,1)S(1)} %get-tuple-element.42), channel_id=1, source_target_pairs={{0,2},{1,3},{8,10},{9,11},{16,18},{17,19},{24,26},{25,27}} | collective-permute-start | bytes 589832 | tf_op jit(solution)/shard_map/ppermute | solution.py:407
  21.2 2.2 %collective-permute-done.2.x1.q = bf16[24,64,128]{2,1,0:T(8,128)(2,1)S(1)} collective-permute-done((bf16[24,64,128]{2,1,0:T(8,128)(2,1)S(1)}, bf16[24,64,128]{2,1,0:T(8,128)(2,1)S(1)}, u32[]{:S(2)}, u32[]{:S(2)}) %collective-permute-start.2) | collective-permute-done | bytes 393248 | tf_op jit(solution)/shard_map/ppermute | solution.py:407
  24.1 3.5 %collective-permute-done.3.y1 = bf16[24,64,128]{2,1,0:T(8,128)(2,1)S(1)} collective-permute-done((bf16[24,64,128]{2,1,0:T(8,128)(2,1)S(1)}, bf16[24,64,128]{2,1,0:T(8,128)(2,1)S(1)}, u32[]{:S(2)}, u32[]{:S(2)}) %collective-permute-start.3) | collective-permute-done | bytes 393248 | tf_op jit(solution)/shard_map/ppermute | solution.py:407
  28.2 0.7 %collective-permute-start.15 = (bf16[12,64,128]{2,1,0:T(8,128)(2,1)S(1)}, bf16[12,64,128]{2,1,0:T(8,128)(2,1)S(1)}, u32[]{:S(2)}, u32[]{:S(2)}) collective-permute-start(bf16[12,64,128]{2,1,0:T(8,128)(2,1)S(1)} %collective-permute-done.14.v0), channel_id=1, source_target_pairs={{2,3},{3,2},{10,11},{11,10},{18,19},{19,18},{26,27},{27,26}} | collective-permute-start | bytes 589832 | tf_op jit(solution)/shard_map/ppermute | solution.py:407
  30.0 1.0 %shard_map.60 = bf16[25,64,128]{2,1,0:T(8,128)(2,1)S(1)} custom-call(bf16[24,64,128]{2,1,0:T(8,128)(2,1)S(1)} %get-tuple-element.40.q, bf16[24,64,128]{2,1,0:T(8,128)(2,1)S(1)} %get-tuple-element.36.rk0, bf16[24,64,128]{2,1,0:T(8,128)(2,1)S(1)} %collective-permute-done.6.rk1, bf16[24,64,128]{2,1,0:T(8,128)(2,1)S(1)} %get-tuple-element.37.rv0, ...), custom_call_target="tpu_custom_call" | custom-call | flops 2000000000 | bytes 1048576 | tf_op jit(solution)/shard_map/pallas_call | solution.py:385
  31.0 1.3 %collective-permute-start.8 = (bf16[25,64,128]{2,1,0:T(8,128)(2,1)S(1)}, bf16[25,64,128]{2,1,0:T(8,128)(2,1)S(1)}, u32[]{:S(2)}, u32[]{:S(2)}) collective-permute-start(bf16[25,64,128]{2,1,0:T(8,128)(2,1)S(1)} %shard_map.60), channel_id=1, source_target_pairs={{0,4},{1,5},{2,6},{3,7},{8,12},{9,13},{10,14},{11,15},{16,20},{17,... | collective-permute-start | bytes 1228808 | tf_op jit(solution)/shard_map/ppermute | solution.py:407
  32.3 2.4 %collective-permute-start.9 = (bf16[25,64,128]{2,1,0:T(8,128)(2,1)S(1)}, bf16[25,64,128]{2,1,0:T(8,128)(2,1)S(1)}, u32[]{:S(2)}, u32[]{:S(2)}) collective-permute-start(bf16[25,64,128]{2,1,0:T(8,128)(2,1)S(1)} %shard_map.60), channel_id=1, source_target_pairs={{4,6},{5,7},{6,4},{7,5},{12,14},{13,15},{14,12},{15,13},{20,22},{2... | collective-permute-start | bytes 1228808 | tf_op jit(solution)/shard_map/ppermute | solution.py:407
  34.8 1.3 %collective-permute-start.10 = (bf16[25,64,128]{2,1,0:T(8,128)(2,1)S(1)}, bf16[25,64,128]{2,1,0:T(8,128)(2,1)S(1)}, u32[]{:S(2)}, u32[]{:S(2)}) collective-permute-start(bf16[25,64,128]{2,1,0:T(8,128)(2,1)S(1)} %shard_map.61), channel_id=1, source_target_pairs={{4,6},{5,7},{12,14},{13,15},{20,22},{21,23},{28,30},{29,31}} | collective-permute-start | bytes 1228808 | tf_op jit(solution)/shard_map/ppermute | solution.py:407
  36.1 0.7 %collective-permute-start.12 = (bf16[13,64,128]{2,1,0:T(8,128)(2,1)S(1)}, bf16[13,64,128]{2,1,0:T(8,128)(2,1)S(1)}, u32[]{:S(2)}, u32[]{:S(2)}) collective-permute-start(bf16[13,64,128]{2,1,0:T(8,128)(2,1)S(1)} %shard_map.62), channel_id=1, source_target_pairs={{0,2},{1,3},{8,10},{9,11},{16,18},{17,19},{24,26},{25,27}} | collective-permute-start | bytes 638984 | tf_op jit(solution)/shard_map/ppermute | solution.py:407
  36.8 1.0 %shard_map.59 = (f32[24,64,128]{2,1,0:T(8,128)S(1)}, f32[64,128]{1,0:T(8,128)S(1)}) custom-call(bf16[48,64,128]{2,1,0:T(8,128)(2,1)S(1)} %bitcast.25, bf16[24,64,128]{2,1,0:T(8,128)(2,1)S(1)} %get-tuple-element.36.rk0, bf16[24,64,128]{2,1,0:T(8,128)(2,1)S(1)} %collective-permute-done.6.rk1, bf16[24,64,128]{2,1,0:T(8,128)(2,1)S(1)} %get-tuple-element.37.rv0, ...), custom_call_target="tpu_custom_call" | custom-call | flops 2000000000 | bytes 1048576 | tf_op jit(solution)/shard_map/pallas_call | solution.py:385
  37.8 0.9 %shard_map.56 = (f32[24,64,128]{2,1,0:T(8,128)S(1)}, f32[64,128]{1,0:T(8,128)S(1)}) custom-call(bf16[48,64,128]{2,1,0:T(8,128)(2,1)S(1)} %bitcast.26, bf16[48,64,128]{2,1,0:T(8,128)(2,1)S(1)} %bitcast.22, bf16[48,64,128]{2,1,0:T(8,128)(2,1)S(1)} %collective-permute-done.k1, bf16[48,64,128]{2,1,0:T(8,128)(2,1)S(1)} %bitcast.15, ...), custom_call_target="tpu_custom_call" | custom-call | flops 2000000000 | bytes 1048576 | tf_op jit(solution)/shard_map/pallas_call | solution.py:385
  38.7 12.0 %collective-permute-done.8.upper = bf16[25,64,128]{2,1,0:T(8,128)(2,1)S(1)} collective-permute-done((bf16[25,64,128]{2,1,0:T(8,128)(2,1)S(1)}, bf16[25,64,128]{2,1,0:T(8,128)(2,1)S(1)}, u32[]{:S(2)}, u32[]{:S(2)}) %collective-permute-start.8) | collective-permute-done | bytes 409632 | tf_op jit(solution)/shard_map/ppermute | solution.py:407
  50.7 3.8 %collective-permute-done.10.extra = bf16[25,64,128]{2,1,0:T(8,128)(2,1)S(1)} collective-permute-done((bf16[25,64,128]{2,1,0:T(8,128)(2,1)S(1)}, bf16[25,64,128]{2,1,0:T(8,128)(2,1)S(1)}, u32[]{:S(2)}, u32[]{:S(2)}) %collective-permute-start.10) | collective-permute-done | bytes 409632 | tf_op jit(solution)/shard_map/ppermute | solution.py:407
  54.5 0.7 %copy-done.4 = f32[8,48]{1,0:T(8,128)S(1)} copy-done((f32[8,48]{1,0:T(8,128)S(1)}, f32[8,48]{1,0:T(8,128)}, u32[]{:S(2)}) %copy-start.4) | copy-done | bytes 1560
  55.1 3.5 %shard_map.64 = bf16[64,48,128]{2,1,0:T(8,128)(2,1)} custom-call(s32[2]{0:T(128)S(1)} %copy-done.5, f32[8,48]{1,0:T(8,128)S(1)} %copy-done.4, f32[24,64,128]{2,1,0:T(8,128)S(1)} %get-tuple-element.30.other, f32[64,128]{1,0:T(8,128)S(1)} %get-tuple-element.31.other_table, f32[24,64,128]{2,1,0:T(8,128)S(1)} %get-tuple-element.38.mine, ...), custom_call_target="tpu_custom_call" | custom-call | flops 2000000000 | bytes 1048576 | tf_op jit(solution)/shard_map/pallas_call | solution.py:385
  (35 shorter events, 4.9 us)
Async XLA Ops:
  0.0 1.1 %copy-start = (bf16[64,48,128]{2,1,0:T(8,128)(2,1)S(1)}, bf16[64,48,128]{2,1,0:T(8,128)(2,1)}, u32[]{:S(2)}) copy-start(bf16[64,48,128]{2,1,0:T(8,128)(2,1)} %key_rows.1) | copy-start | bytes 2359300
  1.1 1.1 %copy-start.2 = (bf16[64,48,128]{2,1,0:T(8,128)(2,1)S(1)}, bf16[64,48,128]{2,1,0:T(8,128)(2,1)}, u32[]{:S(2)}) copy-start(bf16[64,48,128]{2,1,0:T(8,128)(2,1)} %queries.1) | copy-start | bytes 2359300
  2.3 1.1 %copy-start.6 = (bf16[64,48,128]{2,1,0:T(8,128)(2,1)S(1)}, bf16[64,48,128]{2,1,0:T(8,128)(2,1)}, u32[]{:S(2)}) copy-start(bf16[64,48,128]{2,1,0:T(8,128)(2,1)} %param.7) | copy-start | bytes 2359300
  3.4 1.1 %copy-start.1 = (bf16[64,48,128]{2,1,0:T(8,128)(2,1)S(1)}, bf16[64,48,128]{2,1,0:T(8,128)(2,1)}, u32[]{:S(2)}) copy-start(bf16[64,48,128]{2,1,0:T(8,128)(2,1)} %key_rows.1) | copy-start | bytes 2359300
  4.5 1.1 %copy-start.3 = (bf16[64,48,128]{2,1,0:T(8,128)(2,1)S(1)}, bf16[64,48,128]{2,1,0:T(8,128)(2,1)}, u32[]{:S(2)}) copy-start(bf16[64,48,128]{2,1,0:T(8,128)(2,1)} %queries.1) | copy-start | bytes 2359300
  6.0 10.9 %collective-permute-start.4 = (bf16[24,64,128]{2,1,0:T(8,128)(2,1)S(1)}, bf16[24,64,128]{2,1,0:T(8,128)(2,1)S(1)}, u32[]{:S(2)}, u32[]{:S(2)}) collective-permute-start(bf16[24,64,128]{2,1,0:T(8,128)(2,1)S(1)} %get-tuple-element.34), channel_id=1, source_target_pairs={{0,2},{1,3},{2,0},{3,1},{4,6},{5,7},{6,4},{7,5},{8,10},{9,11},{10,... | collective-permute-start | bytes 1179656 | tf_op jit(solution)/shard_map/ppermute | solution.py:407
  6.6 6.5 %collective-permute-start.11 = (bf16[12,64,128]{2,1,0:T(8,128)(2,1)S(1)}, bf16[12,64,128]{2,1,0:T(8,128)(2,1)S(1)}, u32[]{:S(2)}, u32[]{:S(2)}) collective-permute-start(bf16[12,64,128]{2,1,0:T(8,128)(2,1)S(1)} %get-tuple-element.41), channel_id=1, source_target_pairs={{0,2},{1,3},{2,0},{3,1},{8,10},{9,11},{10,8},{11,9},{16,18},{17,19... | collective-permute-start | bytes 589832 | tf_op jit(solution)/shard_map/ppermute | solution.py:407
  7.3 13.3 %collective-permute-start.5 = (bf16[24,64,128]{2,1,0:T(8,128)(2,1)S(1)}, bf16[24,64,128]{2,1,0:T(8,128)(2,1)S(1)}, u32[]{:S(2)}, u32[]{:S(2)}) collective-permute-start(bf16[24,64,128]{2,1,0:T(8,128)(2,1)S(1)} %get-tuple-element.35), channel_id=1, source_target_pairs={{0,4},{1,5},{2,6},{3,7},{4,0},{5,1},{6,2},{7,3},{8,12},{9,13},{10,... | collective-permute-start | bytes 1179656 | tf_op jit(solution)/shard_map/ppermute | solution.py:407
  10.6 12.8 %collective-permute-start.2 = (bf16[24,64,128]{2,1,0:T(8,128)(2,1)S(1)}, bf16[24,64,128]{2,1,0:T(8,128)(2,1)S(1)}, u32[]{:S(2)}, u32[]{:S(2)}) collective-permute-start(bf16[24,64,128]{2,1,0:T(8,128)(2,1)S(1)} %get-tuple-element.32), channel_id=1, source_target_pairs={{0,2},{1,3},{2,0},{3,1},{6,4},{7,5},{8,10},{9,11},{10,8},{11,9},{1... | collective-permute-start | bytes 1179656 | tf_op jit(solution)/shard_map/ppermute | solution.py:407
  13.0 14.5 %collective-permute-start.3 = (bf16[24,64,128]{2,1,0:T(8,128)(2,1)S(1)}, bf16[24,64,128]{2,1,0:T(8,128)(2,1)S(1)}, u32[]{:S(2)}, u32[]{:S(2)}) collective-permute-start(bf16[24,64,128]{2,1,0:T(8,128)(2,1)S(1)} %get-tuple-element.33), channel_id=1, source_target_pairs={{0,4},{1,5},{2,6},{3,7},{4,0},{5,1},{6,2},{7,3},{8,12},{9,13},{10,... | collective-permute-start | bytes 1179656 | tf_op jit(solution)/shard_map/ppermute | solution.py:407
  13.1 15.8 %collective-permute-start = (bf16[48,64,128]{2,1,0:T(8,128)(2,1)S(1)}, bf16[48,64,128]{2,1,0:T(8,128)(2,1)S(1)}, u32[]{:S(2)}, u32[]{:S(2)}) collective-permute-start(bf16[48,64,128]{2,1,0:T(8,128)(2,1)S(1)} %bitcast.17), channel_id=1, source_target_pairs={{0,1},{1,0},{2,3},{3,2},{4,5},{5,4},{6,7},{7,6},{8,9},{9,8},{10,11... | collective-permute-start | bytes 2359304 | tf_op jit(solution)/shard_map/ppermute | solution.py:407
  16.9 12.0 %collective-permute-start.1 = (bf16[48,64,128]{2,1,0:T(8,128)(2,1)S(1)}, bf16[48,64,128]{2,1,0:T(8,128)(2,1)S(1)}, u32[]{:S(2)}, u32[]{:S(2)}) collective-permute-start(bf16[48,64,128]{2,1,0:T(8,128)(2,1)S(1)} %bitcast.10), channel_id=1, source_target_pairs={{0,1},{1,0},{2,3},{3,2},{4,5},{5,4},{6,7},{7,6},{8,9},{9,8},{10,11... | collective-permute-start | bytes 2359304 | tf_op jit(solution)/shard_map/ppermute | solution.py:407
  20.5 7.2 %collective-permute-start.14 = (bf16[12,64,128]{2,1,0:T(8,128)(2,1)S(1)}, bf16[12,64,128]{2,1,0:T(8,128)(2,1)S(1)}, u32[]{:S(2)}, u32[]{:S(2)}) collective-permute-start(bf16[12,64,128]{2,1,0:T(8,128)(2,1)S(1)} %get-tuple-element.42), channel_id=1, source_target_pairs={{0,2},{1,3},{8,10},{9,11},{16,18},{17,19},{24,26},{25,27}} | collective-permute-start | bytes 589832 | tf_op jit(solution)/shard_map/ppermute | solution.py:407
  23.4 4.8 %collective-permute-start.13 = (bf16[12,64,128]{2,1,0:T(8,128)(2,1)S(1)}, bf16[12,64,128]{2,1,0:T(8,128)(2,1)S(1)}, u32[]{:S(2)}, u32[]{:S(2)}) collective-permute-start(bf16[12,64,128]{2,1,0:T(8,128)(2,1)S(1)} %collective-permute-done.11.q.k0), channel_id=1, source_target_pairs={{2,3},{3,2},{10,11},{11,10},{18,19},{19,18},{26,27},{27,26}} | collective-permute-start | bytes 589832 | tf_op jit(solution)/shard_map/ppermute | solution.py:407
  27.6 1.8 %collective-permute-start.6 = (bf16[24,64,128]{2,1,0:T(8,128)(2,1)S(1)}, bf16[24,64,128]{2,1,0:T(8,128)(2,1)S(1)}, u32[]{:S(2)}, u32[]{:S(2)}) collective-permute-start(bf16[24,64,128]{2,1,0:T(8,128)(2,1)S(1)} %get-tuple-element.36.rk0), channel_id=1, source_target_pairs={{0,1},{1,0},{2,3},{3,2},{4,5},{5,4},{6,7},{7,6},{8,9},{9,8},{10,11... | collective-permute-start | bytes 1179656 | tf_op jit(solution)/shard_map/ppermute | solution.py:407
  27.7 2.3 %collective-permute-start.7 = (bf16[24,64,128]{2,1,0:T(8,128)(2,1)S(1)}, bf16[24,64,128]{2,1,0:T(8,128)(2,1)S(1)}, u32[]{:S(2)}, u32[]{:S(2)}) collective-permute-start(bf16[24,64,128]{2,1,0:T(8,128)(2,1)S(1)} %get-tuple-element.37.rv0), channel_id=1, source_target_pairs={{0,1},{1,0},{2,3},{3,2},{4,5},{5,4},{6,7},{7,6},{8,9},{9,8},{10,11... | collective-permute-start | bytes 1179656 | tf_op jit(solution)/shard_map/ppermute | solution.py:407
  28.2 0.7 %collective-permute-start.15 = (bf16[12,64,128]{2,1,0:T(8,128)(2,1)S(1)}, bf16[12,64,128]{2,1,0:T(8,128)(2,1)S(1)}, u32[]{:S(2)}, u32[]{:S(2)}) collective-permute-start(bf16[12,64,128]{2,1,0:T(8,128)(2,1)S(1)} %collective-permute-done.14.v0), channel_id=1, source_target_pairs={{2,3},{3,2},{10,11},{11,10},{18,19},{19,18},{26,27},{27,26}} | collective-permute-start | bytes 589832 | tf_op jit(solution)/shard_map/ppermute | solution.py:407
  31.0 19.7 %collective-permute-start.8 = (bf16[25,64,128]{2,1,0:T(8,128)(2,1)S(1)}, bf16[25,64,128]{2,1,0:T(8,128)(2,1)S(1)}, u32[]{:S(2)}, u32[]{:S(2)}) collective-permute-start(bf16[25,64,128]{2,1,0:T(8,128)(2,1)S(1)} %shard_map.60), channel_id=1, source_target_pairs={{0,4},{1,5},{2,6},{3,7},{8,12},{9,13},{10,14},{11,15},{16,20},{17,... | collective-permute-start | bytes 1228808 | tf_op jit(solution)/shard_map/ppermute | solution.py:407
  32.3 18.4 %collective-permute-start.9 = (bf16[25,64,128]{2,1,0:T(8,128)(2,1)S(1)}, bf16[25,64,128]{2,1,0:T(8,128)(2,1)S(1)}, u32[]{:S(2)}, u32[]{:S(2)}) collective-permute-start(bf16[25,64,128]{2,1,0:T(8,128)(2,1)S(1)} %shard_map.60), channel_id=1, source_target_pairs={{4,6},{5,7},{6,4},{7,5},{12,14},{13,15},{14,12},{15,13},{20,22},{2... | collective-permute-start | bytes 1228808 | tf_op jit(solution)/shard_map/ppermute | solution.py:407
  34.8 19.7 %collective-permute-start.10 = (bf16[25,64,128]{2,1,0:T(8,128)(2,1)S(1)}, bf16[25,64,128]{2,1,0:T(8,128)(2,1)S(1)}, u32[]{:S(2)}, u32[]{:S(2)}) collective-permute-start(bf16[25,64,128]{2,1,0:T(8,128)(2,1)S(1)} %shard_map.61), channel_id=1, source_target_pairs={{4,6},{5,7},{12,14},{13,15},{20,22},{21,23},{28,30},{29,31}} | collective-permute-start | bytes 1228808 | tf_op jit(solution)/shard_map/ppermute | solution.py:407
  36.1 2.6 %collective-permute-start.12 = (bf16[13,64,128]{2,1,0:T(8,128)(2,1)S(1)}, bf16[13,64,128]{2,1,0:T(8,128)(2,1)S(1)}, u32[]{:S(2)}, u32[]{:S(2)}) collective-permute-start(bf16[13,64,128]{2,1,0:T(8,128)(2,1)S(1)} %shard_map.62), channel_id=1, source_target_pairs={{0,2},{1,3},{8,10},{9,11},{16,18},{17,19},{24,26},{25,27}} | collective-permute-start | bytes 638984 | tf_op jit(solution)/shard_map/ppermute | solution.py:407
  54.5 0.7 %copy-start.4 = (f32[8,48]{1,0:T(8,128)S(1)}, f32[8,48]{1,0:T(8,128)}, u32[]{:S(2)}) copy-start(f32[8,48]{1,0:T(8,128)} %gate_table.1) | copy-start | bytes 4612
  54.5 0.7 %copy-start.5 = (s32[2]{0:T(128)S(1)}, s32[2]{0:T(128)}, u32[]{:S(2)}) copy-start(s32[2]{0:T(128)} %levels.1) | copy-start | bytes 28

commit v3 on v2

--- a/solution.py
+++ b/solution.py
@@ -10,6 +10,7 @@
 
 BLOCK = 128
 LEVELS = 8
+ROOM = 62 << 20
 TILE = 8
 LANES = 32
 
@@ -193,114 +194,163 @@
     return jnp.where(seen, 0.0, -jnp.inf)
 
 
-def first_kernel(queries, key_rows, x1, y1, held, sems):
+def first_kernel(queries, key_rows, value_rows, x1, y1, held, sems):
     span, _ = where_am_i()
     half = x1.shape[0]
-
-    def fetch(array, start, slot):
-        source = array.at[:, pl.ds(start, half), :]
-        return pltpu.make_async_copy(source, held.at[slot], sems.at[slot])
-
-    def load(array, starts):
-        for slot, start in enumerate(starts):
-            fetch(array, start, slot).start()
+    part = half // 2
+
+    def fetch(array, start, count, slot, place=0):
+        source = array.at[:, pl.ds(start, count), :]
+        return pltpu.make_async_copy(source, held.at[slot, :, pl.ds(place, count), :], sems.at[slot])
 
     @pl.when(span == 0)
     def _():
-        load(key_rows, (0, half))
+        for slot in range(2):
+            fetch(key_rows, slot * half, TILE * 2, slot).start()
+            fetch(value_rows, slot * half, TILE * 2, slot, TILE * 2).start()
 
     @pl.when(span == 1)
     def _():
-        load(queries, (0, 0))
+        fetch(queries, 0, TILE * 4, 0).start()
+        fetch(queries, 0, TILE * 4, 1).start()
 
     for slot, out in enumerate((x1, y1)):
-        fetch(queries, 0, slot).wait()
-        for h in range(0, half, TILE):
-            out[h : h + TILE] = jnp.swapaxes(held[slot, :, h : h + TILE, :], 0, 1)
-
-
-def second_kernel(lent, q, k, v, x2, y2, x3, x4):
+        fetch(queries, 0, TILE * 4, slot).wait()
+
+        def turned(start):
+            return jnp.swapaxes(held[slot, :, start : start + TILE, :], 0, 1)
+
+        @pl.when(span == 0)
+        def _():
+            for base, place in ((0, 0), (2 * TILE, part)):
+                out[place : place + TILE] = turned(base)
+                out[place + TILE : place + part] = turned(base + TILE)[: part - TILE]
+
+        @pl.when(span == 1)
+        def _():
+            for start in range(0, half, TILE):
+                out[start : start + TILE] = turned(start)
+
+
+def second_kernel(q, k, v, x2, x3, y2, x4):
     span, block = where_am_i()
-    half = x2.shape[0]
-    y2[...] = v[half:]
-    x4[...] = v[half + lent :]
+    part = x2.shape[0]
+    half = 2 * part
+    lent = x4.shape[0]
+    y2[:part] = k[half + part :]
+    y2[part:] = v[half + part :]
 
     @pl.when(span == 0)
     def _():
-        x2[...] = v[:half]
+        x2[...] = k[part:half]
+        x3[...] = v[part:half]
 
     @pl.when(span == 1)
     def _():
-        x2[...] = q[half:]
+        x2[...] = q[half : half + part]
+        x3[...] = q[half + part :]
 
     @pl.when(block == 0)
     def _():
-        x3[...] = k[half + lent :]
+        x4[: lent // 2] = k[half + lent :]
+        x4[lent // 2 :] = v[half + lent :]
 
     @pl.when(block != 0)
     def _():
-        x3[: half - lent] = q[half : 2 * half - lent]
-
-
-def choose_kernel(x1, y1, x2, y2, keys, visitor, values):
+        x4[...] = q[half : half + lent]
+
+
+def choose_kernel(x, y, out):
     span, _ = where_am_i()
 
     @pl.when(span == 0)
     def _():
-        keys[...] = x1[...]
-        visitor[...] = y1[...]
-        values[...] = x2[...]
+        out[...] = x[...]
 
     @pl.when(span == 1)
     def _():
-        keys[...] = y1[...]
-        visitor[...] = x2[...]
-        values[...] = y2[...]
-
-
-def own_kernel(factor, q, k0, k1, v0, v1, out, table):
+        out[...] = y[...]
+
+
+def choose_second_kernel(x2, x3, y2, out):
+    span, _ = where_am_i()
+    part = x2.shape[0]
+
+    @pl.when(span == 0)
+    def _():
+        out[:part] = x2[...]
+        out[part:] = x3[...]
+
+    @pl.when(span == 1)
+    def _():
+        out[...] = y2[...]
+
+
+def own_kernel(factor, levels, gate_table, q, k0, k1, v0, v1, out, table, gates):
     span, _ = where_am_i()
     rows, width = q.shape[1:]
     half = out.shape[0]
     heads = [(1 - span) * half + h for h in range(half)]
     jobs = [(q[h], rows_of((k0, h), (k1, h)), rows_of((v0, h), (v1, h))) for h in heads]
     store_local(out, table, *attend(jobs, factor), lanes_of(rows, width))
-
-
-def two_blocks(q, received, own, span, half, seen_received, seen_own):
-    rk0, rk1, rv0, rv1 = received
-    k0, k1, v0, v1 = own
-    keys = 4 * rk0.shape[1]
+    level = levels[span]
+    lane = lanes_of(1, width)
+    for group in range(2):
+        row = jnp.zeros((1, width), jnp.float32)
+        for h in range(half):
+            row = jnp.where(lane == h, gate_table[level, group * half + h], row)
+        gates[group : group + 1] = row
+
+
+def hide(keys, seen_first, seen_second):
     place = lax.broadcasted_iota(jnp.int32, (1, keys), 1)
-    shift = jnp.where(place < keys // 2, unless(seen_received), unless(seen_own))
+    return jnp.where(place < keys // 2, unless(seen_first), unless(seen_second))
+
+
+def visit_kernel(factor, chunk, y1, x, got, got1, k0, k1, v0, v1, out, q):
+    span, block = where_am_i()
+    part, rows, width = x.shape
+
+    @pl.when(span == 0)
+    def _():
+        q[...] = y1[chunk * part : (chunk + 1) * part]
+
+    @pl.when(span == 1)
+    def _():
+        q[...] = x[...]
+
+    jobs = []
+    for h in range(part):
+        g = (2 * span + chunk) * part + h
+        jobs.append(
+            (
+                q[h],
+                rows_of((got, h), (got1, h), (k0, g), (k1, g)),
+                rows_of((got, part + h), (got1, part + h), (v0, g), (v1, g)),
+            )
+        )
+    shift = hide(4 * rows, block >= 0, block != 3)
+    store(out, *attend(jobs, factor, shift), lanes_of(rows, width))
+
+
+def stay_kernel(factor, q, a, a1, b, b1, k0, k1, v0, v1, out, table):
+    span, block = where_am_i()
+    rows, width = q.shape[1:]
+    half = out.shape[0]
+    part = half // 2
     jobs = []
     for h in range(half):
         g = span * half + h
+        first, second = (a, a1) if h < part else (b, b1)
+        i = h % part
         jobs.append(
             (
-                q(h, g),
-                rows_of((rk0, h), (rk1, h), (k0, g), (k1, g)),
-                rows_of((rv0, h), (rv1, h), (v0, g), (v1, g)),
+                q[g],
+                rows_of((first, i), (second, i), (k0, g), (k1, g)),
+                rows_of((first, part + i), (second, part + i), (v0, g), (v1, g)),
             )
         )
-    return jobs, shift
-
-
-def visit_kernel(factor, q, rk0, rk1, rv0, rv1, k0, k1, v0, v1, out):
-    span, block = where_am_i()
-    half, rows, width = q.shape
-    jobs, shift = two_blocks(
-        lambda h, g: q[h], (rk0, rk1, rv0, rv1), (k0, k1, v0, v1), span, half, block >= 0, block != 3
-    )
-    store(out, *attend(jobs, factor, shift), lanes_of(rows, width))
-
-
-def stay_kernel(factor, q, rk0, rk1, rv0, rv1, k0, k1, v0, v1, out, table):
-    span, block = where_am_i()
-    rows, width = q.shape[1:]
-    jobs, shift = two_blocks(
-        lambda h, g: q[g], (rk0, rk1, rv0, rv1), (k0, k1, v0, v1), span, out.shape[0], block != 0, block >= 0
-    )
+    shift = hide(4 * rows, block != 0, block >= 0)
     store_local(out, table, *attend(jobs, factor, shift), lanes_of(rows, width))
 
 
@@ -317,92 +367,141 @@
         store(out, *attend(jobs, factor), lanes_of(rows, width))
 
 
-def fetched_kernel(factor, host, first, q, k0, k1, v0, v1, out, table):
+def fetched_kernel(factor, host, first, q, got, got1, out, table):
     _, block = where_am_i()
     heads, rows, width = out.shape
 
     @pl.when(block == host)
     def _():
-        jobs = [(q[first + h], rows_of((k0, h), (k1, h)), rows_of((v0, h), (v1, h))) for h in range(heads)]
+        jobs = [
+            (q[first + h], rows_of((got, h), (got1, h)), rows_of((got, heads + h), (got1, heads + h)))
+            for h in range(heads)
+        ]
         store_local(out, table, *attend(jobs, factor), lanes_of(rows, width))
 
 
-def merge_kernel(
-    levels, gate_table, other, other_table, mine, mine_table, upper, across, extra, lent, fetched, fetched_table, out
+def merged(gate_row, logs, parts_of, half, held, group, out, sem):
+    top = functools.reduce(jnp.maximum, logs)
+    scaled = [jnp.exp2(table - top) for table in logs]
+    ratio = gate_row / sum(scaled)
+    scaled = [s * ratio for s in scaled]
+    for start in range(0, half, TILE):
+        sums = [
+            sum(part.astype(jnp.float32) * s[:, h : h + 1] for part, s in zip(parts_of(h), scaled))
+            for h in range(start, start + TILE)
+        ]
+        together = jnp.swapaxes(jnp.stack(sums), 0, 1)
+        held[:, start : start + TILE, :] = together.astype(held.dtype)
+    leave(held, out, group, sem).start()
+
+
+def leave(held, out, group, sem):
+    half = held.shape[1]
+    return pltpu.make_async_copy(held, out.at[:, pl.ds(group * half, half), :], sem)
+
+
+def logs_of(slab):
+    return joined(slab[slab.shape[0] - 1])
+
+
+def side_by_side(first, second, count):
+    lane = lanes_of(*first.shape)
+    return jnp.where(lane < count, first, pltpu.roll(second, count, 1))
+
+
+def picked(first, second, h, count):
+    return first[h] if h < count else second[h - count]
+
+
+def merge_first_kernel(gates, other, other_table, mine, mine_table, upper, upper2, extra, out, held, sem):
+    span, block = where_am_i()
+    half = mine.shape[0]
+    part = half // 2
+    gate_row = gates[0:1]
+
+    @pl.when(span == 1)
+    def _():
+        logs = [
+            other_table[...],
+            side_by_side(logs_of(upper), logs_of(upper2), part),
+            logs_of(extra) + unless(block == 3),
+        ]
+        merged(
+            gate_row,
+            logs,
+            lambda h: [other[h], picked(upper, upper2, h, part), extra[h]],
+            half, held, 0, out, sem,
+        )
+
+    @pl.when(span == 0)
+    def _():
+        merged(gate_row, [mine_table[...]], lambda h: [mine[h]], half, held, 0, out, sem)
+
+    leave(held, out, 0, sem).wait()
+
+
+def merge_second_kernel(
+    gates, other, other_table, mine, mine_table, across, across2, lent, fetched, fetched_table, _, out, held, sem
 ):
     span, block = where_am_i()
-    half, _, width = mine.shape
+    half = mine.shape[0]
+    part = half // 2
     lent_heads = half - fetched.shape[0]
-    level = levels[span]
-    lane = lanes_of(1, width)
-
-    def finish(first, sources, last=half, begin=0):
-        gates = jnp.zeros((1, width), jnp.float32)
-        for h in range(begin, last):
-            gates = jnp.where(lane == h, gate_table[level, first + h], gates)
-        logs = [table for _, table, _ in sources]
-        top = functools.reduce(jnp.maximum, logs)
-        scaled = [jnp.exp2(table - top) for table in logs]
-        ratio = gates / sum(scaled)
-        scaled = [s * ratio for s in scaled]
-        for start in range(begin, last, TILE // 2):
-            sums = [
-                sum(
-                    parts[h - skip].astype(jnp.float32) * s[:, h : h + 1]
-                    for (parts, _, skip), s in zip(sources, scaled)
-                )
-                for h in range(start, start + TILE // 2)
-            ]
-            together = jnp.swapaxes(jnp.stack(sums), 0, 1)
-            out[:, first + start : first + start + TILE // 2, :] = together.astype(out.dtype)
-
-    def sent(slab, shift=0.0):
-        return slab, joined(slab[slab.shape[0] - 1]) + shift, 0
-
-    def kept(parts, table):
-        return parts, table[...], 0
+    gate_row = gates[1:2]
 
     @pl.when(span == 1)
     def _():
-        finish(0, [kept(other, other_table), sent(upper), sent(extra, unless(block == 3))])
-        finish(half, [kept(mine, mine_table), sent(across)])
+        logs = [mine_table[...], side_by_side(logs_of(across), logs_of(across2), part)]
+        merged(
+            gate_row, logs, lambda h: [mine[h], picked(across, across2, h, part)], half, held, 1, out, sem
+        )
 
     @pl.when(block == 0)
     def _():
-        finish(0, [kept(mine, mine_table)])
-        finish(half, [kept(other, other_table)])
+        merged(gate_row, [other_table[...]], lambda h: [other[h]], half, held, 1, out, sem)
 
     @pl.when(block == 1)
     def _():
-        finish(0, [kept(mine, mine_table)])
-        finish(half, [kept(other, other_table), sent(lent)], last=lent_heads)
-        moved = pltpu.roll(fetched_table[...], lent_heads, 1)
-        finish(half, [kept(other, other_table), (fetched, moved, lent_heads)], begin=lent_heads)
-
-
-def run(kernel, out_shape, operands, scalars=(), space=pltpu.VMEM, scratch=()):
-    in_vmem, in_smem = pl.BlockSpec(memory_space=pltpu.VMEM), pl.BlockSpec(memory_space=pltpu.SMEM)
+        logs = [other_table[...], side_by_side(logs_of(lent), fetched_table[...], lent_heads)]
+        merged(
+            gate_row, logs, lambda h: [other[h], picked(lent, fetched, h, lent_heads)], half, held, 1, out, sem
+        )
+
+    leave(held, out, 1, sem).wait()
+
+
+def run(
+    kernel, out_shape, operands, scalars=(), space=pltpu.VMEM, scratch=(), room=8 << 20, out_space=pltpu.VMEM, into=None
+):
+    in_smem, anywhere = pl.BlockSpec(memory_space=pltpu.SMEM), pl.BlockSpec(memory_space=pl.ANY)
+    inputs = [in_smem] * len(scalars) + [pl.BlockSpec(memory_space=space)] * len(operands)
+    operands = [*scalars, *operands]
+    if into is not None:
+        operands.append(into)
+        inputs.append(anywhere)
     return pl.pallas_call(
         kernel,
         out_shape=out_shape,
-        in_specs=[in_smem] * len(scalars) + [pl.BlockSpec(memory_space=space)] * len(operands),
-        out_specs=jax.tree.map(lambda _: in_vmem, out_shape),
+        in_specs=inputs,
+        out_specs=jax.tree.map(lambda _: pl.BlockSpec(memory_space=out_space), out_shape),
         scratch_shapes=scratch,
-        compiler_params=pltpu.CompilerParams(vmem_limit_bytes=8 << 20),
+        input_output_aliases={} if into is None else {len(operands) - 1: 0},
+        compiler_params=pltpu.CompilerParams(vmem_limit_bytes=room),
         cost_estimate=pl.CostEstimate(flops=2_000_000_000, bytes_accessed=1 << 20, transcendentals=0),
-    )(*scalars, *operands)
+    )(*operands)
 
 
 def by_block(queries, key_rows, value_rows, noise_levels, gate_table):
     rows, heads, width = queries.shape
     half = heads // 2
-    lent = half // 2
+    part = half // 2
+    lent = 2 * (half // 3)
     per_span = lax.axis_size("head")
     share = per_span // 2
     factor = math.log2(math.e) / math.sqrt(width)
     devices = range(2 * per_span)
 
-    def send(block, target):
+    def moved(block, target):
         route = [(p, target(p)) for p in devices if target(p) is not None]
         return lax.ppermute(block, ("span", "head"), route)
 
@@ -418,17 +517,17 @@
     def only(numbers, target):
         return lambda p: target(p) if p // share in numbers else None
 
-    def up(p):
-        return p + per_span if p < per_span else None
-
-    def moved(block, target):
-        return send(block, target)
-
-    def by_head_first(a):
-        return jnp.transpose(a, (1, 0, 2))
-
     def blocks(*counts):
         return tuple(jax.ShapeDtypeStruct((n, rows, width), jnp.bfloat16) for n in counts)
+
+    def slab(n):
+        return blocks(n + 1)[0]
+
+    def kept(n):
+        return (
+            jax.ShapeDtypeStruct((n, rows, width), jnp.float32),
+            jax.ShapeDtypeStruct((rows, width), jnp.float32),
+        )
 
     def kernel(body, out_shape, *operands, **more):
         return run(body, out_shape, operands, **more)
@@ -438,55 +537,65 @@
         blocks(half, half),
         queries,
         key_rows,
+        value_rows,
         space=pl.ANY,
-        scratch=[pltpu.VMEM((2, rows, half, width), jnp.bfloat16), pltpu.SemaphoreType.DMA((2,))],
+        room=ROOM,
+        scratch=[pltpu.VMEM((2, rows, 4 * TILE, width), jnp.bfloat16), pltpu.SemaphoreType.DMA((2,))],
     )
     x1, y1, *raw = lax.optimization_barrier((x1, y1, queries, key_rows, value_rows))
-    q, k, v = map(by_head_first, raw)
-    x2, y2, x3, x4 = kernel(
-        functools.partial(second_kernel, lent), blocks(half, half, half - lent, half - lent), q, k, v
-    )
+    q, k, v = (jnp.transpose(a, (1, 0, 2)) for a in raw)
+    x2, x3, y2, x4 = kernel(second_kernel, blocks(part, part, half, lent), q, k, v)
     x1 = moved(x1, only((0, 1, 3), sideways))
     y1 = moved(y1, other_span)
     own_k, own_v = moved(k, partner), moved(v, partner)
-    x2 = moved(x2, sideways)
+    x2, x3 = moved(x2, sideways), moved(x3, sideways)
     y2 = moved(y2, other_span)
-    x3 = moved(x3, only((0, 1), sideways))
-    x4 = moved(x4, only((0,), sideways))
-
-    def slab(n):
-        return jax.ShapeDtypeStruct((n + 1, rows, width), jnp.bfloat16)
-
-    def kept(n):
-        return (
-            jax.ShapeDtypeStruct((n, rows, width), jnp.float32),
-            jax.ShapeDtypeStruct((rows, width), jnp.float32),
-        )
+    x4 = moved(x4, only((0, 1), sideways))
 
     own = (k, own_k, v, own_v)
-    other = kernel(functools.partial(own_kernel, factor), kept(half), q, *own)
+    *other, gates = kernel(
+        functools.partial(own_kernel, factor),
+        (*kept(half), jax.ShapeDtypeStruct((2, width), jnp.float32)),
+        q,
+        *own,
+        scalars=(noise_levels, gate_table),
+    )
+    a = kernel(choose_kernel, blocks(half)[0], x1, y1)
+    a1 = moved(a, partner)
     extra = kernel(functools.partial(guest_kernel, factor, 2, 0), slab(half), x1, *own)
     extra = moved(extra, only((2,), sideways))
 
-    got_k, visitor, got_v = kernel(choose_kernel, blocks(half, half, half), x1, y1, x2, y2)
-    got_k1, got_v1 = moved(got_k, partner), moved(got_v, partner)
-    received = (got_k, got_k1, got_v, got_v1)
-    away = kernel(functools.partial(visit_kernel, factor), slab(half), visitor, *received, *own)
-    upper = moved(away, up)
-    across = moved(away, only((2, 3), sideways))
-    mine = kernel(functools.partial(stay_kernel, factor), kept(half), q, *received, *own)
-
-    helped = kernel(functools.partial(guest_kernel, factor, 0, half), slab(lent), x3, *own)
+    def visit(chunk, x, got, got1):
+        return kernel(
+            functools.partial(visit_kernel, factor, chunk),
+            slab(part),
+            y1,
+            x,
+            got,
+            got1,
+            *own,
+            scratch=[pltpu.VMEM((part, rows, width), jnp.bfloat16)],
+        )
+
+    away = visit(0, x2, a, a1)
+    upper, across = moved(away, other_span), moved(away, only((2, 3), sideways))
+    b = kernel(choose_second_kernel, blocks(half)[0], x2, x3, y2)
+    b1 = moved(b, partner)
+    away = visit(1, x3, b, b1)
+    upper2, across2 = moved(away, other_span), moved(away, only((2, 3), sideways))
+    helped = kernel(functools.partial(guest_kernel, factor, 0, half), slab(lent), x4, *own)
     helped = moved(helped, only((0,), sideways))
-    x3_1, x4_1 = (moved(a, only((1,), partner)) for a in (x3, x4))
-    fetched = kernel(
-        functools.partial(fetched_kernel, factor, 1, half + lent), kept(half - lent), q, x3, x3_1, x4, x4_1
-    )
-    return run(
-        merge_kernel,
-        jax.ShapeDtypeStruct((rows, heads, width), jnp.bfloat16),
-        (*other, *mine, upper, across, extra, helped, *fetched),
-        (noise_levels, gate_table),
+    x4_1 = moved(x4, only((1,), partner))
+    mine = kernel(functools.partial(stay_kernel, factor), kept(half), q, a, a1, b, b1, *own)
+    fetched = kernel(functools.partial(fetched_kernel, factor, 1, half + lent), kept(half - lent), q, x4, x4_1)
+    outcome = jax.ShapeDtypeStruct((rows, heads, width), jnp.bfloat16)
+    more = dict(
+        out_space=pl.ANY,
+        scratch=[pltpu.VMEM((rows, half, width), jnp.bfloat16), pltpu.SemaphoreType.DMA(())],
+    )
+    out = kernel(merge_first_kernel, outcome, gates, *other, *mine, upper, upper2, extra, **more)
+    return kernel(
+        merge_second_kernel, outcome, gates, *other, *mine, across, across2, helped, *fetched, into=out, **more
     )
 
 
@@ -494,7 +603,7 @@
     rows, heads, _ = queries.shape
     spans, per_span = lax.axis_size("span"), lax.axis_size("head")
     two_by_two = spans == 2 and 2 * rows == BLOCK and per_span * rows == 2 * BLOCK
-    if two_by_two and heads % (2 * TILE) == 0 and heads <= 2 * LANES:
+    if two_by_two and heads == 6 * TILE:
         return by_block(queries, key_rows, value_rows, noise_levels, gate_table)
     return by_head(queries, key_rows, value_rows, noise_levels, gate_table)
 

time: 59.1 us -> 65 us (1.100)
  the two profiles are of different devices: /device:TPU:30 before, /device:TPU:22 now
where the time goes in v3:
time: 65 us; the launch traced here: 64.7 us
  starting transfers between devices  29.2 us (45%)
  waiting for transfers between devices  23 us (35%)
  Pallas kernels  9.66 us (15%)
  local copies, waits for them, and re-layouts  2.48 us (4%)
    ppermute x17, starting transfers between devices, moved(): return lax.ppermute(block, ('span', 'head'), route)  29.2 us
    ppermute x17, waiting for transfers between devices, moved(): return lax.ppermute(block, ('span', 'head'), route)  23 us
    pallas_call x13, Pallas kernels, run(): pl.pallas_call(kernel, out_shape=out_shape, in_specs=inputs, out_specs=ja...  9.66 us
    unnamed x14, local copies, waits for them, and re-layouts  1.87 us
  transfers between devices with their start and end apart: 17, of which 4 were waited for; matrix products, arithmetic and copies ran while one was open for 0% of the time, Pallas kernels for 9%

profile of v3, /device:TPU:22, one launch (start us, length us, event | category | flops | bytes accessed | tf_op | source)
XLA Modules:
  0.0 64.7 jit_solution(6338849963302886497)
XLA Ops:
  0.0 2.3 %shard_map.55 = (bf16[24,64,128]{2,1,0:T(8,128)(2,1)}, bf16[24,64,128]{2,1,0:T(8,128)(2,1)}) custom-call(bf16[64,48,128]{2,1,0:T(8,128)(2,1)} %queries.1, bf16[64,48,128]{2,1,0:T(8,128)(2,1)} %key_rows.1, bf16[64,48,128]{2,1,0:T(8,128)(2,1)} %value_rows.1), custom_call_target="tpu_custom_call" | custom-call | flops 2000000000 | bytes 1048576 | tf_op jit(solution)/shard_map/pallas_call | solution.py:482
  2.5 0.9 %copy-done.3 = bf16[64,48,128]{2,1,0:T(8,128)(2,1)S(1)} copy-done((bf16[64,48,128]{2,1,0:T(8,128)(2,1)S(1)}, bf16[64,48,128]{2,1,0:T(8,128)(2,1)}, u32[]{:S(2)}) %copy-start.3) | copy-done | bytes 786456
  3.7 0.9 %copy-done.4 = bf16[64,48,128]{2,1,0:T(8,128)(2,1)S(1)} copy-done((bf16[64,48,128]{2,1,0:T(8,128)(2,1)S(1)}, bf16[64,48,128]{2,1,0:T(8,128)(2,1)}, u32[]{:S(2)}) %copy-start.4) | copy-done | bytes 786456
  4.9 0.8 %collective-permute-start.11 = (bf16[16,64,128]{2,1,0:T(8,128)(2,1)S(1)}, bf16[16,64,128]{2,1,0:T(8,128)(2,1)S(1)}, u32[]{:S(2)}, u32[]{:S(2)}) collective-permute-start(bf16[16,64,128]{2,1,0:T(8,128)(2,1)S(1)} %get-tuple-element.38), channel_id=1, source_target_pairs={{0,2},{1,3},{2,0},{3,1},{8,10},{9,11},{10,8},{11,9},{16,18},{17,19... | collective-permute-start | bytes 786440 | tf_op jit(solution)/shard_map/ppermute | solution.py:506
  6.3 1.5 %collective-permute-start.6 = (bf16[12,64,128]{2,1,0:T(8,128)(2,1)S(1)}, bf16[12,64,128]{2,1,0:T(8,128)(2,1)S(1)}, u32[]{:S(2)}, u32[]{:S(2)}) collective-permute-start(bf16[12,64,128]{2,1,0:T(8,128)(2,1)S(1)} %get-tuple-element.34), channel_id=1, source_target_pairs={{0,2},{1,3},{2,0},{3,1},{4,6},{5,7},{6,4},{7,5},{8,10},{9,11},{10,... | collective-permute-start | bytes 589832 | tf_op jit(solution)/shard_map/ppermute | solution.py:506
  7.8 2.3 %collective-permute-start.7 = (bf16[24,64,128]{2,1,0:T(8,128)(2,1)S(1)}, bf16[24,64,128]{2,1,0:T(8,128)(2,1)S(1)}, u32[]{:S(2)}, u32[]{:S(2)}) collective-permute-start(bf16[24,64,128]{2,1,0:T(8,128)(2,1)S(1)} %get-tuple-element.35), channel_id=1, source_target_pairs={{0,4},{1,5},{2,6},{3,7},{4,0},{5,1},{6,2},{7,3},{8,12},{9,13},{10,... | collective-permute-start | bytes 1179656 | tf_op jit(solution)/shard_map/ppermute | solution.py:506
  10.1 3.5 %collective-permute-done.5.x2.x = bf16[12,64,128]{2,1,0:T(8,128)(2,1)S(1)} collective-permute-done((bf16[12,64,128]{2,1,0:T(8,128)(2,1)S(1)}, bf16[12,64,128]{2,1,0:T(8,128)(2,1)S(1)}, u32[]{:S(2)}, u32[]{:S(2)}) %collective-permute-start.5) | collective-permute-done | bytes 196640 | tf_op jit(solution)/shard_map/ppermute | solution.py:506
  13.6 7.3 %collective-permute-start.3 = (bf16[24,64,128]{2,1,0:T(8,128)(2,1)S(1)}, bf16[24,64,128]{2,1,0:T(8,128)(2,1)S(1)}, u32[]{:S(2)}, u32[]{:S(2)}) collective-permute-start(bf16[24,64,128]{2,1,0:T(8,128)(2,1)S(1)} %copy-done.6), channel_id=1, source_target_pairs={{0,4},{1,5},{2,6},{3,7},{4,0},{5,1},{6,2},{7,3},{8,12},{9,13},{10,... | collective-permute-start | bytes 1179656 | tf_op jit(solution)/shard_map/ppermute | solution.py:506
  20.9 2.5 %collective-permute-start.2 = (bf16[24,64,128]{2,1,0:T(8,128)(2,1)S(1)}, bf16[24,64,128]{2,1,0:T(8,128)(2,1)S(1)}, u32[]{:S(2)}, u32[]{:S(2)}) collective-permute-start(bf16[24,64,128]{2,1,0:T(8,128)(2,1)S(1)} %copy-done.5), channel_id=1, source_target_pairs={{0,2},{1,3},{2,0},{3,1},{6,4},{7,5},{8,10},{9,11},{10,8},{11,9},{1... | collective-permute-start | bytes 1179656 | tf_op jit(solution)/shard_map/ppermute | solution.py:506
  23.3 0.7 %collective-permute-start.13 = (bf16[16,64,128]{2,1,0:T(8,128)(2,1)S(1)}, bf16[16,64,128]{2,1,0:T(8,128)(2,1)S(1)}, u32[]{:S(2)}, u32[]{:S(2)}) collective-permute-start(bf16[16,64,128]{2,1,0:T(8,128)(2,1)S(1)} %collective-permute-done.11.q.got), channel_id=1, source_target_pairs={{2,3},{3,2},{10,11},{11,10},{18,19},{19,18},{26,27},{27,26}} | collective-permute-start | bytes 786440 | tf_op jit(solution)/shard_map/ppermute | solution.py:506
  24.1 3.9 %collective-permute-done.3.y.y1 = bf16[24,64,128]{2,1,0:T(8,128)(2,1)S(1)} collective-permute-done((bf16[24,64,128]{2,1,0:T(8,128)(2,1)S(1)}, bf16[24,64,128]{2,1,0:T(8,128)(2,1)S(1)}, u32[]{:S(2)}, u32[]{:S(2)}) %collective-permute-start.3) | collective-permute-done | bytes 393248 | tf_op jit(solution)/shard_map/ppermute | solution.py:506
  28.0 4.3 %collective-permute-done.2.x.q = bf16[24,64,128]{2,1,0:T(8,128)(2,1)S(1)} collective-permute-done((bf16[24,64,128]{2,1,0:T(8,128)(2,1)S(1)}, bf16[24,64,128]{2,1,0:T(8,128)(2,1)S(1)}, u32[]{:S(2)}, u32[]{:S(2)}) %collective-permute-start.2) | collective-permute-done | bytes 393248 | tf_op jit(solution)/shard_map/ppermute | solution.py:506
  32.5 0.7 %shard_map.62 = bf16[13,64,128]{2,1,0:T(8,128)(2,1)S(1)} custom-call(bf16[24,64,128]{2,1,0:T(8,128)(2,1)S(1)} %collective-permute-done.3.y.y1, bf16[12,64,128]{2,1,0:T(8,128)(2,1)S(1)} %collective-permute-done.6.x3.x, bf16[24,64,128]{2,1,0:T(8,128)(2,1)S(1)} %shard_map.59.b.got, bf16[24,64,128]{2,1,0:T(8,128)(2,1)S(1)} %collective-permute-done.8.b1.got1, ...), custom_call_target="tpu_custom_call" | custom-call | flops 2000000000 | bytes 1048576 | tf_op jit(solution)/shard_map/pallas_call | solution.py:482
  33.2 5.6 %collective-permute-start.15 = (bf16[13,64,128]{2,1,0:T(8,128)(2,1)S(1)}, bf16[13,64,128]{2,1,0:T(8,128)(2,1)S(1)}, u32[]{:S(2)}, u32[]{:S(2)}) collective-permute-start(bf16[13,64,128]{2,1,0:T(8,128)(2,1)S(1)} %shard_map.62), channel_id=1, source_target_pairs={{0,4},{1,5},{2,6},{3,7},{4,0},{5,1},{6,2},{7,3},{8,12},{9,13},{10,... | collective-permute-start | bytes 638984 | tf_op jit(solution)/shard_map/ppermute | solution.py:506
  38.8 1.9 %collective-permute-start.10 = (bf16[13,64,128]{2,1,0:T(8,128)(2,1)S(1)}, bf16[13,64,128]{2,1,0:T(8,128)(2,1)S(1)}, u32[]{:S(2)}, u32[]{:S(2)}) collective-permute-start(bf16[13,64,128]{2,1,0:T(8,128)(2,1)S(1)} %shard_map.62), channel_id=1, source_target_pairs={{4,6},{5,7},{6,4},{7,5},{12,14},{13,15},{14,12},{15,13},{20,22},{2... | collective-permute-start | bytes 638984 | tf_op jit(solution)/shard_map/ppermute | solution.py:506
  40.8 0.7 %shard_map.61 = bf16[13,64,128]{2,1,0:T(8,128)(2,1)S(1)} custom-call(bf16[24,64,128]{2,1,0:T(8,128)(2,1)S(1)} %collective-permute-done.3.y.y1, bf16[12,64,128]{2,1,0:T(8,128)(2,1)S(1)} %collective-permute-done.5.x2.x, bf16[24,64,128]{2,1,0:T(8,128)(2,1)S(1)} %shard_map.57.a.got, bf16[24,64,128]{2,1,0:T(8,128)(2,1)S(1)} %collective-permute-done.4.a1.got1, ...), custom_call_target="tpu_custom_call" | custom-call | flops 2000000000 | bytes 1048576 | tf_op jit(solution)/shard_map/pallas_call | solution.py:482
  41.6 3.9 %collective-permute-start.9 = (bf16[13,64,128]{2,1,0:T(8,128)(2,1)S(1)}, bf16[13,64,128]{2,1,0:T(8,128)(2,1)S(1)}, u32[]{:S(2)}, u32[]{:S(2)}) collective-permute-start(bf16[13,64,128]{2,1,0:T(8,128)(2,1)S(1)} %shard_map.61), channel_id=1, source_target_pairs={{4,6},{5,7},{6,4},{7,5},{12,14},{13,15},{14,12},{15,13},{20,22},{2... | collective-permute-start | bytes 638984 | tf_op jit(solution)/shard_map/ppermute | solution.py:506
  45.5 1.3 %collective-permute-start.16 = (bf16[25,64,128]{2,1,0:T(8,128)(2,1)S(1)}, bf16[25,64,128]{2,1,0:T(8,128)(2,1)S(1)}, u32[]{:S(2)}, u32[]{:S(2)}) collective-permute-start(bf16[25,64,128]{2,1,0:T(8,128)(2,1)S(1)} %shard_map.65), channel_id=1, source_target_pairs={{4,6},{5,7},{12,14},{13,15},{20,22},{21,23},{28,30},{29,31}} | collective-permute-start | bytes 1228808 | tf_op jit(solution)/shard_map/ppermute | solution.py:506
  46.8 1.0 %shard_map.60 = (f32[24,64,128]{2,1,0:T(8,128)S(1)}, f32[64,128]{1,0:T(8,128)S(1)}) custom-call(bf16[48,64,128]{2,1,0:T(8,128)(2,1)S(1)} %bitcast.27, bf16[24,64,128]{2,1,0:T(8,128)(2,1)S(1)} %shard_map.57.a.got, bf16[24,64,128]{2,1,0:T(8,128)(2,1)S(1)} %collective-permute-done.4.a1.got1, bf16[24,64,128]{2,1,0:T(8,128)(2,1)S(1)} %shard_map.59.b.got, ...), custom_call_target="tpu_custom_call" | custom-call | flops 2000000000 | bytes 1048576 | tf_op jit(solution)/shard_map/pallas_call | solution.py:482
  47.9 0.7 %collective-permute-start.12 = (bf16[17,64,128]{2,1,0:T(8,128)(2,1)S(1)}, bf16[17,64,128]{2,1,0:T(8,128)(2,1)S(1)}, u32[]{:S(2)}, u32[]{:S(2)}) collective-permute-start(bf16[17,64,128]{2,1,0:T(8,128)(2,1)S(1)} %shard_map.63), channel_id=1, source_target_pairs={{0,2},{1,3},{8,10},{9,11},{16,18},{17,19},{24,26},{25,27}} | collective-permute-start | bytes 835592 | tf_op jit(solution)/shard_map/ppermute | solution.py:506
  48.6 1.5 %shard_map.56 = (f32[24,64,128]{2,1,0:T(8,128)S(1)}, f32[64,128]{1,0:T(8,128)S(1)}, f32[2,128]{1,0:T(2,128)S(1)}) custom-call(s32[2]{0:T(128)S(1)} %copy-done.1, f32[8,48]{1,0:T(8,128)S(1)} %copy-done, bf16[48,64,128]{2,1,0:T(8,128)(2,1)S(1)} %bitcast.28, bf16[48,64,128]{2,1,0:T(8,128)(2,1)S(1)} %bitcast.24, ...), custom_call_target="tpu_custom_call" | custom-call | flops 2000000000 | bytes 1048576 | tf_op jit(solution)/shard_map/pallas_call | solution.py:482
  50.1 11.3 %collective-permute-done.16.extra = bf16[25,64,128]{2,1,0:T(8,128)(2,1)S(1)} collective-permute-done((bf16[25,64,128]{2,1,0:T(8,128)(2,1)S(1)}, bf16[25,64,128]{2,1,0:T(8,128)(2,1)S(1)}, u32[]{:S(2)}, u32[]{:S(2)}) %collective-permute-start.16) | collective-permute-done | bytes 409632 | tf_op jit(solution)/shard_map/ppermute | solution.py:506
  61.4 1.7 %shard_map.66._ = bf16[64,48,128]{2,1,0:T(8,128)(2,1)} custom-call(f32[2,128]{1,0:T(2,128)S(1)} %get-tuple-element.28.gates, f32[24,64,128]{2,1,0:T(8,128)S(1)} %get-tuple-element.29.other, f32[64,128]{1,0:T(8,128)S(1)} %get-tuple-element.30.other_table, f32[24,64,128]{2,1,0:T(8,128)S(1)} %get-tuple-element.36.mine, ...), custom_call_target="tpu_custom_call" | custom-call | flops 2000000000 | bytes 1048576 | tf_op jit(solution)/shard_map/pallas_call | solution.py:482
  63.2 1.5 %shard_map.67 = bf16[64,48,128]{2,1,0:T(8,128)(2,1)} custom-call(f32[2,128]{1,0:T(2,128)S(1)} %get-tuple-element.28.gates, f32[24,64,128]{2,1,0:T(8,128)S(1)} %get-tuple-element.29.other, f32[64,128]{1,0:T(8,128)S(1)} %get-tuple-element.30.other_table, f32[24,64,128]{2,1,0:T(8,128)S(1)} %get-tuple-element.36.mine, ...), custom_call_target="tpu_custom_call", output_to_operand_aliasing={{}: (10, {})} | custom-call | flops 2000000000 | bytes 1048576 | tf_op jit(solution)/shard_map/pallas_call | solution.py:482
  (40 shorter events, 1.6 us)
Async XLA Ops:
  0.0 2.3 %copy-start.2 = (bf16[64,48,128]{2,1,0:T(8,128)(2,1)S(1)}, bf16[64,48,128]{2,1,0:T(8,128)(2,1)}, u32[]{:S(2)}) copy-start(bf16[64,48,128]{2,1,0:T(8,128)(2,1)} %value_rows.1) | copy-start | bytes 2359300
  2.3 1.1 %copy-start.3 = (bf16[64,48,128]{2,1,0:T(8,128)(2,1)S(1)}, bf16[64,48,128]{2,1,0:T(8,128)(2,1)}, u32[]{:S(2)}) copy-start(bf16[64,48,128]{2,1,0:T(8,128)(2,1)} %key_rows.1) | copy-start | bytes 2359300
  3.5 1.1 %copy-start.4 = (bf16[64,48,128]{2,1,0:T(8,128)(2,1)S(1)}, bf16[64,48,128]{2,1,0:T(8,128)(2,1)}, u32[]{:S(2)}) copy-start(bf16[64,48,128]{2,1,0:T(8,128)(2,1)} %queries.1) | copy-start | bytes 2359300
  4.8 8.8 %copy-start.6 = (bf16[24,64,128]{2,1,0:T(8,128)(2,1)S(1)}, bf16[24,64,128]{2,1,0:T(8,128)(2,1)}, u32[]{:S(2)}) copy-start(bf16[24,64,128]{2,1,0:T(8,128)(2,1)} %get-tuple-element.32) | copy-start | bytes 1179652
  4.8 16.1 %copy-start.5 = (bf16[24,64,128]{2,1,0:T(8,128)(2,1)S(1)}, bf16[24,64,128]{2,1,0:T(8,128)(2,1)}, u32[]{:S(2)}) copy-start(bf16[24,64,128]{2,1,0:T(8,128)(2,1)} %get-tuple-element.31) | copy-start | bytes 1179652
  4.9 15.9 %collective-permute-start.11 = (bf16[16,64,128]{2,1,0:T(8,128)(2,1)S(1)}, bf16[16,64,128]{2,1,0:T(8,128)(2,1)S(1)}, u32[]{:S(2)}, u32[]{:S(2)}) collective-permute-start(bf16[16,64,128]{2,1,0:T(8,128)(2,1)S(1)} %get-tuple-element.38), channel_id=1, source_target_pairs={{0,2},{1,3},{2,0},{3,1},{8,10},{9,11},{10,8},{11,9},{16,18},{17,19... | collective-permute-start | bytes 786440 | tf_op jit(solution)/shard_map/ppermute | solution.py:506
  5.7 7.8 %collective-permute-start.5 = (bf16[12,64,128]{2,1,0:T(8,128)(2,1)S(1)}, bf16[12,64,128]{2,1,0:T(8,128)(2,1)S(1)}, u32[]{:S(2)}, u32[]{:S(2)}) collective-permute-start(bf16[12,64,128]{2,1,0:T(8,128)(2,1)S(1)} %get-tuple-element.33), channel_id=1, source_target_pairs={{0,2},{1,3},{2,0},{3,1},{4,6},{5,7},{6,4},{7,5},{8,10},{9,11},{10,... | collective-permute-start | bytes 589832 | tf_op jit(solution)/shard_map/ppermute | solution.py:506
  6.3 14.5 %collective-permute-start.6 = (bf16[12,64,128]{2,1,0:T(8,128)(2,1)S(1)}, bf16[12,64,128]{2,1,0:T(8,128)(2,1)S(1)}, u32[]{:S(2)}, u32[]{:S(2)}) collective-permute-start(bf16[12,64,128]{2,1,0:T(8,128)(2,1)S(1)} %get-tuple-element.34), channel_id=1, source_target_pairs={{0,2},{1,3},{2,0},{3,1},{4,6},{5,7},{6,4},{7,5},{8,10},{9,11},{10,... | collective-permute-start | bytes 589832 | tf_op jit(solution)/shard_map/ppermute | solution.py:506
  7.8 15.5 %collective-permute-start.7 = (bf16[24,64,128]{2,1,0:T(8,128)(2,1)S(1)}, bf16[24,64,128]{2,1,0:T(8,128)(2,1)S(1)}, u32[]{:S(2)}, u32[]{:S(2)}) collective-permute-start(bf16[24,64,128]{2,1,0:T(8,128)(2,1)S(1)} %get-tuple-element.35), channel_id=1, source_target_pairs={{0,4},{1,5},{2,6},{3,7},{4,0},{5,1},{6,2},{7,3},{8,12},{9,13},{10,... | collective-permute-start | bytes 1179656 | tf_op jit(solution)/shard_map/ppermute | solution.py:506
  10.1 22.4 %collective-permute-start = (bf16[48,64,128]{2,1,0:T(8,128)(2,1)S(1)}, bf16[48,64,128]{2,1,0:T(8,128)(2,1)S(1)}, u32[]{:S(2)}, u32[]{:S(2)}) collective-permute-start(bf16[48,64,128]{2,1,0:T(8,128)(2,1)S(1)} %bitcast.18), channel_id=1, source_target_pairs={{0,1},{1,0},{2,3},{3,2},{4,5},{5,4},{6,7},{7,6},{8,9},{9,8},{10,11... | collective-permute-start | bytes 2359304 | tf_op jit(solution)/shard_map/ppermute | solution.py:506
  13.6 14.4 %collective-permute-start.3 = (bf16[24,64,128]{2,1,0:T(8,128)(2,1)S(1)}, bf16[24,64,128]{2,1,0:T(8,128)(2,1)S(1)}, u32[]{:S(2)}, u32[]{:S(2)}) collective-permute-start(bf16[24,64,128]{2,1,0:T(8,128)(2,1)S(1)} %copy-done.6), channel_id=1, source_target_pairs={{0,4},{1,5},{2,6},{3,7},{4,0},{5,1},{6,2},{7,3},{8,12},{9,13},{10,... | collective-permute-start | bytes 1179656 | tf_op jit(solution)/shard_map/ppermute | solution.py:506
  20.8 11.6 %collective-permute-start.1 = (bf16[48,64,128]{2,1,0:T(8,128)(2,1)S(1)}, bf16[48,64,128]{2,1,0:T(8,128)(2,1)S(1)}, u32[]{:S(2)}, u32[]{:S(2)}) collective-permute-start(bf16[48,64,128]{2,1,0:T(8,128)(2,1)S(1)} %bitcast.10), channel_id=1, source_target_pairs={{0,1},{1,0},{2,3},{3,2},{4,5},{5,4},{6,7},{7,6},{8,9},{9,8},{10,11... | collective-permute-start | bytes 2359304 | tf_op jit(solution)/shard_map/ppermute | solution.py:506
  20.9 11.5 %collective-permute-start.2 = (bf16[24,64,128]{2,1,0:T(8,128)(2,1)S(1)}, bf16[24,64,128]{2,1,0:T(8,128)(2,1)S(1)}, u32[]{:S(2)}, u32[]{:S(2)}) collective-permute-start(bf16[24,64,128]{2,1,0:T(8,128)(2,1)S(1)} %copy-done.5), channel_id=1, source_target_pairs={{0,2},{1,3},{2,0},{3,1},{6,4},{7,5},{8,10},{9,11},{10,8},{11,9},{1... | collective-permute-start | bytes 1179656 | tf_op jit(solution)/shard_map/ppermute | solution.py:506
  23.3 9.1 %collective-permute-start.13 = (bf16[16,64,128]{2,1,0:T(8,128)(2,1)S(1)}, bf16[16,64,128]{2,1,0:T(8,128)(2,1)S(1)}, u32[]{:S(2)}, u32[]{:S(2)}) collective-permute-start(bf16[16,64,128]{2,1,0:T(8,128)(2,1)S(1)} %collective-permute-done.11.q.got), channel_id=1, source_target_pairs={{2,3},{3,2},{10,11},{11,10},{18,19},{19,18},{26,27},{27,26}} | collective-permute-start | bytes 786440 | tf_op jit(solution)/shard_map/ppermute | solution.py:506
  28.0 4.5 %collective-permute-start.8 = (bf16[24,64,128]{2,1,0:T(8,128)(2,1)S(1)}, bf16[24,64,128]{2,1,0:T(8,128)(2,1)S(1)}, u32[]{:S(2)}, u32[]{:S(2)}) collective-permute-start(bf16[24,64,128]{2,1,0:T(8,128)(2,1)S(1)} %shard_map.59.b.got), channel_id=1, source_target_pairs={{0,1},{1,0},{2,3},{3,2},{4,5},{5,4},{6,7},{7,6},{8,9},{9,8},{10,11... | collective-permute-start | bytes 1179656 | tf_op jit(solution)/shard_map/ppermute | solution.py:506
  32.4 8.4 %collective-permute-start.4 = (bf16[24,64,128]{2,1,0:T(8,128)(2,1)S(1)}, bf16[24,64,128]{2,1,0:T(8,128)(2,1)S(1)}, u32[]{:S(2)}, u32[]{:S(2)}) collective-permute-start(bf16[24,64,128]{2,1,0:T(8,128)(2,1)S(1)} %shard_map.57.a.got), channel_id=1, source_target_pairs={{0,1},{1,0},{2,3},{3,2},{4,5},{5,4},{6,7},{7,6},{8,9},{9,8},{10,11... | collective-permute-start | bytes 1179656 | tf_op jit(solution)/shard_map/ppermute | solution.py:506
  33.2 14.7 %collective-permute-start.15 = (bf16[13,64,128]{2,1,0:T(8,128)(2,1)S(1)}, bf16[13,64,128]{2,1,0:T(8,128)(2,1)S(1)}, u32[]{:S(2)}, u32[]{:S(2)}) collective-permute-start(bf16[13,64,128]{2,1,0:T(8,128)(2,1)S(1)} %shard_map.62), channel_id=1, source_target_pairs={{0,4},{1,5},{2,6},{3,7},{4,0},{5,1},{6,2},{7,3},{8,12},{9,13},{10,... | collective-permute-start | bytes 638984 | tf_op jit(solution)/shard_map/ppermute | solution.py:506
  38.8 24.3 %collective-permute-start.10 = (bf16[13,64,128]{2,1,0:T(8,128)(2,1)S(1)}, bf16[13,64,128]{2,1,0:T(8,128)(2,1)S(1)}, u32[]{:S(2)}, u32[]{:S(2)}) collective-permute-start(bf16[13,64,128]{2,1,0:T(8,128)(2,1)S(1)} %shard_map.62), channel_id=1, source_target_pairs={{4,6},{5,7},{6,4},{7,5},{12,14},{13,15},{14,12},{15,13},{20,22},{2... | collective-permute-start | bytes 638984 | tf_op jit(solution)/shard_map/ppermute | solution.py:506
  41.5 8.6 %collective-permute-start.14 = (bf16[13,64,128]{2,1,0:T(8,128)(2,1)S(1)}, bf16[13,64,128]{2,1,0:T(8,128)(2,1)S(1)}, u32[]{:S(2)}, u32[]{:S(2)}) collective-permute-start(bf16[13,64,128]{2,1,0:T(8,128)(2,1)S(1)} %shard_map.61), channel_id=1, source_target_pairs={{0,4},{1,5},{2,6},{3,7},{4,0},{5,1},{6,2},{7,3},{8,12},{9,13},{10,... | collective-permute-start | bytes 638984 | tf_op jit(solution)/shard_map/ppermute | solution.py:506
  41.6 21.6 %collective-permute-start.9 = (bf16[13,64,128]{2,1,0:T(8,128)(2,1)S(1)}, bf16[13,64,128]{2,1,0:T(8,128)(2,1)S(1)}, u32[]{:S(2)}, u32[]{:S(2)}) collective-permute-start(bf16[13,64,128]{2,1,0:T(8,128)(2,1)S(1)} %shard_map.61), channel_id=1, source_target_pairs={{4,6},{5,7},{6,4},{7,5},{12,14},{13,15},{14,12},{15,13},{20,22},{2... | collective-permute-start | bytes 638984 | tf_op jit(solution)/shard_map/ppermute | solution.py:506
  45.5 15.9 %collective-permute-start.16 = (bf16[25,64,128]{2,1,0:T(8,128)(2,1)S(1)}, bf16[25,64,128]{2,1,0:T(8,128)(2,1)S(1)}, u32[]{:S(2)}, u32[]{:S(2)}) collective-permute-start(bf16[25,64,128]{2,1,0:T(8,128)(2,1)S(1)} %shard_map.65), channel_id=1, source_target_pairs={{4,6},{5,7},{12,14},{13,15},{20,22},{21,23},{28,30},{29,31}} | collective-permute-start | bytes 1228808 | tf_op jit(solution)/shard_map/ppermute | solution.py:506
  47.8 0.8 %copy-start = (f32[8,48]{1,0:T(8,128)S(1)}, f32[8,48]{1,0:T(8,128)}, u32[]{:S(2)}) copy-start(f32[8,48]{1,0:T(8,128)} %gate_table.1) | copy-start | bytes 4612
  47.8 0.8 %copy-start.1 = (s32[2]{0:T(128)S(1)}, s32[2]{0:T(128)}, u32[]{:S(2)}) copy-start(s32[2]{0:T(128)} %levels.1) | copy-start | bytes 28
  47.9 15.3 %collective-permute-start.12 = (bf16[17,64,128]{2,1,0:T(8,128)(2,1)S(1)}, bf16[17,64,128]{2,1,0:T(8,128)(2,1)S(1)}, u32[]{:S(2)}, u32[]{:S(2)}) collective-permute-start(bf16[17,64,128]{2,1,0:T(8,128)(2,1)S(1)} %shard_map.63), channel_id=1, source_target_pairs={{0,2},{1,3},{8,10},{9,11},{16,18},{17,19},{24,26},{25,27}} | collective-permute-start | bytes 835592 | tf_op jit(solution)/shard_map/ppermute | solution.py:506

commit v4 on v3

--- a/solution.py
+++ b/solution.py
@@ -195,7 +195,7 @@
 
 
 def first_kernel(queries, key_rows, value_rows, x1, y1, held, sems):
-    span, _ = where_am_i()
+    span, block = where_am_i()
     half = x1.shape[0]
     part = half // 2
 
@@ -203,30 +203,31 @@
         source = array.at[:, pl.ds(start, count), :]
         return pltpu.make_async_copy(source, held.at[slot, :, pl.ds(place, count), :], sems.at[slot])
 
-    @pl.when(span == 0)
-    def _():
-        for slot in range(2):
+    pairs = (block != 3, span == 0)
+    for slot, of_keys in enumerate(pairs):
+
+        @pl.when(of_keys)
+        def _():
             fetch(key_rows, slot * half, TILE * 2, slot).start()
             fetch(value_rows, slot * half, TILE * 2, slot, TILE * 2).start()
 
-    @pl.when(span == 1)
-    def _():
-        fetch(queries, 0, TILE * 4, 0).start()
-        fetch(queries, 0, TILE * 4, 1).start()
-
-    for slot, out in enumerate((x1, y1)):
+        @pl.when(jnp.logical_not(of_keys))
+        def _():
+            fetch(queries, 0, TILE * 4, slot).start()
+
+    for slot, (out, of_keys) in enumerate(zip((x1, y1), pairs)):
         fetch(queries, 0, TILE * 4, slot).wait()
 
         def turned(start):
             return jnp.swapaxes(held[slot, :, start : start + TILE, :], 0, 1)
 
-        @pl.when(span == 0)
+        @pl.when(of_keys)
         def _():
             for base, place in ((0, 0), (2 * TILE, part)):
                 out[place : place + TILE] = turned(base)
                 out[place + TILE : place + part] = turned(base + TILE)[: part - TILE]
 
-        @pl.when(span == 1)
+        @pl.when(jnp.logical_not(of_keys))
         def _():
             for start in range(0, half, TILE):
                 out[start : start + TILE] = turned(start)
@@ -236,7 +237,7 @@
     span, block = where_am_i()
     part = x2.shape[0]
     half = 2 * part
-    lent = x4.shape[0]
+    taken = x4.shape[0] // 2
     y2[:part] = k[half + part :]
     y2[part:] = v[half + part :]
 
@@ -252,12 +253,12 @@
 
     @pl.when(block == 0)
     def _():
-        x4[: lent // 2] = k[half + lent :]
-        x4[lent // 2 :] = v[half + lent :]
+        x4[:taken] = k[2 * half - taken :]
+        x4[taken:] = v[2 * half - taken :]
 
     @pl.when(block != 0)
     def _():
-        x4[...] = q[half : half + lent]
+        x4[...] = q[half : half + 2 * taken]
 
 
 def choose_kernel(x, y, out):
@@ -354,14 +355,14 @@
     store_local(out, table, *attend(jobs, factor, shift), lanes_of(rows, width))
 
 
-def guest_kernel(factor, host, first, q, k0, k1, v0, v1, out):
+def guest_kernel(factor, host, first, skip, q, k0, k1, v0, v1, out):
     _, block = where_am_i()
-    heads, rows, width = q.shape
+    heads, rows, width = out.shape[0] - 1, *q.shape[1:]
 
     @pl.when(block == host)
     def _():
         jobs = [
-            (q[h], rows_of((k0, first + h), (k1, first + h)), rows_of((v0, first + h), (v1, first + h)))
+            (q[skip + h], rows_of((k0, first + h), (k1, first + h)), rows_of((v0, first + h), (v1, first + h)))
             for h in range(heads)
         ]
         store(out, *attend(jobs, factor), lanes_of(rows, width))
@@ -413,23 +414,32 @@
     return first[h] if h < count else second[h - count]
 
 
-def merge_first_kernel(gates, other, other_table, mine, mine_table, upper, upper2, extra, out, held, sem):
+def merge_first_kernel(
+    gates, other, other_table, mine, mine_table, upper, upper2, extra, third, third_table, out, held, sem
+):
     span, block = where_am_i()
     half = mine.shape[0]
     part = half // 2
     gate_row = gates[0:1]
 
-    @pl.when(span == 1)
+    @pl.when(block == 2)
+    def _():
+        logs = [other_table[...], side_by_side(logs_of(upper), logs_of(upper2), part)]
+        merged(
+            gate_row, logs, lambda h: [other[h], picked(upper, upper2, h, part)], half, held, 0, out, sem
+        )
+
+    @pl.when(block == 3)
     def _():
         logs = [
             other_table[...],
             side_by_side(logs_of(upper), logs_of(upper2), part),
-            logs_of(extra) + unless(block == 3),
+            side_by_side(third_table[...], logs_of(extra), part),
         ]
         merged(
             gate_row,
             logs,
-            lambda h: [other[h], picked(upper, upper2, h, part), extra[h]],
+            lambda h: [other[h], picked(upper, upper2, h, part), picked(third, extra, h, part)],
             half, held, 0, out, sem,
         )
 
@@ -495,7 +505,7 @@
     rows, heads, width = queries.shape
     half = heads // 2
     part = half // 2
-    lent = 2 * (half // 3)
+    lent = half // 2
     per_span = lax.axis_size("head")
     share = per_span // 2
     factor = math.log2(math.e) / math.sqrt(width)
@@ -516,6 +526,9 @@
 
     def only(numbers, target):
         return lambda p: target(p) if p // share in numbers else None
+
+    def up(p):
+        return p + per_span if p < per_span else None
 
     def blocks(*counts):
         return tuple(jax.ShapeDtypeStruct((n, rows, width), jnp.bfloat16) for n in counts)
@@ -544,8 +557,8 @@
     )
     x1, y1, *raw = lax.optimization_barrier((x1, y1, queries, key_rows, value_rows))
     q, k, v = (jnp.transpose(a, (1, 0, 2)) for a in raw)
-    x2, x3, y2, x4 = kernel(second_kernel, blocks(part, part, half, lent), q, k, v)
-    x1 = moved(x1, only((0, 1, 3), sideways))
+    x2, x3, y2, x4 = kernel(second_kernel, blocks(part, part, half, 2 * (half - lent)), q, k, v)
+    x1 = moved(x1, sideways)
     y1 = moved(y1, other_span)
     own_k, own_v = moved(k, partner), moved(v, partner)
     x2, x3 = moved(x2, sideways), moved(x3, sideways)
@@ -562,8 +575,10 @@
     )
     a = kernel(choose_kernel, blocks(half)[0], x1, y1)
     a1 = moved(a, partner)
-    extra = kernel(functools.partial(guest_kernel, factor, 2, 0), slab(half), x1, *own)
+    x1_1 = moved(x1, only((3,), partner))
+    extra = kernel(functools.partial(guest_kernel, factor, 2, part, part), slab(half - part), x1, *own)
     extra = moved(extra, only((2,), sideways))
+    third = kernel(functools.partial(fetched_kernel, factor, 3, 0), kept(part), q, x1, x1_1)
 
     def visit(chunk, x, got, got1):
         return kernel(
@@ -582,8 +597,8 @@
     b = kernel(choose_second_kernel, blocks(half)[0], x2, x3, y2)
     b1 = moved(b, partner)
     away = visit(1, x3, b, b1)
-    upper2, across2 = moved(away, other_span), moved(away, only((2, 3), sideways))
-    helped = kernel(functools.partial(guest_kernel, factor, 0, half), slab(lent), x4, *own)
+    upper2, across2 = moved(away, up), moved(away, only((2, 3), sideways))
+    helped = kernel(functools.partial(guest_kernel, factor, 0, half, 0), slab(lent), x4, *own)
     helped = moved(helped, only((0,), sideways))
     x4_1 = moved(x4, only((1,), partner))
     mine = kernel(functools.partial(stay_kernel, factor), kept(half), q, a, a1, b, b1, *own)
@@ -593,7 +608,7 @@
         out_space=pl.ANY,
         scratch=[pltpu.VMEM((rows, half, width), jnp.bfloat16), pltpu.SemaphoreType.DMA(())],
     )
-    out = kernel(merge_first_kernel, outcome, gates, *other, *mine, upper, upper2, extra, **more)
+    out = kernel(merge_first_kernel, outcome, gates, *other, *mine, upper, upper2, extra, *third, **more)
     return kernel(
         merge_second_kernel, outcome, gates, *other, *mine, across, across2, helped, *fetched, into=out, **more
     )

time: 65 us -> 59.4 us (0.914)
  the two profiles are of different devices: /device:TPU:22 before, /device:TPU:30 now
where the time goes in v4:
time: 59.4 us; the launch traced here: 59.1 us
  waiting for transfers between devices  23.2 us (39%)
  starting transfers between devices  22.8 us (38%)
  Pallas kernels  10.3 us (17%)
  local copies, waits for them, and re-layouts  2.48 us (4%)
    ppermute x18, waiting for transfers between devices, moved(): return lax.ppermute(block, ('span', 'head'), route)  23.2 us
    ppermute x18, starting transfers between devices, moved(): return lax.ppermute(block, ('span', 'head'), route)  22.8 us
    pallas_call x14, Pallas kernels, run(): pl.pallas_call(kernel, out_shape=out_shape, in_specs=inputs, out_specs=ja...  10.3 us
    unnamed x14, local copies, waits for them, and re-layouts  1.87 us
  transfers between devices with their start and end apart: 18, of which 7 were waited for; matrix products, arithmetic and copies ran while one was open for 0% of the time, Pallas kernels for 11%

profile of v4, /device:TPU:30, one launch (start us, length us, event | category | flops | bytes accessed | tf_op | source)
XLA Modules:
  0.0 59.1 jit_solution(16096416577360644378)
XLA Ops:
  0.0 2.3 %shard_map.55 = (bf16[24,64,128]{2,1,0:T(8,128)(2,1)}, bf16[24,64,128]{2,1,0:T(8,128)(2,1)}) custom-call(bf16[64,48,128]{2,1,0:T(8,128)(2,1)} %queries.1, bf16[64,48,128]{2,1,0:T(8,128)(2,1)} %key_rows.1, bf16[64,48,128]{2,1,0:T(8,128)(2,1)} %value_rows.1), custom_call_target="tpu_custom_call" | custom-call | flops 2000000000 | bytes 1048576 | tf_op jit(solution)/shard_map/pallas_call | solution.py:492
  2.5 0.9 %copy-done.3 = bf16[64,48,128]{2,1,0:T(8,128)(2,1)S(1)} copy-done((bf16[64,48,128]{2,1,0:T(8,128)(2,1)S(1)}, bf16[64,48,128]{2,1,0:T(8,128)(2,1)}, u32[]{:S(2)}) %copy-start.3) | copy-done | bytes 786456
  3.7 0.9 %copy-done.4 = bf16[64,48,128]{2,1,0:T(8,128)(2,1)S(1)} copy-done((bf16[64,48,128]{2,1,0:T(8,128)(2,1)S(1)}, bf16[64,48,128]{2,1,0:T(8,128)(2,1)}, u32[]{:S(2)}) %copy-start.4) | copy-done | bytes 786456
  5.5 1.5 %collective-permute-start.6 = (bf16[12,64,128]{2,1,0:T(8,128)(2,1)S(1)}, bf16[12,64,128]{2,1,0:T(8,128)(2,1)S(1)}, u32[]{:S(2)}, u32[]{:S(2)}) collective-permute-start(bf16[12,64,128]{2,1,0:T(8,128)(2,1)S(1)} %get-tuple-element.36), channel_id=1, source_target_pairs={{0,2},{1,3},{2,0},{3,1},{4,6},{5,7},{6,4},{7,5},{8,10},{9,11},{10,... | collective-permute-start | bytes 589832 | tf_op jit(solution)/shard_map/ppermute | solution.py:516
  7.5 1.5 %collective-permute-start.3 = (bf16[24,64,128]{2,1,0:T(8,128)(2,1)S(1)}, bf16[24,64,128]{2,1,0:T(8,128)(2,1)S(1)}, u32[]{:S(2)}, u32[]{:S(2)}) collective-permute-start(bf16[24,64,128]{2,1,0:T(8,128)(2,1)S(1)} %copy-done.6), channel_id=1, source_target_pairs={{0,4},{1,5},{2,6},{3,7},{4,0},{5,1},{6,2},{7,3},{8,12},{9,13},{10,... | collective-permute-start | bytes 1179656 | tf_op jit(solution)/shard_map/ppermute | solution.py:516
  9.0 3.7 %collective-permute-done.5.x2.x = bf16[12,64,128]{2,1,0:T(8,128)(2,1)S(1)} collective-permute-done((bf16[12,64,128]{2,1,0:T(8,128)(2,1)S(1)}, bf16[12,64,128]{2,1,0:T(8,128)(2,1)S(1)}, u32[]{:S(2)}, u32[]{:S(2)}) %collective-permute-start.5) | collective-permute-done | bytes 196640 | tf_op jit(solution)/shard_map/ppermute | solution.py:516
  12.8 3.1 %collective-permute-done.6.x3.x = bf16[12,64,128]{2,1,0:T(8,128)(2,1)S(1)} collective-permute-done((bf16[12,64,128]{2,1,0:T(8,128)(2,1)S(1)}, bf16[12,64,128]{2,1,0:T(8,128)(2,1)S(1)}, u32[]{:S(2)}, u32[]{:S(2)}) %collective-permute-start.6) | collective-permute-done | bytes 196640 | tf_op jit(solution)/shard_map/ppermute | solution.py:516
  16.4 2.6 %collective-permute-done.7.y2 = bf16[24,64,128]{2,1,0:T(8,128)(2,1)S(1)} collective-permute-done((bf16[24,64,128]{2,1,0:T(8,128)(2,1)S(1)}, bf16[24,64,128]{2,1,0:T(8,128)(2,1)S(1)}, u32[]{:S(2)}, u32[]{:S(2)}) %collective-permute-start.7) | collective-permute-done | bytes 393248 | tf_op jit(solution)/shard_map/ppermute | solution.py:516
  19.7 6.0 %collective-permute-done.3.y.y1 = bf16[24,64,128]{2,1,0:T(8,128)(2,1)S(1)} collective-permute-done((bf16[24,64,128]{2,1,0:T(8,128)(2,1)S(1)}, bf16[24,64,128]{2,1,0:T(8,128)(2,1)S(1)}, u32[]{:S(2)}, u32[]{:S(2)}) %collective-permute-start.3) | collective-permute-done | bytes 393248 | tf_op jit(solution)/shard_map/ppermute | solution.py:516
  26.3 2.0 %collective-permute-start.17 = (bf16[24,64,128]{2,1,0:T(8,128)(2,1)S(1)}, bf16[24,64,128]{2,1,0:T(8,128)(2,1)S(1)}, u32[]{:S(2)}, u32[]{:S(2)}) collective-permute-start(bf16[24,64,128]{2,1,0:T(8,128)(2,1)S(1)} %collective-permute-done.2.x.q.got), channel_id=1, source_target_pairs={{6,7},{7,6},{14,15},{15,14},{22,23},{23,22},{30,31},{31,30}} | collective-permute-start | bytes 1179656 | tf_op jit(solution)/shard_map/ppermute | solution.py:516
  28.4 0.7 %collective-permute-start.13 = (bf16[24,64,128]{2,1,0:T(8,128)(2,1)S(1)}, bf16[24,64,128]{2,1,0:T(8,128)(2,1)S(1)}, u32[]{:S(2)}, u32[]{:S(2)}) collective-permute-start(bf16[24,64,128]{2,1,0:T(8,128)(2,1)S(1)} %collective-permute-done.11.q.got), channel_id=1, source_target_pairs={{2,3},{3,2},{10,11},{11,10},{18,19},{19,18},{26,27},{27,26}} | collective-permute-start | bytes 1179656 | tf_op jit(solution)/shard_map/ppermute | solution.py:516
  29.1 0.7 %shard_map.62 = bf16[13,64,128]{2,1,0:T(8,128)(2,1)S(1)} custom-call(bf16[24,64,128]{2,1,0:T(8,128)(2,1)S(1)} %collective-permute-done.3.y.y1, bf16[12,64,128]{2,1,0:T(8,128)(2,1)S(1)} %collective-permute-done.6.x3.x, bf16[24,64,128]{2,1,0:T(8,128)(2,1)S(1)} %shard_map.59.b.got, bf16[24,64,128]{2,1,0:T(8,128)(2,1)S(1)} %collective-permute-done.8.b1.got1, ...), custom_call_target="tpu_custom_call" | custom-call | flops 2000000000 | bytes 1048576 | tf_op jit(solution)/shard_map/pallas_call | solution.py:492
  29.8 1.3 %collective-permute-start.15 = (bf16[13,64,128]{2,1,0:T(8,128)(2,1)S(1)}, bf16[13,64,128]{2,1,0:T(8,128)(2,1)S(1)}, u32[]{:S(2)}, u32[]{:S(2)}) collective-permute-start(bf16[13,64,128]{2,1,0:T(8,128)(2,1)S(1)} %shard_map.62), channel_id=1, source_target_pairs={{0,4},{1,5},{2,6},{3,7},{8,12},{9,13},{10,14},{11,15},{16,20},{17,... | collective-permute-start | bytes 638984 | tf_op jit(solution)/shard_map/ppermute | solution.py:516
  31.1 1.9 %collective-permute-start.10 = (bf16[13,64,128]{2,1,0:T(8,128)(2,1)S(1)}, bf16[13,64,128]{2,1,0:T(8,128)(2,1)S(1)}, u32[]{:S(2)}, u32[]{:S(2)}) collective-permute-start(bf16[13,64,128]{2,1,0:T(8,128)(2,1)S(1)} %shard_map.62), channel_id=1, source_target_pairs={{4,6},{5,7},{6,4},{7,5},{12,14},{13,15},{14,12},{15,13},{20,22},{2... | collective-permute-start | bytes 638984 | tf_op jit(solution)/shard_map/ppermute | solution.py:516
  33.0 0.7 %shard_map.61 = bf16[13,64,128]{2,1,0:T(8,128)(2,1)S(1)} custom-call(bf16[24,64,128]{2,1,0:T(8,128)(2,1)S(1)} %collective-permute-done.3.y.y1, bf16[12,64,128]{2,1,0:T(8,128)(2,1)S(1)} %collective-permute-done.5.x2.x, bf16[24,64,128]{2,1,0:T(8,128)(2,1)S(1)} %shard_map.57.a.got, bf16[24,64,128]{2,1,0:T(8,128)(2,1)S(1)} %collective-permute-done.4.a1.got1, ...), custom_call_target="tpu_custom_call" | custom-call | flops 2000000000 | bytes 1048576 | tf_op jit(solution)/shard_map/pallas_call | solution.py:492
  33.7 7.2 %collective-permute-start.14 = (bf16[13,64,128]{2,1,0:T(8,128)(2,1)S(1)}, bf16[13,64,128]{2,1,0:T(8,128)(2,1)S(1)}, u32[]{:S(2)}, u32[]{:S(2)}) collective-permute-start(bf16[13,64,128]{2,1,0:T(8,128)(2,1)S(1)} %shard_map.61), channel_id=1, source_target_pairs={{0,4},{1,5},{2,6},{3,7},{4,0},{5,1},{6,2},{7,3},{8,12},{9,13},{10,... | collective-permute-start | bytes 638984 | tf_op jit(solution)/shard_map/ppermute | solution.py:516
  40.9 1.0 %shard_map.60 = (f32[24,64,128]{2,1,0:T(8,128)S(1)}, f32[64,128]{1,0:T(8,128)S(1)}) custom-call(bf16[48,64,128]{2,1,0:T(8,128)(2,1)S(1)} %bitcast.26, bf16[24,64,128]{2,1,0:T(8,128)(2,1)S(1)} %shard_map.57.a.got, bf16[24,64,128]{2,1,0:T(8,128)(2,1)S(1)} %collective-permute-done.4.a1.got1, bf16[24,64,128]{2,1,0:T(8,128)(2,1)S(1)} %shard_map.59.b.got, ...), custom_call_target="tpu_custom_call" | custom-call | flops 2000000000 | bytes 1048576 | tf_op jit(solution)/shard_map/pallas_call | solution.py:492
  42.0 1.9 %collective-permute-start.9 = (bf16[13,64,128]{2,1,0:T(8,128)(2,1)S(1)}, bf16[13,64,128]{2,1,0:T(8,128)(2,1)S(1)}, u32[]{:S(2)}, u32[]{:S(2)}) collective-permute-start(bf16[13,64,128]{2,1,0:T(8,128)(2,1)S(1)} %shard_map.61), channel_id=1, source_target_pairs={{4,6},{5,7},{6,4},{7,5},{12,14},{13,15},{14,12},{15,13},{20,22},{2... | collective-permute-start | bytes 638984 | tf_op jit(solution)/shard_map/ppermute | solution.py:516
  44.6 1.3 %collective-permute-start.16 = (bf16[13,64,128]{2,1,0:T(8,128)(2,1)S(1)}, bf16[13,64,128]{2,1,0:T(8,128)(2,1)S(1)}, u32[]{:S(2)}, u32[]{:S(2)}) collective-permute-start(bf16[13,64,128]{2,1,0:T(8,128)(2,1)S(1)} %shard_map.65), channel_id=1, source_target_pairs={{4,6},{5,7},{12,14},{13,15},{20,22},{21,23},{28,30},{29,31}} | collective-permute-start | bytes 638984 | tf_op jit(solution)/shard_map/ppermute | solution.py:516
  46.6 1.5 %shard_map.56 = (f32[24,64,128]{2,1,0:T(8,128)S(1)}, f32[64,128]{1,0:T(8,128)S(1)}, f32[2,128]{1,0:T(2,128)S(1)}) custom-call(s32[2]{0:T(128)S(1)} %copy-done.1, f32[8,48]{1,0:T(8,128)S(1)} %copy-done, bf16[48,64,128]{2,1,0:T(8,128)(2,1)S(1)} %bitcast.29, bf16[48,64,128]{2,1,0:T(8,128)(2,1)S(1)} %bitcast.24, ...), custom_call_target="tpu_custom_call" | custom-call | flops 2000000000 | bytes 1048576 | tf_op jit(solution)/shard_map/pallas_call | solution.py:492
  48.1 1.8 %collective-permute-done.14.upper = bf16[13,64,128]{2,1,0:T(8,128)(2,1)S(1)} collective-permute-done((bf16[13,64,128]{2,1,0:T(8,128)(2,1)S(1)}, bf16[13,64,128]{2,1,0:T(8,128)(2,1)S(1)}, u32[]{:S(2)}, u32[]{:S(2)}) %collective-permute-start.14) | collective-permute-done | bytes 213024 | tf_op jit(solution)/shard_map/ppermute | solution.py:516
  49.9 5.9 %collective-permute-done.16.extra = bf16[13,64,128]{2,1,0:T(8,128)(2,1)S(1)} collective-permute-done((bf16[13,64,128]{2,1,0:T(8,128)(2,1)S(1)}, bf16[13,64,128]{2,1,0:T(8,128)(2,1)S(1)}, u32[]{:S(2)}, u32[]{:S(2)}) %collective-permute-start.16) | collective-permute-done | bytes 213024 | tf_op jit(solution)/shard_map/ppermute | solution.py:516
  55.8 1.7 %shard_map.67._ = bf16[64,48,128]{2,1,0:T(8,128)(2,1)} custom-call(f32[2,128]{1,0:T(2,128)S(1)} %get-tuple-element.30.gates, f32[24,64,128]{2,1,0:T(8,128)S(1)} %get-tuple-element.31.other, f32[64,128]{1,0:T(8,128)S(1)} %get-tuple-element.32.other_table, f32[24,64,128]{2,1,0:T(8,128)S(1)} %get-tuple-element.38.mine, ...), custom_call_target="tpu_custom_call" | custom-call | flops 2000000000 | bytes 1048576 | tf_op jit(solution)/shard_map/pallas_call | solution.py:492
  57.6 1.5 %shard_map.68 = bf16[64,48,128]{2,1,0:T(8,128)(2,1)} custom-call(f32[2,128]{1,0:T(2,128)S(1)} %get-tuple-element.30.gates, f32[24,64,128]{2,1,0:T(8,128)S(1)} %get-tuple-element.31.other, f32[64,128]{1,0:T(8,128)S(1)} %get-tuple-element.32.other_table, f32[24,64,128]{2,1,0:T(8,128)S(1)} %get-tuple-element.38.mine, ...), custom_call_target="tpu_custom_call", output_to_operand_aliasing={{}: (10, {})} | custom-call | flops 2000000000 | bytes 1048576 | tf_op jit(solution)/shard_map/pallas_call | solution.py:492
  (43 shorter events, 5.1 us)
Async XLA Ops:
  0.0 2.3 %copy-start.2 = (bf16[64,48,128]{2,1,0:T(8,128)(2,1)S(1)}, bf16[64,48,128]{2,1,0:T(8,128)(2,1)}, u32[]{:S(2)}) copy-start(bf16[64,48,128]{2,1,0:T(8,128)(2,1)} %value_rows.1) | copy-start | bytes 2359300
  2.3 1.1 %copy-start.3 = (bf16[64,48,128]{2,1,0:T(8,128)(2,1)S(1)}, bf16[64,48,128]{2,1,0:T(8,128)(2,1)}, u32[]{:S(2)}) copy-start(bf16[64,48,128]{2,1,0:T(8,128)(2,1)} %key_rows.1) | copy-start | bytes 2359300
  4.8 2.7 %copy-start.6 = (bf16[24,64,128]{2,1,0:T(8,128)(2,1)S(1)}, bf16[24,64,128]{2,1,0:T(8,128)(2,1)}, u32[]{:S(2)}) copy-start(bf16[24,64,128]{2,1,0:T(8,128)(2,1)} %get-tuple-element.34) | copy-start | bytes 1179652
  4.8 11.0 %copy-start.5 = (bf16[24,64,128]{2,1,0:T(8,128)(2,1)S(1)}, bf16[24,64,128]{2,1,0:T(8,128)(2,1)}, u32[]{:S(2)}) copy-start(bf16[24,64,128]{2,1,0:T(8,128)(2,1)} %get-tuple-element.33) | copy-start | bytes 1179652
  4.9 7.8 %collective-permute-start.5 = (bf16[12,64,128]{2,1,0:T(8,128)(2,1)S(1)}, bf16[12,64,128]{2,1,0:T(8,128)(2,1)S(1)}, u32[]{:S(2)}, u32[]{:S(2)}) collective-permute-start(bf16[12,64,128]{2,1,0:T(8,128)(2,1)S(1)} %get-tuple-element.35), channel_id=1, source_target_pairs={{0,2},{1,3},{2,0},{3,1},{4,6},{5,7},{6,4},{7,5},{8,10},{9,11},{10,... | collective-permute-start | bytes 589832 | tf_op jit(solution)/shard_map/ppermute | solution.py:516
  5.5 10.3 %collective-permute-start.6 = (bf16[12,64,128]{2,1,0:T(8,128)(2,1)S(1)}, bf16[12,64,128]{2,1,0:T(8,128)(2,1)S(1)}, u32[]{:S(2)}, u32[]{:S(2)}) collective-permute-start(bf16[12,64,128]{2,1,0:T(8,128)(2,1)S(1)} %get-tuple-element.36), channel_id=1, source_target_pairs={{0,2},{1,3},{2,0},{3,1},{4,6},{5,7},{6,4},{7,5},{8,10},{9,11},{10,... | collective-permute-start | bytes 589832 | tf_op jit(solution)/shard_map/ppermute | solution.py:516
  7.0 12.0 %collective-permute-start.7 = (bf16[24,64,128]{2,1,0:T(8,128)(2,1)S(1)}, bf16[24,64,128]{2,1,0:T(8,128)(2,1)S(1)}, u32[]{:S(2)}, u32[]{:S(2)}) collective-permute-start(bf16[24,64,128]{2,1,0:T(8,128)(2,1)S(1)} %get-tuple-element.37), channel_id=1, source_target_pairs={{0,4},{1,5},{2,6},{3,7},{4,0},{5,1},{6,2},{7,3},{8,12},{9,13},{10,... | collective-permute-start | bytes 1179656 | tf_op jit(solution)/shard_map/ppermute | solution.py:516
  7.5 18.2 %collective-permute-start.3 = (bf16[24,64,128]{2,1,0:T(8,128)(2,1)S(1)}, bf16[24,64,128]{2,1,0:T(8,128)(2,1)S(1)}, u32[]{:S(2)}, u32[]{:S(2)}) collective-permute-start(bf16[24,64,128]{2,1,0:T(8,128)(2,1)S(1)} %copy-done.6), channel_id=1, source_target_pairs={{0,4},{1,5},{2,6},{3,7},{4,0},{5,1},{6,2},{7,3},{8,12},{9,13},{10,... | collective-permute-start | bytes 1179656 | tf_op jit(solution)/shard_map/ppermute | solution.py:516
  9.0 20.0 %collective-permute-start = (bf16[48,64,128]{2,1,0:T(8,128)(2,1)S(1)}, bf16[48,64,128]{2,1,0:T(8,128)(2,1)S(1)}, u32[]{:S(2)}, u32[]{:S(2)}) collective-permute-start(bf16[48,64,128]{2,1,0:T(8,128)(2,1)S(1)} %bitcast.18), channel_id=1, source_target_pairs={{0,1},{1,0},{2,3},{3,2},{4,5},{5,4},{6,7},{7,6},{8,9},{9,8},{10,11... | collective-permute-start | bytes 2359304 | tf_op jit(solution)/shard_map/ppermute | solution.py:516
  12.8 16.3 %collective-permute-start.1 = (bf16[48,64,128]{2,1,0:T(8,128)(2,1)S(1)}, bf16[48,64,128]{2,1,0:T(8,128)(2,1)S(1)}, u32[]{:S(2)}, u32[]{:S(2)}) collective-permute-start(bf16[48,64,128]{2,1,0:T(8,128)(2,1)S(1)} %bitcast.10), channel_id=1, source_target_pairs={{0,1},{1,0},{2,3},{3,2},{4,5},{5,4},{6,7},{7,6},{8,9},{9,8},{10,11... | collective-permute-start | bytes 2359304 | tf_op jit(solution)/shard_map/ppermute | solution.py:516
  15.8 10.0 %collective-permute-start.2 = (bf16[24,64,128]{2,1,0:T(8,128)(2,1)S(1)}, bf16[24,64,128]{2,1,0:T(8,128)(2,1)S(1)}, u32[]{:S(2)}, u32[]{:S(2)}) collective-permute-start(bf16[24,64,128]{2,1,0:T(8,128)(2,1)S(1)} %copy-done.5), channel_id=1, source_target_pairs={{0,2},{1,3},{2,0},{3,1},{4,6},{5,7},{6,4},{7,5},{8,10},{9,11},{10,... | collective-permute-start | bytes 1179656 | tf_op jit(solution)/shard_map/ppermute | solution.py:516
  19.0 7.3 %collective-permute-start.11 = (bf16[24,64,128]{2,1,0:T(8,128)(2,1)S(1)}, bf16[24,64,128]{2,1,0:T(8,128)(2,1)S(1)}, u32[]{:S(2)}, u32[]{:S(2)}) collective-permute-start(bf16[24,64,128]{2,1,0:T(8,128)(2,1)S(1)} %get-tuple-element.40), channel_id=1, source_target_pairs={{0,2},{1,3},{2,0},{3,1},{8,10},{9,11},{10,8},{11,9},{16,18},{17,19... | collective-permute-start | bytes 1179656 | tf_op jit(solution)/shard_map/ppermute | solution.py:516
  25.7 2.6 %collective-permute-start.8 = (bf16[24,64,128]{2,1,0:T(8,128)(2,1)S(1)}, bf16[24,64,128]{2,1,0:T(8,128)(2,1)S(1)}, u32[]{:S(2)}, u32[]{:S(2)}) collective-permute-start(bf16[24,64,128]{2,1,0:T(8,128)(2,1)S(1)} %shard_map.59.b.got), channel_id=1, source_target_pairs={{0,1},{1,0},{2,3},{3,2},{4,5},{5,4},{6,7},{7,6},{8,9},{9,8},{10,11... | collective-permute-start | bytes 1179656 | tf_op jit(solution)/shard_map/ppermute | solution.py:516
  25.9 7.2 %collective-permute-start.4 = (bf16[24,64,128]{2,1,0:T(8,128)(2,1)S(1)}, bf16[24,64,128]{2,1,0:T(8,128)(2,1)S(1)}, u32[]{:S(2)}, u32[]{:S(2)}) collective-permute-start(bf16[24,64,128]{2,1,0:T(8,128)(2,1)S(1)} %shard_map.57.a.got), channel_id=1, source_target_pairs={{0,1},{1,0},{2,3},{3,2},{4,5},{5,4},{6,7},{7,6},{8,9},{9,8},{10,11... | collective-permute-start | bytes 1179656 | tf_op jit(solution)/shard_map/ppermute | solution.py:516
  26.3 15.6 %collective-permute-start.17 = (bf16[24,64,128]{2,1,0:T(8,128)(2,1)S(1)}, bf16[24,64,128]{2,1,0:T(8,128)(2,1)S(1)}, u32[]{:S(2)}, u32[]{:S(2)}) collective-permute-start(bf16[24,64,128]{2,1,0:T(8,128)(2,1)S(1)} %collective-permute-done.2.x.q.got), channel_id=1, source_target_pairs={{6,7},{7,6},{14,15},{15,14},{22,23},{23,22},{30,31},{31,30}} | collective-permute-start | bytes 1179656 | tf_op jit(solution)/shard_map/ppermute | solution.py:516
  28.4 16.2 %collective-permute-start.13 = (bf16[24,64,128]{2,1,0:T(8,128)(2,1)S(1)}, bf16[24,64,128]{2,1,0:T(8,128)(2,1)S(1)}, u32[]{:S(2)}, u32[]{:S(2)}) collective-permute-start(bf16[24,64,128]{2,1,0:T(8,128)(2,1)S(1)} %collective-permute-done.11.q.got), channel_id=1, source_target_pairs={{2,3},{3,2},{10,11},{11,10},{18,19},{19,18},{26,27},{27,26}} | collective-permute-start | bytes 1179656 | tf_op jit(solution)/shard_map/ppermute | solution.py:516
  29.8 16.1 %collective-permute-start.15 = (bf16[13,64,128]{2,1,0:T(8,128)(2,1)S(1)}, bf16[13,64,128]{2,1,0:T(8,128)(2,1)S(1)}, u32[]{:S(2)}, u32[]{:S(2)}) collective-permute-start(bf16[13,64,128]{2,1,0:T(8,128)(2,1)S(1)} %shard_map.62), channel_id=1, source_target_pairs={{0,4},{1,5},{2,6},{3,7},{8,12},{9,13},{10,14},{11,15},{16,20},{17,... | collective-permute-start | bytes 638984 | tf_op jit(solution)/shard_map/ppermute | solution.py:516
  31.1 26.5 %collective-permute-start.10 = (bf16[13,64,128]{2,1,0:T(8,128)(2,1)S(1)}, bf16[13,64,128]{2,1,0:T(8,128)(2,1)S(1)}, u32[]{:S(2)}, u32[]{:S(2)}) collective-permute-start(bf16[13,64,128]{2,1,0:T(8,128)(2,1)S(1)} %shard_map.62), channel_id=1, source_target_pairs={{4,6},{5,7},{6,4},{7,5},{12,14},{13,15},{14,12},{15,13},{20,22},{2... | collective-permute-start | bytes 638984 | tf_op jit(solution)/shard_map/ppermute | solution.py:516
  33.7 16.2 %collective-permute-start.14 = (bf16[13,64,128]{2,1,0:T(8,128)(2,1)S(1)}, bf16[13,64,128]{2,1,0:T(8,128)(2,1)S(1)}, u32[]{:S(2)}, u32[]{:S(2)}) collective-permute-start(bf16[13,64,128]{2,1,0:T(8,128)(2,1)S(1)} %shard_map.61), channel_id=1, source_target_pairs={{0,4},{1,5},{2,6},{3,7},{4,0},{5,1},{6,2},{7,3},{8,12},{9,13},{10,... | collective-permute-start | bytes 638984 | tf_op jit(solution)/shard_map/ppermute | solution.py:516
  42.0 15.6 %collective-permute-start.9 = (bf16[13,64,128]{2,1,0:T(8,128)(2,1)S(1)}, bf16[13,64,128]{2,1,0:T(8,128)(2,1)S(1)}, u32[]{:S(2)}, u32[]{:S(2)}) collective-permute-start(bf16[13,64,128]{2,1,0:T(8,128)(2,1)S(1)} %shard_map.61), channel_id=1, source_target_pairs={{4,6},{5,7},{6,4},{7,5},{12,14},{13,15},{14,12},{15,13},{20,22},{2... | collective-permute-start | bytes 638984 | tf_op jit(solution)/shard_map/ppermute | solution.py:516
  44.5 2.1 %copy-start = (f32[8,48]{1,0:T(8,128)S(1)}, f32[8,48]{1,0:T(8,128)}, u32[]{:S(2)}) copy-start(f32[8,48]{1,0:T(8,128)} %gate_table.1) | copy-start | bytes 4612
  44.6 2.1 %copy-start.1 = (s32[2]{0:T(128)S(1)}, s32[2]{0:T(128)}, u32[]{:S(2)}) copy-start(s32[2]{0:T(128)} %levels.1) | copy-start | bytes 28
  44.6 11.2 %collective-permute-start.16 = (bf16[13,64,128]{2,1,0:T(8,128)(2,1)S(1)}, bf16[13,64,128]{2,1,0:T(8,128)(2,1)S(1)}, u32[]{:S(2)}, u32[]{:S(2)}) collective-permute-start(bf16[13,64,128]{2,1,0:T(8,128)(2,1)S(1)} %shard_map.65), channel_id=1, source_target_pairs={{4,6},{5,7},{12,14},{13,15},{20,22},{21,23},{28,30},{29,31}} | collective-permute-start | bytes 638984 | tf_op jit(solution)/shard_map/ppermute | solution.py:516
  45.9 11.6 %collective-permute-start.12 = (bf16[13,64,128]{2,1,0:T(8,128)(2,1)S(1)}, bf16[13,64,128]{2,1,0:T(8,128)(2,1)S(1)}, u32[]{:S(2)}, u32[]{:S(2)}) collective-permute-start(bf16[13,64,128]{2,1,0:T(8,128)(2,1)S(1)} %shard_map.63), channel_id=1, source_target_pairs={{0,2},{1,3},{8,10},{9,11},{16,18},{17,19},{24,26},{25,27}} | collective-permute-start | bytes 638984 | tf_op jit(solution)/shard_map/ppermute | solution.py:516
  (1 other events, 1.1 us)

commit v5 on v4

--- a/solution.py
+++ b/solution.py
@@ -10,7 +10,7 @@
 
 BLOCK = 128
 LEVELS = 8
-ROOM = 62 << 20
+ROOM = 211 << 18
 TILE = 8
 LANES = 32
 
@@ -381,24 +381,27 @@
         store_local(out, table, *attend(jobs, factor), lanes_of(rows, width))
 
 
-def merged(gate_row, logs, parts_of, half, held, group, out, sem):
+def merged(gate_row, logs, parts_of, tiles, first_head, slot, held, out, sems):
     top = functools.reduce(jnp.maximum, logs)
     scaled = [jnp.exp2(table - top) for table in logs]
     ratio = gate_row / sum(scaled)
     scaled = [s * ratio for s in scaled]
-    for start in range(0, half, TILE):
+    copies = []
+    for i, start in enumerate(tile * TILE for tile in tiles):
         sums = [
             sum(part.astype(jnp.float32) * s[:, h : h + 1] for part, s in zip(parts_of(h), scaled))
             for h in range(start, start + TILE)
         ]
-        together = jnp.swapaxes(jnp.stack(sums), 0, 1)
-        held[:, start : start + TILE, :] = together.astype(held.dtype)
-    leave(held, out, group, sem).start()
-
-
-def leave(held, out, group, sem):
-    half = held.shape[1]
-    return pltpu.make_async_copy(held, out.at[:, pl.ds(group * half, half), :], sem)
+        held[slot + i] = jnp.swapaxes(jnp.stack(sums), 0, 1).astype(held.dtype)
+        place = out.at[:, pl.ds(first_head + start, TILE), :]
+        copies.append(pltpu.make_async_copy(held.at[slot + i], place, sems.at[slot + i]))
+        copies[-1].start()
+    return copies
+
+
+def finish(copies):
+    for copy in copies:
+        copy.wait()
 
 
 def logs_of(slab):
@@ -415,69 +418,92 @@
 
 
 def merge_first_kernel(
-    gates, other, other_table, mine, mine_table, upper, upper2, extra, third, third_table, out, held, sem
+    gates, other, other_table, mine, mine_table, upper, upper2, extra, third, third_table, across, fetched,
+    fetched_table, out, held, sems,
+):
+    _, block = where_am_i()
+    half = mine.shape[0]
+    part = upper.shape[0] - 1
+    lent_heads = half - fetched.shape[0]
+    every = range(half // TILE)
+    sink = (held, out, sems)
+
+    def visited(more_logs, more_parts):
+        logs = [other_table[...], side_by_side(logs_of(upper), logs_of(upper2), part), *more_logs]
+        copies = merged(
+            gates[0:1],
+            logs,
+            lambda h: [other[h], picked(upper, upper2, h, part), *more_parts(h)],
+            every, 0, 0, *sink,
+        )
+        logs = [mine_table[...], logs_of(across)]
+        early = merged(
+            gates[1:2], logs, lambda h: [mine[h], across[h]], every[: part // TILE], half, len(every), *sink
+        )
+        finish(copies + early)
+
+    @pl.when(block == 2)
+    def _():
+        visited([], lambda h: [])
+
+    @pl.when(block == 3)
+    def _():
+        visited(
+            [side_by_side(third_table[...], logs_of(extra), part)], lambda h: [picked(third, extra, h, part)]
+        )
+
+    @pl.when(block == 0)
+    def _():
+        copies = merged(gates[0:1], [mine_table[...]], lambda h: [mine[h]], every, 0, 0, *sink)
+        early = merged(gates[1:2], [other_table[...]], lambda h: [other[h]], every, half, len(every), *sink)
+        finish(copies + early)
+
+    @pl.when(block == 1)
+    def _():
+        copies = merged(gates[0:1], [mine_table[...]], lambda h: [mine[h]], every, 0, 0, *sink)
+        logs = [other_table[...], pltpu.roll(fetched_table[...], lent_heads, 1)]
+        early = merged(
+            gates[1:2],
+            logs,
+            lambda h: [other[h], fetched[h - lent_heads]],
+            every[-(-lent_heads // TILE) :], half, len(every), *sink,
+        )
+        finish(copies + early)
+
+
+def merge_second_kernel(
+    gates, other, other_table, mine, mine_table, across, across2, lent, fetched, fetched_table, _, out, held, sems
 ):
     span, block = where_am_i()
     half = mine.shape[0]
-    part = half // 2
-    gate_row = gates[0:1]
-
-    @pl.when(block == 2)
-    def _():
-        logs = [other_table[...], side_by_side(logs_of(upper), logs_of(upper2), part)]
-        merged(
-            gate_row, logs, lambda h: [other[h], picked(upper, upper2, h, part)], half, held, 0, out, sem
-        )
-
-    @pl.when(block == 3)
-    def _():
-        logs = [
-            other_table[...],
-            side_by_side(logs_of(upper), logs_of(upper2), part),
-            side_by_side(third_table[...], logs_of(extra), part),
-        ]
-        merged(
-            gate_row,
-            logs,
-            lambda h: [other[h], picked(upper, upper2, h, part), picked(third, extra, h, part)],
-            half, held, 0, out, sem,
-        )
-
-    @pl.when(span == 0)
-    def _():
-        merged(gate_row, [mine_table[...]], lambda h: [mine[h]], half, held, 0, out, sem)
-
-    leave(held, out, 0, sem).wait()
-
-
-def merge_second_kernel(
-    gates, other, other_table, mine, mine_table, across, across2, lent, fetched, fetched_table, _, out, held, sem
-):
-    span, block = where_am_i()
-    half = mine.shape[0]
-    part = half // 2
+    part = across.shape[0] - 1
     lent_heads = half - fetched.shape[0]
-    gate_row = gates[1:2]
+    every = range(half // TILE)
+    sink = (held, out, sems)
 
     @pl.when(span == 1)
     def _():
         logs = [mine_table[...], side_by_side(logs_of(across), logs_of(across2), part)]
-        merged(
-            gate_row, logs, lambda h: [mine[h], picked(across, across2, h, part)], half, held, 1, out, sem
-        )
-
-    @pl.when(block == 0)
-    def _():
-        merged(gate_row, [other_table[...]], lambda h: [other[h]], half, held, 1, out, sem)
+        finish(
+            merged(
+                gates[1:2],
+                logs,
+                lambda h: [mine[h], picked(across, across2, h, part)],
+                every[part // TILE :], half, 0, *sink,
+            )
+        )
 
     @pl.when(block == 1)
     def _():
         logs = [other_table[...], side_by_side(logs_of(lent), fetched_table[...], lent_heads)]
-        merged(
-            gate_row, logs, lambda h: [other[h], picked(lent, fetched, h, lent_heads)], half, held, 1, out, sem
-        )
-
-    leave(held, out, 1, sem).wait()
+        finish(
+            merged(
+                gates[1:2],
+                logs,
+                lambda h: [other[h], picked(lent, fetched, h, lent_heads)],
+                every[: -(-lent_heads // TILE)], half, 0, *sink,
+            )
+        )
 
 
 def run(
@@ -606,9 +632,11 @@
     outcome = jax.ShapeDtypeStruct((rows, heads, width), jnp.bfloat16)
     more = dict(
         out_space=pl.ANY,
-        scratch=[pltpu.VMEM((rows, half, width), jnp.bfloat16), pltpu.SemaphoreType.DMA(())],
-    )
-    out = kernel(merge_first_kernel, outcome, gates, *other, *mine, upper, upper2, extra, *third, **more)
+        scratch=[pltpu.VMEM((heads // TILE, rows, TILE, width), jnp.bfloat16), pltpu.SemaphoreType.DMA((heads // TILE,))],
+    )
+    out = kernel(
+        merge_first_kernel, outcome, gates, *other, *mine, upper, upper2, extra, *third, across, *fetched, **more
+    )
     return kernel(
         merge_second_kernel, outcome, gates, *other, *mine, across, across2, helped, *fetched, into=out, **more
     )

time: 59.4 us -> 59.5 us (level)
  starting transfers between devices: 22.8 us -> 27.2 us
  waiting for transfers between devices: 23.2 us -> 20 us
    ppermute x18, starting transfers between devices: 22.8 us -> 27.2 us  [moved(): return lax.ppermute(block, ('span', 'head'), route)]
    ppermute x18, waiting for transfers between devices: 23.2 us -> 20 us  [moved(): return lax.ppermute(block, ('span', 'head'), route)]
    unnamed x14 -> x10, local copies, waits for them, and re-layouts: 1.87 us -> 1.28 us
  transfers between devices with their start and end apart: 18 -> 18, of which waited for: 7 -> 5; matrix products, arithmetic and copies ran while one was open for 0% -> 1% of each run, Pallas kernels for 11% -> 12%
where the time goes in v5:
time: 59.5 us; the launch traced here: 59.2 us
  starting transfers between devices  27.2 us (46%)
  waiting for transfers between devices  20 us (34%)
  Pallas kernels  9.74 us (16%)
  local copies, waits for them, and re-layouts  1.9 us (3%)
    ppermute x18, starting transfers between devices, moved(): return lax.ppermute(block, ('span', 'head'), route)  27.2 us
    ppermute x18, waiting for transfers between devices, moved(): return lax.ppermute(block, ('span', 'head'), route)  20 us
    pallas_call x14, Pallas kernels, run(): pl.pallas_call(kernel, out_shape=out_shape, in_specs=inputs, out_specs=ja...  9.74 us
    unnamed x10, local copies, waits for them, and re-layouts  1.28 us
  transfers between devices with their start and end apart: 18, of which 5 were waited for; matrix products, arithmetic and copies ran while one was open for 1% of the time, Pallas kernels for 12%

profile of v5, /device:TPU:30, one launch (start us, length us, event | category | flops | bytes accessed | tf_op | source)
XLA Modules:
  0.0 59.2 jit_solution(9292930802205406683)
XLA Ops:
  0.0 1.4 %shard_map.55 = (bf16[24,64,128]{2,1,0:T(8,128)(2,1)S(1)}, bf16[24,64,128]{2,1,0:T(8,128)(2,1)S(1)}) custom-call(bf16[64,48,128]{2,1,0:T(8,128)(2,1)} %queries.1, bf16[64,48,128]{2,1,0:T(8,128)(2,1)} %key_rows.1, bf16[64,48,128]{2,1,0:T(8,128)(2,1)} %value_rows.1), custom_call_target="tpu_custom_call" | custom-call | flops 2000000000 | bytes 1048576 | tf_op jit(solution)/shard_map/pallas_call | solution.py:518
  2.8 0.9 %copy-done.4 = bf16[64,48,128]{2,1,0:T(8,128)(2,1)S(1)} copy-done((bf16[64,48,128]{2,1,0:T(8,128)(2,1)S(1)}, bf16[64,48,128]{2,1,0:T(8,128)(2,1)}, u32[]{:S(2)}) %copy-start.4) | copy-done | bytes 786456
  4.6 1.5 %collective-permute-start.2 = (bf16[24,64,128]{2,1,0:T(8,128)(2,1)S(1)}, bf16[24,64,128]{2,1,0:T(8,128)(2,1)S(1)}, u32[]{:S(2)}, u32[]{:S(2)}) collective-permute-start(bf16[24,64,128]{2,1,0:T(8,128)(2,1)S(1)} %get-tuple-element.33), channel_id=1, source_target_pairs={{0,2},{1,3},{2,0},{3,1},{4,6},{5,7},{6,4},{7,5},{8,10},{9,11},{10,... | collective-permute-start | bytes 1179656 | tf_op jit(solution)/shard_map/ppermute | solution.py:542
  6.6 5.2 %collective-permute-done.5.x2.x = bf16[12,64,128]{2,1,0:T(8,128)(2,1)S(1)} collective-permute-done((bf16[12,64,128]{2,1,0:T(8,128)(2,1)S(1)}, bf16[12,64,128]{2,1,0:T(8,128)(2,1)S(1)}, u32[]{:S(2)}, u32[]{:S(2)}) %collective-permute-start.5) | collective-permute-done | bytes 196640 | tf_op jit(solution)/shard_map/ppermute | solution.py:542
  11.8 1.2 %collective-permute-start.7 = (bf16[24,64,128]{2,1,0:T(8,128)(2,1)S(1)}, bf16[24,64,128]{2,1,0:T(8,128)(2,1)S(1)}, u32[]{:S(2)}, u32[]{:S(2)}) collective-permute-start(bf16[24,64,128]{2,1,0:T(8,128)(2,1)S(1)} %get-tuple-element.37), channel_id=1, source_target_pairs={{0,4},{1,5},{2,6},{3,7},{4,0},{5,1},{6,2},{7,3},{8,12},{9,13},{10,... | collective-permute-start | bytes 1179656 | tf_op jit(solution)/shard_map/ppermute | solution.py:542
  13.6 6.7 %collective-permute-done.2.x.q.got = bf16[24,64,128]{2,1,0:T(8,128)(2,1)S(1)} collective-permute-done((bf16[24,64,128]{2,1,0:T(8,128)(2,1)S(1)}, bf16[24,64,128]{2,1,0:T(8,128)(2,1)S(1)}, u32[]{:S(2)}, u32[]{:S(2)}) %collective-permute-start.2) | collective-permute-done | bytes 393248 | tf_op jit(solution)/shard_map/ppermute | solution.py:542
  20.3 0.7 %collective-permute-start.11 = (bf16[24,64,128]{2,1,0:T(8,128)(2,1)S(1)}, bf16[24,64,128]{2,1,0:T(8,128)(2,1)S(1)}, u32[]{:S(2)}, u32[]{:S(2)}) collective-permute-start(bf16[24,64,128]{2,1,0:T(8,128)(2,1)S(1)} %get-tuple-element.40), channel_id=1, source_target_pairs={{0,2},{1,3},{2,0},{3,1},{8,10},{9,11},{10,8},{11,9},{16,18},{17,19... | collective-permute-start | bytes 1179656 | tf_op jit(solution)/shard_map/ppermute | solution.py:542
  21.0 2.4 %collective-permute-done.6.x3.x = bf16[12,64,128]{2,1,0:T(8,128)(2,1)S(1)} collective-permute-done((bf16[12,64,128]{2,1,0:T(8,128)(2,1)S(1)}, bf16[12,64,128]{2,1,0:T(8,128)(2,1)S(1)}, u32[]{:S(2)}, u32[]{:S(2)}) %collective-permute-start.6) | collective-permute-done | bytes 196640 | tf_op jit(solution)/shard_map/ppermute | solution.py:542
  24.0 1.9 %collective-permute-start.17 = (bf16[24,64,128]{2,1,0:T(8,128)(2,1)S(1)}, bf16[24,64,128]{2,1,0:T(8,128)(2,1)S(1)}, u32[]{:S(2)}, u32[]{:S(2)}) collective-permute-start(bf16[24,64,128]{2,1,0:T(8,128)(2,1)S(1)} %collective-permute-done.2.x.q.got), channel_id=1, source_target_pairs={{6,7},{7,6},{14,15},{15,14},{22,23},{23,22},{30,31},{31,30}} | collective-permute-start | bytes 1179656 | tf_op jit(solution)/shard_map/ppermute | solution.py:542
  25.9 0.7 %collective-permute-start.13 = (bf16[24,64,128]{2,1,0:T(8,128)(2,1)S(1)}, bf16[24,64,128]{2,1,0:T(8,128)(2,1)S(1)}, u32[]{:S(2)}, u32[]{:S(2)}) collective-permute-start(bf16[24,64,128]{2,1,0:T(8,128)(2,1)S(1)} %collective-permute-done.11.q.got), channel_id=1, source_target_pairs={{2,3},{3,2},{10,11},{11,10},{18,19},{19,18},{26,27},{27,26}} | collective-permute-start | bytes 1179656 | tf_op jit(solution)/shard_map/ppermute | solution.py:542
  26.6 0.7 %shard_map.61 = bf16[13,64,128]{2,1,0:T(8,128)(2,1)S(1)} custom-call(bf16[24,64,128]{2,1,0:T(8,128)(2,1)S(1)} %collective-permute-done.3.y.y1, bf16[12,64,128]{2,1,0:T(8,128)(2,1)S(1)} %collective-permute-done.5.x2.x, bf16[24,64,128]{2,1,0:T(8,128)(2,1)S(1)} %shard_map.57.a.got, bf16[24,64,128]{2,1,0:T(8,128)(2,1)S(1)} %collective-permute-done.4.a1.got1, ...), custom_call_target="tpu_custom_call" | custom-call | flops 2000000000 | bytes 1048576 | tf_op jit(solution)/shard_map/pallas_call | solution.py:518
  27.3 8.8 %collective-permute-start.14 = (bf16[13,64,128]{2,1,0:T(8,128)(2,1)S(1)}, bf16[13,64,128]{2,1,0:T(8,128)(2,1)S(1)}, u32[]{:S(2)}, u32[]{:S(2)}) collective-permute-start(bf16[13,64,128]{2,1,0:T(8,128)(2,1)S(1)} %shard_map.61), channel_id=1, source_target_pairs={{0,4},{1,5},{2,6},{3,7},{4,0},{5,1},{6,2},{7,3},{8,12},{9,13},{10,... | collective-permute-start | bytes 638984 | tf_op jit(solution)/shard_map/ppermute | solution.py:542
  36.1 1.9 %collective-permute-start.9 = (bf16[13,64,128]{2,1,0:T(8,128)(2,1)S(1)}, bf16[13,64,128]{2,1,0:T(8,128)(2,1)S(1)}, u32[]{:S(2)}, u32[]{:S(2)}) collective-permute-start(bf16[13,64,128]{2,1,0:T(8,128)(2,1)S(1)} %shard_map.61), channel_id=1, source_target_pairs={{4,6},{5,7},{6,4},{7,5},{12,14},{13,15},{14,12},{15,13},{20,22},{2... | collective-permute-start | bytes 638984 | tf_op jit(solution)/shard_map/ppermute | solution.py:542
  38.0 0.7 %shard_map.62 = bf16[13,64,128]{2,1,0:T(8,128)(2,1)S(1)} custom-call(bf16[24,64,128]{2,1,0:T(8,128)(2,1)S(1)} %collective-permute-done.3.y.y1, bf16[12,64,128]{2,1,0:T(8,128)(2,1)S(1)} %collective-permute-done.6.x3.x, bf16[24,64,128]{2,1,0:T(8,128)(2,1)S(1)} %shard_map.59.b.got, bf16[24,64,128]{2,1,0:T(8,128)(2,1)S(1)} %collective-permute-done.8.b1.got1, ...), custom_call_target="tpu_custom_call" | custom-call | flops 2000000000 | bytes 1048576 | tf_op jit(solution)/shard_map/pallas_call | solution.py:518
  38.7 1.3 %collective-permute-start.15 = (bf16[13,64,128]{2,1,0:T(8,128)(2,1)S(1)}, bf16[13,64,128]{2,1,0:T(8,128)(2,1)S(1)}, u32[]{:S(2)}, u32[]{:S(2)}) collective-permute-start(bf16[13,64,128]{2,1,0:T(8,128)(2,1)S(1)} %shard_map.62), channel_id=1, source_target_pairs={{0,4},{1,5},{2,6},{3,7},{8,12},{9,13},{10,14},{11,15},{16,20},{17,... | collective-permute-start | bytes 638984 | tf_op jit(solution)/shard_map/ppermute | solution.py:542
  40.0 1.0 %shard_map.60 = (f32[24,64,128]{2,1,0:T(8,128)S(1)}, f32[64,128]{1,0:T(8,128)S(1)}) custom-call(bf16[48,64,128]{2,1,0:T(8,128)(2,1)S(1)} %bitcast.26, bf16[24,64,128]{2,1,0:T(8,128)(2,1)S(1)} %shard_map.57.a.got, bf16[24,64,128]{2,1,0:T(8,128)(2,1)S(1)} %collective-permute-done.4.a1.got1, bf16[24,64,128]{2,1,0:T(8,128)(2,1)S(1)} %shard_map.59.b.got, ...), custom_call_target="tpu_custom_call" | custom-call | flops 2000000000 | bytes 1048576 | tf_op jit(solution)/shard_map/pallas_call | solution.py:518
  41.1 4.5 %collective-permute-start.10 = (bf16[13,64,128]{2,1,0:T(8,128)(2,1)S(1)}, bf16[13,64,128]{2,1,0:T(8,128)(2,1)S(1)}, u32[]{:S(2)}, u32[]{:S(2)}) collective-permute-start(bf16[13,64,128]{2,1,0:T(8,128)(2,1)S(1)} %shard_map.62), channel_id=1, source_target_pairs={{4,6},{5,7},{6,4},{7,5},{12,14},{13,15},{14,12},{15,13},{20,22},{2... | collective-permute-start | bytes 638984 | tf_op jit(solution)/shard_map/ppermute | solution.py:542
  45.7 1.3 %collective-permute-start.16 = (bf16[13,64,128]{2,1,0:T(8,128)(2,1)S(1)}, bf16[13,64,128]{2,1,0:T(8,128)(2,1)S(1)}, u32[]{:S(2)}, u32[]{:S(2)}) collective-permute-start(bf16[13,64,128]{2,1,0:T(8,128)(2,1)S(1)} %shard_map.65), channel_id=1, source_target_pairs={{4,6},{5,7},{12,14},{13,15},{20,22},{21,23},{28,30},{29,31}} | collective-permute-start | bytes 638984 | tf_op jit(solution)/shard_map/ppermute | solution.py:542
  47.0 0.6 %shard_map.66 = (f32[12,64,128]{2,1,0:T(8,128)S(1)}, f32[64,128]{1,0:T(8,128)S(1)}) custom-call(bf16[48,64,128]{2,1,0:T(8,128)(2,1)S(1)} %bitcast.28, bf16[24,64,128]{2,1,0:T(8,128)(2,1)S(1)} %collective-permute-done.2.x.q.got, bf16[24,64,128]{2,1,0:T(8,128)(2,1)S(1)} %collective-permute-done.17.got1), custom_call_target="tpu_custom_call" | custom-call | flops 2000000000 | bytes 1048576 | tf_op jit(solution)/shard_map/pallas_call | solution.py:518
  48.0 0.7 %collective-permute-start.12 = (bf16[13,64,128]{2,1,0:T(8,128)(2,1)S(1)}, bf16[13,64,128]{2,1,0:T(8,128)(2,1)S(1)}, u32[]{:S(2)}, u32[]{:S(2)}) collective-permute-start(bf16[13,64,128]{2,1,0:T(8,128)(2,1)S(1)} %shard_map.63), channel_id=1, source_target_pairs={{0,2},{1,3},{8,10},{9,11},{16,18},{17,19},{24,26},{25,27}} | collective-permute-start | bytes 638984 | tf_op jit(solution)/shard_map/ppermute | solution.py:542
  48.7 1.5 %shard_map.56 = (f32[24,64,128]{2,1,0:T(8,128)S(1)}, f32[64,128]{1,0:T(8,128)S(1)}, f32[2,128]{1,0:T(2,128)S(1)}) custom-call(s32[2]{0:T(128)S(1)} %copy-done.1, f32[8,48]{1,0:T(8,128)S(1)} %copy-done, bf16[48,64,128]{2,1,0:T(8,128)(2,1)S(1)} %bitcast.29, bf16[48,64,128]{2,1,0:T(8,128)(2,1)S(1)} %bitcast.24, ...), custom_call_target="tpu_custom_call" | custom-call | flops 2000000000 | bytes 1048576 | tf_op jit(solution)/shard_map/pallas_call | solution.py:518
  50.2 5.3 %collective-permute-done.16.extra = bf16[13,64,128]{2,1,0:T(8,128)(2,1)S(1)} collective-permute-done((bf16[13,64,128]{2,1,0:T(8,128)(2,1)S(1)}, bf16[13,64,128]{2,1,0:T(8,128)(2,1)S(1)}, u32[]{:S(2)}, u32[]{:S(2)}) %collective-permute-start.16) | collective-permute-done | bytes 213024 | tf_op jit(solution)/shard_map/ppermute | solution.py:542
  55.6 2.3 %shard_map.67._ = bf16[64,48,128]{2,1,0:T(8,128)(2,1)} custom-call(f32[2,128]{1,0:T(2,128)S(1)} %get-tuple-element.30.gates, f32[24,64,128]{2,1,0:T(8,128)S(1)} %get-tuple-element.31.other, f32[64,128]{1,0:T(8,128)S(1)} %get-tuple-element.32.other_table, f32[24,64,128]{2,1,0:T(8,128)S(1)} %get-tuple-element.38.mine, ...), custom_call_target="tpu_custom_call" | custom-call | flops 2000000000 | bytes 1048576 | tf_op jit(solution)/shard_map/pallas_call | solution.py:518
  57.9 1.3 %shard_map.68 = bf16[64,48,128]{2,1,0:T(8,128)(2,1)} custom-call(f32[2,128]{1,0:T(2,128)S(1)} %get-tuple-element.30.gates, f32[24,64,128]{2,1,0:T(8,128)S(1)} %get-tuple-element.31.other, f32[64,128]{1,0:T(8,128)S(1)} %get-tuple-element.32.other_table, f32[24,64,128]{2,1,0:T(8,128)S(1)} %get-tuple-element.38.mine, ...), custom_call_target="tpu_custom_call", output_to_operand_aliasing={{}: (10, {})} | custom-call | flops 2000000000 | bytes 1048576 | tf_op jit(solution)/shard_map/pallas_call | solution.py:518
  (39 shorter events, 4.4 us)
Async XLA Ops:
  0.0 2.0 %copy-start.2 = (bf16[64,48,128]{2,1,0:T(8,128)(2,1)S(1)}, bf16[64,48,128]{2,1,0:T(8,128)(2,1)}, u32[]{:S(2)}) copy-start(bf16[64,48,128]{2,1,0:T(8,128)(2,1)} %value_rows.1) | copy-start | bytes 2359300
  1.4 1.1 %copy-start.3 = (bf16[64,48,128]{2,1,0:T(8,128)(2,1)S(1)}, bf16[64,48,128]{2,1,0:T(8,128)(2,1)}, u32[]{:S(2)}) copy-start(bf16[64,48,128]{2,1,0:T(8,128)(2,1)} %key_rows.1) | copy-start | bytes 2359300
  1.4 11.6 %collective-permute-start.3 = (bf16[24,64,128]{2,1,0:T(8,128)(2,1)S(1)}, bf16[24,64,128]{2,1,0:T(8,128)(2,1)S(1)}, u32[]{:S(2)}, u32[]{:S(2)}) collective-permute-start(bf16[24,64,128]{2,1,0:T(8,128)(2,1)S(1)} %get-tuple-element.34), channel_id=1, source_target_pairs={{0,4},{1,5},{2,6},{3,7},{4,0},{5,1},{6,2},{7,3},{8,12},{9,13},{10,... | collective-permute-start | bytes 1179656 | tf_op jit(solution)/shard_map/ppermute | solution.py:542
  2.6 1.1 %copy-start.4 = (bf16[64,48,128]{2,1,0:T(8,128)(2,1)S(1)}, bf16[64,48,128]{2,1,0:T(8,128)(2,1)}, u32[]{:S(2)}) copy-start(bf16[64,48,128]{2,1,0:T(8,128)(2,1)} %queries.1) | copy-start | bytes 2359300
  4.0 7.8 %collective-permute-start.5 = (bf16[12,64,128]{2,1,0:T(8,128)(2,1)S(1)}, bf16[12,64,128]{2,1,0:T(8,128)(2,1)S(1)}, u32[]{:S(2)}, u32[]{:S(2)}) collective-permute-start(bf16[12,64,128]{2,1,0:T(8,128)(2,1)S(1)} %get-tuple-element.35), channel_id=1, source_target_pairs={{0,2},{1,3},{2,0},{3,1},{4,6},{5,7},{6,4},{7,5},{8,10},{9,11},{10,... | collective-permute-start | bytes 589832 | tf_op jit(solution)/shard_map/ppermute | solution.py:542
  4.6 15.7 %collective-permute-start.2 = (bf16[24,64,128]{2,1,0:T(8,128)(2,1)S(1)}, bf16[24,64,128]{2,1,0:T(8,128)(2,1)S(1)}, u32[]{:S(2)}, u32[]{:S(2)}) collective-permute-start(bf16[24,64,128]{2,1,0:T(8,128)(2,1)S(1)} %get-tuple-element.33), channel_id=1, source_target_pairs={{0,2},{1,3},{2,0},{3,1},{4,6},{5,7},{6,4},{7,5},{8,10},{9,11},{10,... | collective-permute-start | bytes 1179656 | tf_op jit(solution)/shard_map/ppermute | solution.py:542
  6.1 19.8 %collective-permute-start = (bf16[48,64,128]{2,1,0:T(8,128)(2,1)S(1)}, bf16[48,64,128]{2,1,0:T(8,128)(2,1)S(1)}, u32[]{:S(2)}, u32[]{:S(2)}) collective-permute-start(bf16[48,64,128]{2,1,0:T(8,128)(2,1)S(1)} %bitcast.18), channel_id=1, source_target_pairs={{0,1},{1,0},{2,3},{3,2},{4,5},{5,4},{6,7},{7,6},{8,9},{9,8},{10,11... | collective-permute-start | bytes 2359304 | tf_op jit(solution)/shard_map/ppermute | solution.py:542
  6.1 20.5 %collective-permute-start.1 = (bf16[48,64,128]{2,1,0:T(8,128)(2,1)S(1)}, bf16[48,64,128]{2,1,0:T(8,128)(2,1)S(1)}, u32[]{:S(2)}, u32[]{:S(2)}) collective-permute-start(bf16[48,64,128]{2,1,0:T(8,128)(2,1)S(1)} %bitcast.10), channel_id=1, source_target_pairs={{0,1},{1,0},{2,3},{3,2},{4,5},{5,4},{6,7},{7,6},{8,9},{9,8},{10,11... | collective-permute-start | bytes 2359304 | tf_op jit(solution)/shard_map/ppermute | solution.py:542
  11.8 11.5 %collective-permute-start.7 = (bf16[24,64,128]{2,1,0:T(8,128)(2,1)S(1)}, bf16[24,64,128]{2,1,0:T(8,128)(2,1)S(1)}, u32[]{:S(2)}, u32[]{:S(2)}) collective-permute-start(bf16[24,64,128]{2,1,0:T(8,128)(2,1)S(1)} %get-tuple-element.37), channel_id=1, source_target_pairs={{0,4},{1,5},{2,6},{3,7},{4,0},{5,1},{6,2},{7,3},{8,12},{9,13},{10,... | collective-permute-start | bytes 1179656 | tf_op jit(solution)/shard_map/ppermute | solution.py:542
  13.0 10.3 %collective-permute-start.6 = (bf16[12,64,128]{2,1,0:T(8,128)(2,1)S(1)}, bf16[12,64,128]{2,1,0:T(8,128)(2,1)S(1)}, u32[]{:S(2)}, u32[]{:S(2)}) collective-permute-start(bf16[12,64,128]{2,1,0:T(8,128)(2,1)S(1)} %get-tuple-element.36), channel_id=1, source_target_pairs={{0,2},{1,3},{2,0},{3,1},{4,6},{5,7},{6,4},{7,5},{8,10},{9,11},{10,... | collective-permute-start | bytes 589832 | tf_op jit(solution)/shard_map/ppermute | solution.py:542
  20.3 3.7 %collective-permute-start.11 = (bf16[24,64,128]{2,1,0:T(8,128)(2,1)S(1)}, bf16[24,64,128]{2,1,0:T(8,128)(2,1)S(1)}, u32[]{:S(2)}, u32[]{:S(2)}) collective-permute-start(bf16[24,64,128]{2,1,0:T(8,128)(2,1)S(1)} %get-tuple-element.40), channel_id=1, source_target_pairs={{0,2},{1,3},{2,0},{3,1},{8,10},{9,11},{10,8},{11,9},{16,18},{17,19... | collective-permute-start | bytes 1179656 | tf_op jit(solution)/shard_map/ppermute | solution.py:542
  23.3 3.3 %collective-permute-start.4 = (bf16[24,64,128]{2,1,0:T(8,128)(2,1)S(1)}, bf16[24,64,128]{2,1,0:T(8,128)(2,1)S(1)}, u32[]{:S(2)}, u32[]{:S(2)}) collective-permute-start(bf16[24,64,128]{2,1,0:T(8,128)(2,1)S(1)} %shard_map.57.a.got), channel_id=1, source_target_pairs={{0,1},{1,0},{2,3},{3,2},{4,5},{5,4},{6,7},{7,6},{8,9},{9,8},{10,11... | collective-permute-start | bytes 1179656 | tf_op jit(solution)/shard_map/ppermute | solution.py:542
  23.4 14.6 %collective-permute-start.8 = (bf16[24,64,128]{2,1,0:T(8,128)(2,1)S(1)}, bf16[24,64,128]{2,1,0:T(8,128)(2,1)S(1)}, u32[]{:S(2)}, u32[]{:S(2)}) collective-permute-start(bf16[24,64,128]{2,1,0:T(8,128)(2,1)S(1)} %shard_map.59.b.got), channel_id=1, source_target_pairs={{0,1},{1,0},{2,3},{3,2},{4,5},{5,4},{6,7},{7,6},{8,9},{9,8},{10,11... | collective-permute-start | bytes 1179656 | tf_op jit(solution)/shard_map/ppermute | solution.py:542
  24.0 21.7 %collective-permute-start.17 = (bf16[24,64,128]{2,1,0:T(8,128)(2,1)S(1)}, bf16[24,64,128]{2,1,0:T(8,128)(2,1)S(1)}, u32[]{:S(2)}, u32[]{:S(2)}) collective-permute-start(bf16[24,64,128]{2,1,0:T(8,128)(2,1)S(1)} %collective-permute-done.2.x.q.got), channel_id=1, source_target_pairs={{6,7},{7,6},{14,15},{15,14},{22,23},{23,22},{30,31},{31,30}} | collective-permute-start | bytes 1179656 | tf_op jit(solution)/shard_map/ppermute | solution.py:542
  25.9 15.2 %collective-permute-start.13 = (bf16[24,64,128]{2,1,0:T(8,128)(2,1)S(1)}, bf16[24,64,128]{2,1,0:T(8,128)(2,1)S(1)}, u32[]{:S(2)}, u32[]{:S(2)}) collective-permute-start(bf16[24,64,128]{2,1,0:T(8,128)(2,1)S(1)} %collective-permute-done.11.q.got), channel_id=1, source_target_pairs={{2,3},{3,2},{10,11},{11,10},{18,19},{19,18},{26,27},{27,26}} | collective-permute-start | bytes 1179656 | tf_op jit(solution)/shard_map/ppermute | solution.py:542
  27.3 22.9 %collective-permute-start.14 = (bf16[13,64,128]{2,1,0:T(8,128)(2,1)S(1)}, bf16[13,64,128]{2,1,0:T(8,128)(2,1)S(1)}, u32[]{:S(2)}, u32[]{:S(2)}) collective-permute-start(bf16[13,64,128]{2,1,0:T(8,128)(2,1)S(1)} %shard_map.61), channel_id=1, source_target_pairs={{0,4},{1,5},{2,6},{3,7},{4,0},{5,1},{6,2},{7,3},{8,12},{9,13},{10,... | collective-permute-start | bytes 638984 | tf_op jit(solution)/shard_map/ppermute | solution.py:542
  36.1 14.1 %collective-permute-start.9 = (bf16[13,64,128]{2,1,0:T(8,128)(2,1)S(1)}, bf16[13,64,128]{2,1,0:T(8,128)(2,1)S(1)}, u32[]{:S(2)}, u32[]{:S(2)}) collective-permute-start(bf16[13,64,128]{2,1,0:T(8,128)(2,1)S(1)} %shard_map.61), channel_id=1, source_target_pairs={{4,6},{5,7},{6,4},{7,5},{12,14},{13,15},{14,12},{15,13},{20,22},{2... | collective-permute-start | bytes 638984 | tf_op jit(solution)/shard_map/ppermute | solution.py:542
  38.7 9.3 %collective-permute-start.15 = (bf16[13,64,128]{2,1,0:T(8,128)(2,1)S(1)}, bf16[13,64,128]{2,1,0:T(8,128)(2,1)S(1)}, u32[]{:S(2)}, u32[]{:S(2)}) collective-permute-start(bf16[13,64,128]{2,1,0:T(8,128)(2,1)S(1)} %shard_map.62), channel_id=1, source_target_pairs={{0,4},{1,5},{2,6},{3,7},{8,12},{9,13},{10,14},{11,15},{16,20},{17,... | collective-permute-start | bytes 638984 | tf_op jit(solution)/shard_map/ppermute | solution.py:542
  41.1 16.8 %collective-permute-start.10 = (bf16[13,64,128]{2,1,0:T(8,128)(2,1)S(1)}, bf16[13,64,128]{2,1,0:T(8,128)(2,1)S(1)}, u32[]{:S(2)}, u32[]{:S(2)}) collective-permute-start(bf16[13,64,128]{2,1,0:T(8,128)(2,1)S(1)} %shard_map.62), channel_id=1, source_target_pairs={{4,6},{5,7},{6,4},{7,5},{12,14},{13,15},{14,12},{15,13},{20,22},{2... | collective-permute-start | bytes 638984 | tf_op jit(solution)/shard_map/ppermute | solution.py:542
  45.7 3.0 %copy-start = (f32[8,48]{1,0:T(8,128)S(1)}, f32[8,48]{1,0:T(8,128)}, u32[]{:S(2)}) copy-start(f32[8,48]{1,0:T(8,128)} %gate_table.1) | copy-start | bytes 4612
  45.7 3.0 %copy-start.1 = (s32[2]{0:T(128)S(1)}, s32[2]{0:T(128)}, u32[]{:S(2)}) copy-start(s32[2]{0:T(128)} %levels.1) | copy-start | bytes 28
  45.7 9.8 %collective-permute-start.16 = (bf16[13,64,128]{2,1,0:T(8,128)(2,1)S(1)}, bf16[13,64,128]{2,1,0:T(8,128)(2,1)S(1)}, u32[]{:S(2)}, u32[]{:S(2)}) collective-permute-start(bf16[13,64,128]{2,1,0:T(8,128)(2,1)S(1)} %shard_map.65), channel_id=1, source_target_pairs={{4,6},{5,7},{12,14},{13,15},{20,22},{21,23},{28,30},{29,31}} | collective-permute-start | bytes 638984 | tf_op jit(solution)/shard_map/ppermute | solution.py:542
  48.0 9.8 %collective-permute-start.12 = (bf16[13,64,128]{2,1,0:T(8,128)(2,1)S(1)}, bf16[13,64,128]{2,1,0:T(8,128)(2,1)S(1)}, u32[]{:S(2)}, u32[]{:S(2)}) collective-permute-start(bf16[13,64,128]{2,1,0:T(8,128)(2,1)S(1)} %shard_map.63), channel_id=1, source_target_pairs={{0,2},{1,3},{8,10},{9,11},{16,18},{17,19},{24,26},{25,27}} | collective-permute-start | bytes 638984 | tf_op jit(solution)/shard_map/ppermute | solution.py:542
